TPU v7x, 512 devices: a whole 4x8x8 slice. The times are simulated.
512 devices in a mesh: seq: 128 (over x, z, y_lo), head: 4 (over y_hi, core).
Axes of the slice: x: 4, y: 8 (y_hi: 2, y_lo: 4; y = y_hi * 4 + y_lo), z: 8, core: 2. Of those that a mesh axis runs over, the one named last changes fastest.
Arguments:
- queries: bfloat16 [32768, 2048], P('seq', 'head'), may hold values from -6 to 6
- key_rows: bfloat16 [32768, 2048], P('seq', 'head'), may hold values from -6 to 6
- value_rows: bfloat16 [32768, 2048], P('seq', 'head'), may hold values from -6 to 6
- out_weight: bfloat16 [2048, 2048], P('head'), may hold values from -3 to 3
Outputs:
- layer_out: bfloat16 [32768, 2048], P('seq', 'head')
All inputs are finite; a program needn't handle non-finite values.
Results may differ from a plain program's by a relative error of at most 0.012.
Values may be sent and summed in bfloat16 or wider, within the bound.
No kernel may reach another device: no remote copies, remote signals or barrier semaphores. Data moves between devices by JAX's collectives and lax.ppermute only.
A program may use at most 64 MiB of HBM per device.

v0:
```python
import jax
import jax.numpy as jnp
from jax import lax
from jax.experimental import pallas as pl
from jax.experimental.pallas import tpu as pltpu
from jax.sharding import PartitionSpec as P


HEAD_DIM = 128
LOG2E = 1.4426950408889634
MIB = 1024 * 1024


def seq_permute(value, target_of):
    count = lax.axis_size("seq")
    pairs = [(i, target_of(i)) for i in range(count)]
    pairs = [(i, j) for i, j in pairs if 0 <= j < count]
    return lax.ppermute(value, "seq", pairs)


def head_permute(value, bit):
    count = lax.axis_size("head")
    return lax.ppermute(value, "head", [(i, i ^ bit) for i in range(count)])


def mean_matrix(rows, factor):
    row = lax.broadcasted_iota(jnp.int32, (rows, rows * factor), 0)
    col = lax.broadcasted_iota(jnp.int32, (rows, rows * factor), 1)
    return jnp.where(col // factor == row, 1.0 / factor, 0.0).astype(jnp.bfloat16)


def spread_mean_matrix(rows, factor):
    row = lax.broadcasted_iota(jnp.int32, (rows, rows), 0)
    col = lax.broadcasted_iota(jnp.int32, (rows, rows), 1)
    return jnp.where(col // factor == row // factor, 1.0 / factor, 0.0).astype(jnp.bfloat16)


def dot(left, right):
    return jnp.dot(left, right, preferred_element_type=jnp.float32)


def dot_t(left, right):
    return lax.dot_general(left, right, (((1,), (1,)), ((), ())), preferred_element_type=jnp.float32)


def coarse_kernel(k_ref, v_ref, raw_ref, one_ref, two_ref):
    half, quarter = mean_matrix(128, 2), mean_matrix(64, 4)
    for index, ref in enumerate((k_ref, v_ref)):
        value = ref[...]
        raw_ref[index * 256 : (index + 1) * 256] = value
        one_ref[index * 128 : (index + 1) * 128] = dot(half, value).astype(jnp.bfloat16)
        two_ref[index * 64 : (index + 1) * 64] = dot(quarter, value).astype(jnp.bfloat16)


def coarse(k, v):
    width = k.shape[1]
    return pl.pallas_call(
        coarse_kernel,
        out_shape=(
            jax.ShapeDtypeStruct((512, width), jnp.bfloat16),
            jax.ShapeDtypeStruct((256, width), jnp.bfloat16),
            jax.ShapeDtypeStruct((128, width), jnp.bfloat16),
        ),
        compiler_params=pltpu.CompilerParams(vmem_limit_bytes=8 * MIB),
        cost_estimate=pl.CostEstimate(flops=10**8, bytes_accessed=10**6, transcendentals=0),
        name="coarse",
    )(k, v)


def join_kernel(a_ref, b_ref, out_ref):
    out_ref[:128] = a_ref[...]
    out_ref[128:] = b_ref[...]


def join(a, b):
    return pl.pallas_call(
        join_kernel,
        out_shape=jax.ShapeDtypeStruct((256, a.shape[1]), a.dtype),
        compiler_params=pltpu.CompilerParams(vmem_limit_bytes=4 * MIB),
        cost_estimate=pl.CostEstimate(flops=10**8, bytes_accessed=10**6, transcendentals=0),
        name="join",
    )(a, b)


def pack_kernel(a_ref, b_ref, two_ref, three_ref):
    half = mean_matrix(32, 2)
    for index, (ref, base) in enumerate(((a_ref, 0), (a_ref, 128), (b_ref, 0), (b_ref, 128))):
        for part in range(2):
            value = ref[base + part * 64 : base + (part + 1) * 64]
            two_ref[part * 256 + index * 64 : part * 256 + (index + 1) * 64] = value
            three_ref[part * 128 + index * 32 : part * 128 + (index + 1) * 32] = dot(
                half, value
            ).astype(jnp.bfloat16)


def pack(pieces):
    width = pieces[0].shape[1]
    return pl.pallas_call(
        pack_kernel,
        out_shape=(
            jax.ShapeDtypeStruct((512, width), jnp.bfloat16),
            jax.ShapeDtypeStruct((256, width), jnp.bfloat16),
        ),
        compiler_params=pltpu.CompilerParams(vmem_limit_bytes=8 * MIB),
        cost_estimate=pl.CostEstimate(flops=10**8, bytes_accessed=10**6, transcendentals=0),
        name="pack",
    )(*pieces)


KEYS = 768 + 3 * 512


def attend_kernel(flags, q_ref, *refs):
    k_ref, v_ref, left, right = refs[0:4]
    ones = refs[4:7]
    twos = refs[7:9]
    threes = refs[9:12]
    out_ref = refs[12]
    scores, weights, values = refs[13:16]

    def bias(index):
        return jnp.where(flags[index] > 0, 0.0, -jnp.inf)

    even = flags[6] > 0
    half = mean_matrix(128, 2)
    beside_left = flags[2] > 0
    fourth = [
        dot(half, jnp.where(beside_left, left[p * 256 : (p + 1) * 256], right[p * 256 : (p + 1) * 256]))
        .astype(jnp.bfloat16)
        for p in range(2)
    ]
    near = [
        dot(half, jnp.where(even, twos[0][p * 256 : (p + 1) * 256], twos[1][p * 256 : (p + 1) * 256]))
        .astype(jnp.bfloat16)
        for p in range(2)
    ]
    pieces = [
        (k_ref[...], v_ref[...], 0, None),
        (left[:256], left[256:], 0, 0),
        (right[:256], right[256:], 0, 1),
    ]
    for index, ref in enumerate(ones):
        pieces.append((ref[:128], ref[128:], 1, (None, 10, 11)[index]))
    pieces.append((fourth[0], fourth[1], 1, 12))
    for index, ref in enumerate(twos):
        pieces.append((ref[:256], ref[256:], 2, 3 + index))
    for index, ref in enumerate(threes):
        pieces.append((ref[:128], ref[128:], 3, (5, 7, 8)[index]))
    pieces.append((near[0], near[1], 3, 9))

    query = q_ref[...]
    queries = [query] + [
        dot(spread_mean_matrix(query.shape[0], 2**level), query).astype(jnp.bfloat16)
        for level in range(1, 4)
    ]
    values[:, HEAD_DIM:] = jnp.ones((KEYS, HEAD_DIM), jnp.bfloat16)
    largest = None
    start = 0
    spans = []
    for keys, vals, level, flag in pieces:
        count = keys.shape[0]
        part = dot_t(queries[level], keys)
        if flag is not None:
            part = part + bias(flag)
        scores[:, start : start + count] = part
        values[start : start + count, :HEAD_DIM] = vals
        for column in range(0, count, 128):
            piece = part[:, column : column + 128]
            largest = piece if largest is None else jnp.maximum(largest, piece)
        spans.append((start, count, level))
        start += count
    scale = LOG2E * HEAD_DIM**-0.5
    top = jnp.max(largest, axis=1, keepdims=True) * scale
    for start, count, level in spans:
        shifted = scores[:, start : start + count] * scale - (top - level)
        weights[:, start : start + count] = jnp.exp2(shifted).astype(jnp.bfloat16)
    total = dot(weights[...], values[...])
    out_ref[...] = (total[:, :HEAD_DIM] / total[:, HEAD_DIM:]).astype(jnp.bfloat16)


def attend(flags, q, tensors):
    rows, width = q.shape
    heads = width // HEAD_DIM

    def spec(value):
        return pl.BlockSpec((value.shape[0], HEAD_DIM), lambda h: (0, h))

    return pl.pallas_call(
        attend_kernel,
        grid=(heads,),
        in_specs=[pl.BlockSpec(memory_space=pltpu.SMEM), spec(q)] + [spec(t) for t in tensors],
        out_specs=spec(q),
        out_shape=jax.ShapeDtypeStruct((rows, width), jnp.bfloat16),
        scratch_shapes=[
            pltpu.VMEM((rows, KEYS), jnp.float32),
            pltpu.VMEM((rows, KEYS), jnp.bfloat16),
            pltpu.VMEM((KEYS, 2 * HEAD_DIM), jnp.bfloat16),
        ],
        compiler_params=pltpu.CompilerParams(vmem_limit_bytes=32 * MIB),
        cost_estimate=pl.CostEstimate(flops=3 * 10**9, bytes_accessed=6 * 10**6, transcendentals=0),
        name="attend",
    )(flags, q, *tensors)


def project_kernel(column, a_ref, b_ref, wa_ref, wb_ref, out_ref):
    total = dot(a_ref[...], wa_ref[...]) + dot(b_ref[...], wb_ref[...])
    out_ref[...] = total.astype(out_ref.dtype)


def project(column, own, peer, own_weight, peer_weight, dtype):
    rows, width = own.shape
    block = pl.BlockSpec((rows, width), lambda i, c: (0, 0))
    weight = pl.BlockSpec((width, width), lambda i, c: (0, c[0]))
    return pl.pallas_call(
        project_kernel,
        grid_spec=pltpu.PrefetchScalarGridSpec(
            num_scalar_prefetch=1,
            grid=(1,),
            in_specs=[block, block, weight, weight],
            out_specs=block,
        ),
        out_shape=jax.ShapeDtypeStruct((rows, width), dtype),
        compiler_params=pltpu.CompilerParams(vmem_limit_bytes=12 * MIB),
        cost_estimate=pl.CostEstimate(flops=10**9, bytes_accessed=10**6, transcendentals=0),
    )(column, own, peer, own_weight, peer_weight)


def layer(queries, key_rows, value_rows, out_weight):
    device = lax.axis_index("seq")
    head = lax.axis_index("head")
    last = lax.axis_size("seq") - 1
    lines = lax.axis_size("seq") // 4
    line = device // 4
    spot = device % 4
    even = line % 2 == 0

    raw, own_one, own_two = coarse(key_rows, value_rows)
    two_across = seq_permute(own_two, lambda i: i ^ 2)
    across = seq_permute(own_one, lambda i: i ^ 2)
    two_half = join(own_two, two_across)
    two_beside = seq_permute(two_half, lambda i: i ^ 1)
    left = seq_permute(raw, lambda i: i + 1)
    right = seq_permute(raw, lambda i: i - 1)
    peer_weight = head_permute(out_weight, 1)

    two_block, three_block = pack((two_half, two_beside))
    two_low = seq_permute(two_block, lambda i: i + 4)
    two_high = seq_permute(two_block, lambda i: i - 4)
    three_low = seq_permute(three_block, lambda i: i + 8)
    three_high = seq_permute(three_block, lambda i: i - 8)
    three_skew = seq_permute(three_block, lambda i: i + 12 if i // 4 % 2 == 0 else i - 12)
    far = seq_permute(across, lambda i: i + 4 if i % 4 < 2 else i - 4)
    outer = (spot == 0) | (spot == 3)
    handed = jnp.where(outer, far, across)
    third = seq_permute(handed, lambda i: i ^ 1)

    far_ok = jnp.where(spot < 2, line > 0, line < lines - 1)
    flags = jnp.stack(
        [
            device > 0,
            device < last,
            spot % 2 == 0,
            line > 0,
            line < lines - 1,
            line >= 2,
            even,
            line < lines - 2,
            jnp.where(even, line < lines - 3, line >= 3),
            jnp.where(even, line > 0, line < lines - 1),
            far_ok,
            outer | far_ok,
            jnp.logical_not(outer) | far_ok,
        ]
    ).astype(jnp.int32)
    tensors = [key_rows, value_rows, left, right, across, far, third]
    tensors += [two_low, two_high, three_low, three_high, three_skew]
    attended = attend(flags, queries, tensors)
    peer = head_permute(attended, 1)
    here_column, away_column = head.reshape(1), (head ^ 2).reshape(1)
    weights = (out_weight, peer_weight)
    away = project(away_column, attended, peer, *weights, jnp.bfloat16)
    arrived = head_permute(away, 2)
    here = project(here_column, attended, peer, *weights, jnp.float32)
    return (here + arrived.astype(jnp.float32)).astype(jnp.bfloat16)


def solution(mesh):
    in_specs = (P("seq", "head"), P("seq", "head"), P("seq", "head"), P("head", None))
    out_specs = P("seq", "head")
    return jax.shard_map(layer, mesh=mesh, in_specs=in_specs, out_specs=out_specs, check_vma=False)
```

profile of v0, /device:TPU:134, one launch (start us, length us, event | category | flops | bytes accessed | tf_op | source)
XLA Modules:
  0.0 150.5 jit_solution(6604657988946564633)
XLA Ops:
  0.0 1.9 %collective-permute-start.13 = (bf16[512,2048]{1,0:T(8,128)(2,1)}, bf16[512,2048]{1,0:T(8,128)(2,1)}, u32[]{:S(2)}, u32[]{:S(2)}) collective-permute-start(bf16[512,2048]{1,0:T(8,128)(2,1)} %wa_ref.3), channel_id=1, source_target_pairs={{0,1},{1,0},{2,3},{3,2},{4,5},{5,4},{6,7},{7,6},{8,9},{9,8},{10,11... | collective-permute-start | bytes 6291464 | tf_op jit(solution)/shard_map/ppermute | solution.py:23
  4.2 3.5 %collective-permute-start = (bf16[512,512]{1,0:T(8,128)(2,1)S(1)}, bf16[512,512]{1,0:T(8,128)(2,1)S(1)}, u32[]{:S(2)}, u32[]{:S(2)}) collective-permute-start(bf16[512,512]{1,0:T(8,128)(2,1)S(1)} %get-tuple-element.10), channel_id=1, source_target_pairs={{0,4},{4,8},{8,12},{12,16},{16,20},{20,24},{24,28},{28,32},{32,36}... | collective-permute-start | bytes 1572872 | tf_op jit(solution)/shard_map/ppermute | solution.py:18
  7.6 5.1 %collective-permute-start.1 = (bf16[512,512]{1,0:T(8,128)(2,1)S(1)}, bf16[512,512]{1,0:T(8,128)(2,1)S(1)}, u32[]{:S(2)}, u32[]{:S(2)}) collective-permute-start(bf16[512,512]{1,0:T(8,128)(2,1)S(1)} %get-tuple-element.10), channel_id=1, source_target_pairs={{4,0},{8,4},{12,8},{16,12},{20,16},{24,20},{28,24},{32,28},{36,32}... | collective-permute-start | bytes 1572872 | tf_op jit(solution)/shard_map/ppermute | solution.py:18
  12.7 1.9 %collective-permute-start.2 = (bf16[256,512]{1,0:T(8,128)(2,1)S(1)}, bf16[256,512]{1,0:T(8,128)(2,1)S(1)}, u32[]{:S(2)}, u32[]{:S(2)}) collective-permute-start(bf16[256,512]{1,0:T(8,128)(2,1)S(1)} %get-tuple-element.11), channel_id=1, source_target_pairs={{0,8},{4,12},{8,0},{12,4},{16,24},{20,28},{24,16},{28,20},{32,40},... | collective-permute-start | bytes 786440 | tf_op jit(solution)/shard_map/ppermute | solution.py:18
  14.6 4.8 %collective-permute-start.5 = (bf16[128,512]{1,0:T(8,128)(2,1)S(1)}, bf16[128,512]{1,0:T(8,128)(2,1)S(1)}, u32[]{:S(2)}, u32[]{:S(2)}) collective-permute-start(bf16[128,512]{1,0:T(8,128)(2,1)S(1)} %get-tuple-element.12.a_ref), channel_id=1, source_target_pairs={{0,8},{4,12},{8,0},{12,4},{16,24},{20,28},{24,16},{28,20},{32,40},... | collective-permute-start | bytes 393224 | tf_op jit(solution)/shard_map/ppermute | solution.py:18
  19.5 32.6 %collective-permute-done.5.b_ref = bf16[128,512]{1,0:T(8,128)(2,1)S(1)} collective-permute-done((bf16[128,512]{1,0:T(8,128)(2,1)S(1)}, bf16[128,512]{1,0:T(8,128)(2,1)S(1)}, u32[]{:S(2)}, u32[]{:S(2)}) %collective-permute-start.5) | collective-permute-done | bytes 131104 | tf_op jit(solution)/shard_map/ppermute | solution.py:18
  52.1 1.9 %collective-permute-start.6 = (bf16[256,512]{1,0:T(8,128)(2,1)S(1)}, bf16[256,512]{1,0:T(8,128)(2,1)S(1)}, u32[]{:S(2)}, u32[]{:S(2)}) collective-permute-start(bf16[256,512]{1,0:T(8,128)(2,1)S(1)} %join.1.a_ref), channel_id=1, source_target_pairs={{0,4},{4,0},{8,12},{12,8},{16,20},{20,16},{24,28},{28,24},{32,36},... | collective-permute-start | bytes 786440 | tf_op jit(solution)/shard_map/ppermute | solution.py:18
  54.0 4.9 %collective-permute-start.3 = (bf16[256,512]{1,0:T(8,128)(2,1)S(1)}, bf16[256,512]{1,0:T(8,128)(2,1)S(1)}, u32[]{:S(2)}, u32[]{:S(2)}) collective-permute-start(bf16[256,512]{1,0:T(8,128)(2,1)S(1)} %collective-permute-done.2.refs_4_), channel_id=1, source_target_pairs={{0,16},{4,20},{16,32},{20,36},{24,8},{28,12},{32,48},{36,52},{40,2... | collective-permute-start | bytes 786440 | tf_op jit(solution)/shard_map/ppermute | solution.py:18
  58.9 3.3 %collective-permute-done.6.b_ref = bf16[256,512]{1,0:T(8,128)(2,1)S(1)} collective-permute-done((bf16[256,512]{1,0:T(8,128)(2,1)S(1)}, bf16[256,512]{1,0:T(8,128)(2,1)S(1)}, u32[]{:S(2)}, u32[]{:S(2)}) %collective-permute-start.6) | collective-permute-done | bytes 262176 | tf_op jit(solution)/shard_map/ppermute | solution.py:18
  63.1 6.4 %collective-permute-start.9 = (bf16[256,512]{1,0:T(8,128)(2,1)S(1)}, bf16[256,512]{1,0:T(8,128)(2,1)S(1)}, u32[]{:S(2)}, u32[]{:S(2)}) collective-permute-start(bf16[256,512]{1,0:T(8,128)(2,1)S(1)} %get-tuple-element.14), channel_id=1, source_target_pairs={{0,32},{4,36},{8,40},{12,44},{16,48},{20,52},{24,56},{28,60},{32,6... | collective-permute-start | bytes 786440 | tf_op jit(solution)/shard_map/ppermute | solution.py:18
  70.3 1.9 %collective-permute-start.10 = (bf16[256,512]{1,0:T(8,128)(2,1)S(1)}, bf16[256,512]{1,0:T(8,128)(2,1)S(1)}, u32[]{:S(2)}, u32[]{:S(2)}) collective-permute-start(bf16[256,512]{1,0:T(8,128)(2,1)S(1)} %get-tuple-element.14), channel_id=1, source_target_pairs={{32,0},{36,4},{40,8},{44,12},{48,16},{52,20},{56,24},{60,28},{64,3... | collective-permute-start | bytes 786440 | tf_op jit(solution)/shard_map/ppermute | solution.py:18
  73.1 3.4 %collective-permute-start.7 = (bf16[512,512]{1,0:T(8,128)(2,1)}, bf16[512,512]{1,0:T(8,128)(2,1)}, u32[]{:S(2)}, u32[]{:S(2)}) collective-permute-start(bf16[512,512]{1,0:T(8,128)(2,1)} %get-tuple-element.13), channel_id=1, source_target_pairs={{0,16},{4,20},{8,24},{12,28},{16,32},{20,36},{24,40},{28,44},{32,4... | collective-permute-start | bytes 1572872 | tf_op jit(solution)/shard_map/ppermute | solution.py:18
  76.5 2.5 %collective-permute-start.8 = (bf16[512,512]{1,0:T(8,128)(2,1)}, bf16[512,512]{1,0:T(8,128)(2,1)}, u32[]{:S(2)}, u32[]{:S(2)}) collective-permute-start(bf16[512,512]{1,0:T(8,128)(2,1)} %get-tuple-element.13), channel_id=1, source_target_pairs={{16,0},{20,4},{24,8},{28,12},{32,16},{36,20},{40,24},{44,28},{48,3... | collective-permute-start | bytes 1572872 | tf_op jit(solution)/shard_map/ppermute | solution.py:18
  79.7 2.0 %collective-permute-done.9.refs_9_ = bf16[256,512]{1,0:T(8,128)(2,1)S(1)} collective-permute-done((bf16[256,512]{1,0:T(8,128)(2,1)S(1)}, bf16[256,512]{1,0:T(8,128)(2,1)S(1)}, u32[]{:S(2)}, u32[]{:S(2)}) %collective-permute-start.9) | collective-permute-done | bytes 262176 | tf_op jit(solution)/shard_map/ppermute | solution.py:18
  82.4 4.9 %collective-permute-start.11 = (bf16[256,512]{1,0:T(8,128)(2,1)S(1)}, bf16[256,512]{1,0:T(8,128)(2,1)}, u32[]{:S(2)}, u32[]{:S(2)}) collective-permute-start(bf16[256,512]{1,0:T(8,128)(2,1)S(1)} %get-tuple-element.14), channel_id=1, source_target_pairs={{0,48},{4,52},{8,56},{12,60},{32,80},{36,84},{40,88},{44,92},{48,0... | collective-permute-start | bytes 786440 | tf_op jit(solution)/shard_map/ppermute | solution.py:18
  88.1 2.2 %collective-permute-start.4 = (bf16[256,512]{1,0:T(8,128)(2,1)}, bf16[256,512]{1,0:T(8,128)(2,1)}, u32[]{:S(2)}, u32[]{:S(2)}) collective-permute-start(bf16[256,512]{1,0:T(8,128)(2,1)} %broadcast_select_fusion), channel_id=1, source_target_pairs={{0,4},{4,0},{8,12},{12,8},{16,20},{20,16},{24,28},{28,24},{32,36},... | collective-permute-start | bytes 786440 | tf_op jit(solution)/shard_map/ppermute | solution.py:18
  90.5 20.1 %collective-permute-done.11.refs_11_ = bf16[256,512]{1,0:T(8,128)(2,1)} collective-permute-done((bf16[256,512]{1,0:T(8,128)(2,1)S(1)}, bf16[256,512]{1,0:T(8,128)(2,1)}, u32[]{:S(2)}, u32[]{:S(2)}) %collective-permute-start.11) | collective-permute-done | bytes 262176 | tf_op jit(solution)/shard_map/ppermute | solution.py:18
  115.5 9.4 %attend.1.a_ref = bf16[256,512]{1,0:T(8,128)(2,1)S(1)} custom-call(s32[13]{0:T(128)S(1)} %convert_element_type.9.flags, bf16[256,512]{1,0:T(8,128)(2,1)S(1)} %copy-done.9, bf16[256,512]{1,0:T(8,128)(2,1)S(1)} %copy-done.2, bf16[256,512]{1,0:T(8,128)(2,1)S(1)} %copy-done.4, bf16[512,512]{1,0:T(8,128)(2,1)S(1)} %copy-done.6, bf16[512,512]{1,0:T(8,128)(2,1)S(1)} %copy-done.8, ...), custom_call_target="tpu_custom_call" | custom-call | flops 3000000000 | bytes 6000000 | tf_op jit(solution)/shard_map/attend/pallas_call | solution.py:188
  124.9 1.9 %collective-permute-start.12 = (bf16[256,512]{1,0:T(8,128)(2,1)S(1)}, bf16[256,512]{1,0:T(8,128)(2,1)S(1)}, u32[]{:S(2)}, u32[]{:S(2)}) collective-permute-start(bf16[256,512]{1,0:T(8,128)(2,1)S(1)} %attend.1.a_ref), channel_id=1, source_target_pairs={{0,1},{1,0},{2,3},{3,2},{4,5},{5,4},{6,7},{7,6},{8,9},{9,8},{10,11... | collective-permute-start | bytes 786440 | tf_op jit(solution)/shard_map/ppermute | solution.py:23
  126.9 1.5 collective-permute-done.12.b_ref
  128.4 1.5 %shard_map.47 = bf16[256,512]{1,0:T(8,128)(2,1)S(1)} custom-call(s32[1]{0:T(128)} %bitcast.14.column, bf16[256,512]{1,0:T(8,128)(2,1)S(1)} %attend.1.a_ref, bf16[256,512]{1,0:T(8,128)(2,1)S(1)} %collective-permute-done.12.b_ref, bf16[512,2048]{1,0:T(8,128)(2,1)S(1)} %copy-done, bf16[512,2048]{1,0:T(8,128)(2,1)} %collective-permute-done.13.wb_ref), custom_call_target="tpu_custom_call" | custom-call | flops 1000000000 | bytes 1000000 | tf_op jit(solution)/shard_map/pallas_call | solution.py:214
  129.9 6.8 %collective-permute-start.14 = (bf16[256,512]{1,0:T(8,128)(2,1)S(1)}, bf16[256,512]{1,0:T(8,128)(2,1)S(1)}, u32[]{:S(2)}, u32[]{:S(2)}) collective-permute-start(bf16[256,512]{1,0:T(8,128)(2,1)S(1)} %shard_map.47), channel_id=1, source_target_pairs={{0,2},{1,3},{2,0},{3,1},{4,6},{5,7},{6,4},{7,5},{8,10},{9,11},{10,... | collective-permute-start | bytes 786440 | tf_op jit(solution)/shard_map/ppermute | solution.py:23
  136.7 1.5 %shard_map.46 = f32[256,512]{1,0:T(8,128)S(1)} custom-call(s32[1]{0:T(128)} %bitcast.column, bf16[256,512]{1,0:T(8,128)(2,1)S(1)} %attend.1.a_ref, bf16[256,512]{1,0:T(8,128)(2,1)S(1)} %collective-permute-done.12.b_ref, bf16[512,2048]{1,0:T(8,128)(2,1)S(1)} %copy-done, bf16[512,2048]{1,0:T(8,128)(2,1)} %collective-permute-done.13.wb_ref), custom_call_target="tpu_custom_call" | custom-call | flops 1000000000 | bytes 1000000 | tf_op jit(solution)/shard_map/pallas_call | solution.py:214
  138.3 11.5 %collective-permute-done.14 = bf16[256,512]{1,0:T(8,128)(2,1)S(1)} collective-permute-done((bf16[256,512]{1,0:T(8,128)(2,1)S(1)}, bf16[256,512]{1,0:T(8,128)(2,1)S(1)}, u32[]{:S(2)}, u32[]{:S(2)}) %collective-permute-start.14) | collective-permute-done | bytes 262176 | tf_op jit(solution)/shard_map/ppermute | solution.py:23
  (44 shorter events, 12.7 us)
Async XLA Ops:
  0.0 128.4 %collective-permute-start.13 = (bf16[512,2048]{1,0:T(8,128)(2,1)}, bf16[512,2048]{1,0:T(8,128)(2,1)}, u32[]{:S(2)}, u32[]{:S(2)}) collective-permute-start(bf16[512,2048]{1,0:T(8,128)(2,1)} %wa_ref.3), channel_id=1, source_target_pairs={{0,1},{1,0},{2,3},{3,2},{4,5},{5,4},{6,7},{7,6},{8,9},{9,8},{10,11... | collective-permute-start | bytes 6291464 | tf_op jit(solution)/shard_map/ppermute | solution.py:23
  1.9 1.0 copy-start.1
  2.9 0.9 copy-start.3
  3.8 106.7 %copy-start.2 = (bf16[256,512]{1,0:T(8,128)(2,1)S(1)}, bf16[256,512]{1,0:T(8,128)(2,1)}, u32[]{:S(2)}) copy-start(bf16[256,512]{1,0:T(8,128)(2,1)} %refs_0_.1) | copy-start | bytes 786436
  3.8 106.7 %copy-start.4 = (bf16[256,512]{1,0:T(8,128)(2,1)S(1)}, bf16[256,512]{1,0:T(8,128)(2,1)}, u32[]{:S(2)}) copy-start(bf16[256,512]{1,0:T(8,128)(2,1)} %refs_1_.1) | copy-start | bytes 786436
  4.2 65.4 %collective-permute-start = (bf16[512,512]{1,0:T(8,128)(2,1)S(1)}, bf16[512,512]{1,0:T(8,128)(2,1)S(1)}, u32[]{:S(2)}, u32[]{:S(2)}) collective-permute-start(bf16[512,512]{1,0:T(8,128)(2,1)S(1)} %get-tuple-element.10), channel_id=1, source_target_pairs={{0,4},{4,8},{8,12},{12,16},{16,20},{20,24},{24,28},{28,32},{32,36}... | collective-permute-start | bytes 1572872 | tf_op jit(solution)/shard_map/ppermute | solution.py:18
  7.6 64.6 %collective-permute-start.1 = (bf16[512,512]{1,0:T(8,128)(2,1)S(1)}, bf16[512,512]{1,0:T(8,128)(2,1)S(1)}, u32[]{:S(2)}, u32[]{:S(2)}) collective-permute-start(bf16[512,512]{1,0:T(8,128)(2,1)S(1)} %get-tuple-element.10), channel_id=1, source_target_pairs={{4,0},{8,4},{12,8},{16,12},{20,16},{24,20},{28,24},{32,28},{36,32}... | collective-permute-start | bytes 1572872 | tf_op jit(solution)/shard_map/ppermute | solution.py:18
  12.7 41.3 %collective-permute-start.2 = (bf16[256,512]{1,0:T(8,128)(2,1)S(1)}, bf16[256,512]{1,0:T(8,128)(2,1)S(1)}, u32[]{:S(2)}, u32[]{:S(2)}) collective-permute-start(bf16[256,512]{1,0:T(8,128)(2,1)S(1)} %get-tuple-element.11), channel_id=1, source_target_pairs={{0,8},{4,12},{8,0},{12,4},{16,24},{20,28},{24,16},{28,20},{32,40},... | collective-permute-start | bytes 786440 | tf_op jit(solution)/shard_map/ppermute | solution.py:18
  14.6 37.4 %collective-permute-start.5 = (bf16[128,512]{1,0:T(8,128)(2,1)S(1)}, bf16[128,512]{1,0:T(8,128)(2,1)S(1)}, u32[]{:S(2)}, u32[]{:S(2)}) collective-permute-start(bf16[128,512]{1,0:T(8,128)(2,1)S(1)} %get-tuple-element.12.a_ref), channel_id=1, source_target_pairs={{0,8},{4,12},{8,0},{12,4},{16,24},{20,28},{24,16},{28,20},{32,40},... | collective-permute-start | bytes 393224 | tf_op jit(solution)/shard_map/ppermute | solution.py:18
  52.1 10.1 %collective-permute-start.6 = (bf16[256,512]{1,0:T(8,128)(2,1)S(1)}, bf16[256,512]{1,0:T(8,128)(2,1)S(1)}, u32[]{:S(2)}, u32[]{:S(2)}) collective-permute-start(bf16[256,512]{1,0:T(8,128)(2,1)S(1)} %join.1.a_ref), channel_id=1, source_target_pairs={{0,4},{4,0},{8,12},{12,8},{16,20},{20,16},{24,28},{28,24},{32,36},... | collective-permute-start | bytes 786440 | tf_op jit(solution)/shard_map/ppermute | solution.py:18
  54.0 22.4 %collective-permute-start.3 = (bf16[256,512]{1,0:T(8,128)(2,1)S(1)}, bf16[256,512]{1,0:T(8,128)(2,1)S(1)}, u32[]{:S(2)}, u32[]{:S(2)}) collective-permute-start(bf16[256,512]{1,0:T(8,128)(2,1)S(1)} %collective-permute-done.2.refs_4_), channel_id=1, source_target_pairs={{0,16},{4,20},{16,32},{20,36},{24,8},{28,12},{32,48},{36,52},{40,2... | collective-permute-start | bytes 786440 | tf_op jit(solution)/shard_map/ppermute | solution.py:18
  63.1 18.6 %collective-permute-start.9 = (bf16[256,512]{1,0:T(8,128)(2,1)S(1)}, bf16[256,512]{1,0:T(8,128)(2,1)S(1)}, u32[]{:S(2)}, u32[]{:S(2)}) collective-permute-start(bf16[256,512]{1,0:T(8,128)(2,1)S(1)} %get-tuple-element.14), channel_id=1, source_target_pairs={{0,32},{4,36},{8,40},{12,44},{16,48},{20,52},{24,56},{28,60},{32,6... | collective-permute-start | bytes 786440 | tf_op jit(solution)/shard_map/ppermute | solution.py:18
  70.3 17.0 %collective-permute-start.10 = (bf16[256,512]{1,0:T(8,128)(2,1)S(1)}, bf16[256,512]{1,0:T(8,128)(2,1)S(1)}, u32[]{:S(2)}, u32[]{:S(2)}) collective-permute-start(bf16[256,512]{1,0:T(8,128)(2,1)S(1)} %get-tuple-element.14), channel_id=1, source_target_pairs={{32,0},{36,4},{40,8},{44,12},{48,16},{52,20},{56,24},{60,28},{64,3... | collective-permute-start | bytes 786440 | tf_op jit(solution)/shard_map/ppermute | solution.py:18
  73.1 37.5 %collective-permute-start.7 = (bf16[512,512]{1,0:T(8,128)(2,1)}, bf16[512,512]{1,0:T(8,128)(2,1)}, u32[]{:S(2)}, u32[]{:S(2)}) collective-permute-start(bf16[512,512]{1,0:T(8,128)(2,1)} %get-tuple-element.13), channel_id=1, source_target_pairs={{0,16},{4,20},{8,24},{12,28},{16,32},{20,36},{24,40},{28,44},{32,4... | collective-permute-start | bytes 1572872 | tf_op jit(solution)/shard_map/ppermute | solution.py:18
  76.5 34.1 %collective-permute-start.8 = (bf16[512,512]{1,0:T(8,128)(2,1)}, bf16[512,512]{1,0:T(8,128)(2,1)}, u32[]{:S(2)}, u32[]{:S(2)}) collective-permute-start(bf16[512,512]{1,0:T(8,128)(2,1)} %get-tuple-element.13), channel_id=1, source_target_pairs={{16,0},{20,4},{24,8},{28,12},{32,16},{36,20},{40,24},{44,28},{48,3... | collective-permute-start | bytes 1572872 | tf_op jit(solution)/shard_map/ppermute | solution.py:18
  82.4 28.1 %collective-permute-start.11 = (bf16[256,512]{1,0:T(8,128)(2,1)S(1)}, bf16[256,512]{1,0:T(8,128)(2,1)}, u32[]{:S(2)}, u32[]{:S(2)}) collective-permute-start(bf16[256,512]{1,0:T(8,128)(2,1)S(1)} %get-tuple-element.14), channel_id=1, source_target_pairs={{0,48},{4,52},{8,56},{12,60},{32,80},{36,84},{40,88},{44,92},{48,0... | collective-permute-start | bytes 786440 | tf_op jit(solution)/shard_map/ppermute | solution.py:18
  88.1 22.5 %collective-permute-start.4 = (bf16[256,512]{1,0:T(8,128)(2,1)}, bf16[256,512]{1,0:T(8,128)(2,1)}, u32[]{:S(2)}, u32[]{:S(2)}) collective-permute-start(bf16[256,512]{1,0:T(8,128)(2,1)} %broadcast_select_fusion), channel_id=1, source_target_pairs={{0,4},{4,0},{8,12},{12,8},{16,20},{20,16},{24,28},{28,24},{32,36},... | collective-permute-start | bytes 786440 | tf_op jit(solution)/shard_map/ppermute | solution.py:18
  90.5 37.9 %copy-start = (bf16[512,2048]{1,0:T(8,128)(2,1)S(1)}, bf16[512,2048]{1,0:T(8,128)(2,1)}, u32[]{:S(2)}) copy-start(bf16[512,2048]{1,0:T(8,128)(2,1)} %wa_ref.3) | copy-start | bytes 6291460
  110.6 1.0 copy-start.6
  111.6 1.0 copy-start.8
  112.6 0.9 copy-start.9
  113.6 0.9 copy-start.11
  124.9 3.4 %collective-permute-start.12 = (bf16[256,512]{1,0:T(8,128)(2,1)S(1)}, bf16[256,512]{1,0:T(8,128)(2,1)S(1)}, u32[]{:S(2)}, u32[]{:S(2)}) collective-permute-start(bf16[256,512]{1,0:T(8,128)(2,1)S(1)} %attend.1.a_ref), channel_id=1, source_target_pairs={{0,1},{1,0},{2,3},{3,2},{4,5},{5,4},{6,7},{7,6},{8,9},{9,8},{10,11... | collective-permute-start | bytes 786440 | tf_op jit(solution)/shard_map/ppermute | solution.py:23
  129.9 19.8 %collective-permute-start.14 = (bf16[256,512]{1,0:T(8,128)(2,1)S(1)}, bf16[256,512]{1,0:T(8,128)(2,1)S(1)}, u32[]{:S(2)}, u32[]{:S(2)}) collective-permute-start(bf16[256,512]{1,0:T(8,128)(2,1)S(1)} %shard_map.47), channel_id=1, source_target_pairs={{0,2},{1,3},{2,0},{3,1},{4,6},{5,7},{6,4},{7,5},{8,10},{9,11},{10,... | collective-permute-start | bytes 786440 | tf_op jit(solution)/shard_map/ppermute | solution.py:23
  (5 other events, 4.0 us)
where the time goes:
time: 151 us; the launch traced here: 150 us
  waiting for transfers between devices  71 us (47%)
  starting transfers between devices  54 us (36%)
  Pallas kernels  13.7 us (9%)
  local copies, waits for them, and re-layouts  9.96 us (7%)
  other arithmetic  1.51 us (1%)
    ppermute x12, waiting for transfers between devices, seq_permute(): return lax.ppermute(value, 'seq', pairs)  58 us
    ppermute x12, starting transfers between devices, seq_permute(): return lax.ppermute(value, 'seq', pairs)  43.3 us
    ppermute x3, waiting for transfers between devices, head_permute(): return lax.ppermute(value, 'head', [(i, i ^ bit) for i in range(count)])  13 us
    ppermute x3, starting transfers between devices, head_permute(): return lax.ppermute(value, 'head', [(i, i ^ bit) for i in range(count)])  10.7 us
    unnamed x28, local copies, waits for them, and re-layouts  9.85 us
    pallas_call x1, Pallas kernels, attend(): pl.pallas_call(attend_kernel, grid=(heads,), in_specs=[pl.BlockSpec(memor...  9.44 us
    pallas_call x2, Pallas kernels, project(): pl.pallas_call(project_kernel, grid_spec=pltpu.PrefetchScalarGridSpec(num...  3.02 us
  transfers between devices with their start and end apart: 15, of which 6 were waited for; matrix products, arithmetic and copies ran while one was open for 1% of the time, Pallas kernels for 8%

commit v1 on v0

--- a/solution.py
+++ b/solution.py
@@ -67,44 +67,30 @@
     )(k, v)
 
 
-def join_kernel(a_ref, b_ref, out_ref):
-    out_ref[:128] = a_ref[...]
-    out_ref[128:] = b_ref[...]
-
-
-def join(a, b):
-    return pl.pallas_call(
-        join_kernel,
+def half_kernel(two_ref, one_ref, out_ref):
+    half = mean_matrix(64, 2)
+    for part in range(2):
+        base = part * 128
+        out_ref[base : base + 64] = two_ref[part * 64 : (part + 1) * 64]
+        out_ref[base + 64 : base + 128] = dot(half, one_ref[base : base + 128]).astype(jnp.bfloat16)
+
+
+def halve_kernel(a_ref, b_ref, out_ref):
+    half = mean_matrix(64, 2)
+    for part in range(2):
+        base = part * 128
+        for index, ref in enumerate((a_ref, b_ref)):
+            start = base + index * 64
+            out_ref[start : start + 64] = dot(half, ref[base : base + 128]).astype(jnp.bfloat16)
+
+
+def small(kernel, a, b):
+    return pl.pallas_call(
+        kernel,
         out_shape=jax.ShapeDtypeStruct((256, a.shape[1]), a.dtype),
         compiler_params=pltpu.CompilerParams(vmem_limit_bytes=4 * MIB),
         cost_estimate=pl.CostEstimate(flops=10**8, bytes_accessed=10**6, transcendentals=0),
-        name="join",
     )(a, b)
-
-
-def pack_kernel(a_ref, b_ref, two_ref, three_ref):
-    half = mean_matrix(32, 2)
-    for index, (ref, base) in enumerate(((a_ref, 0), (a_ref, 128), (b_ref, 0), (b_ref, 128))):
-        for part in range(2):
-            value = ref[base + part * 64 : base + (part + 1) * 64]
-            two_ref[part * 256 + index * 64 : part * 256 + (index + 1) * 64] = value
-            three_ref[part * 128 + index * 32 : part * 128 + (index + 1) * 32] = dot(
-                half, value
-            ).astype(jnp.bfloat16)
-
-
-def pack(pieces):
-    width = pieces[0].shape[1]
-    return pl.pallas_call(
-        pack_kernel,
-        out_shape=(
-            jax.ShapeDtypeStruct((512, width), jnp.bfloat16),
-            jax.ShapeDtypeStruct((256, width), jnp.bfloat16),
-        ),
-        compiler_params=pltpu.CompilerParams(vmem_limit_bytes=8 * MIB),
-        cost_estimate=pl.CostEstimate(flops=10**8, bytes_accessed=10**6, transcendentals=0),
-        name="pack",
-    )(*pieces)
 
 
 KEYS = 768 + 3 * 512
@@ -113,10 +99,11 @@
 def attend_kernel(flags, q_ref, *refs):
     k_ref, v_ref, left, right = refs[0:4]
     ones = refs[4:7]
-    twos = refs[7:9]
-    threes = refs[9:12]
-    out_ref = refs[12]
-    scores, weights, values = refs[13:16]
+    twos = refs[7:11]
+    threes = refs[11:14]
+    nears = refs[14:16]
+    out_ref = refs[16]
+    scores, weights, values = refs[17:20]
 
     def bias(index):
         return jnp.where(flags[index] > 0, 0.0, -jnp.inf)
@@ -130,8 +117,7 @@
         for p in range(2)
     ]
     near = [
-        dot(half, jnp.where(even, twos[0][p * 256 : (p + 1) * 256], twos[1][p * 256 : (p + 1) * 256]))
-        .astype(jnp.bfloat16)
+        jnp.where(even, nears[0][p * 128 : (p + 1) * 128], nears[1][p * 128 : (p + 1) * 128])
         for p in range(2)
     ]
     pieces = [
@@ -143,7 +129,7 @@
         pieces.append((ref[:128], ref[128:], 1, (None, 10, 11)[index]))
     pieces.append((fourth[0], fourth[1], 1, 12))
     for index, ref in enumerate(twos):
-        pieces.append((ref[:256], ref[256:], 2, 3 + index))
+        pieces.append((ref[:128], ref[128:], 2, 3 + index // 2))
     for index, ref in enumerate(threes):
         pieces.append((ref[:128], ref[128:], 3, (5, 7, 8)[index]))
     pieces.append((near[0], near[1], 3, 9))
@@ -235,24 +221,26 @@
     even = line % 2 == 0
 
     raw, own_one, own_two = coarse(key_rows, value_rows)
-    two_across = seq_permute(own_two, lambda i: i ^ 2)
     across = seq_permute(own_one, lambda i: i ^ 2)
-    two_half = join(own_two, two_across)
+    two_half = small(half_kernel, own_two, across)
     two_beside = seq_permute(two_half, lambda i: i ^ 1)
+    low_a = seq_permute(two_half, lambda i: i + 4)
+    high_a = seq_permute(two_half, lambda i: i - 4)
+    far = seq_permute(across, lambda i: i + 4 if i % 4 < 2 else i - 4)
     left = seq_permute(raw, lambda i: i + 1)
     right = seq_permute(raw, lambda i: i - 1)
+    low_b = seq_permute(two_beside, lambda i: i + 4)
+    high_b = seq_permute(two_beside, lambda i: i - 4)
+    three_block = small(halve_kernel, two_half, two_beside)
+    three_skew = seq_permute(three_block, lambda i: i + 12 if i // 4 % 2 == 0 else i - 12)
     peer_weight = head_permute(out_weight, 1)
-
-    two_block, three_block = pack((two_half, two_beside))
-    two_low = seq_permute(two_block, lambda i: i + 4)
-    two_high = seq_permute(two_block, lambda i: i - 4)
-    three_low = seq_permute(three_block, lambda i: i + 8)
-    three_high = seq_permute(three_block, lambda i: i - 8)
-    three_skew = seq_permute(three_block, lambda i: i + 12 if i // 4 % 2 == 0 else i - 12)
-    far = seq_permute(across, lambda i: i + 4 if i % 4 < 2 else i - 4)
     outer = (spot == 0) | (spot == 3)
     handed = jnp.where(outer, far, across)
     third = seq_permute(handed, lambda i: i ^ 1)
+    near_low = small(halve_kernel, low_a, low_b)
+    near_high = small(halve_kernel, high_a, high_b)
+    three_low = seq_permute(near_low, lambda i: i + 4)
+    three_high = seq_permute(near_high, lambda i: i - 4)
 
     far_ok = jnp.where(spot < 2, line > 0, line < lines - 1)
     flags = jnp.stack(
@@ -273,8 +261,11 @@
         ]
     ).astype(jnp.int32)
     tensors = [key_rows, value_rows, left, right, across, far, third]
-    tensors += [two_low, two_high, three_low, three_high, three_skew]
-    attended = attend(flags, queries, tensors)
+    tensors += [low_a, low_b, high_a, high_b, three_low, three_high, three_skew]
+    tensors += [near_low, near_high]
+    tensors = [pltpu.with_memory_space_constraint(t, pltpu.HBM) for t in tensors]
+    own_queries = pltpu.with_memory_space_constraint(queries, pltpu.HBM)
+    attended = attend(flags, own_queries, tensors)
     peer = head_permute(attended, 1)
     here_column, away_column = head.reshape(1), (head ^ 2).reshape(1)
     weights = (out_weight, peer_weight)

time: 151 us -> 129 us (0.85)
  the two profiles are of different devices: /device:TPU:134 before, /device:TPU:30 now
where the time goes in v1:
time: 129 us
  starting transfers between devices  55 us (43%)
  waiting for transfers between devices  54.4 us (42%)
  Pallas kernels  15.2 us (12%)
  local copies, waits for them, and re-layouts  2.04 us (2%)
  other arithmetic  1.52 us (1%)
    ppermute x13, starting transfers between devices, seq_permute(): return lax.ppermute(value, 'seq', pairs)  45.2 us
    ppermute x13, waiting for transfers between devices, seq_permute(): return lax.ppermute(value, 'seq', pairs)  40.7 us
    ppermute x3, waiting for transfers between devices, head_permute(): return lax.ppermute(value, 'head', [(i, i ^ bit) for i in range(count)])  13.8 us
    ppermute x3, starting transfers between devices, head_permute(): return lax.ppermute(value, 'head', [(i, i ^ bit) for i in range(count)])  9.85 us
    pallas_call x1, Pallas kernels, attend(): pl.pallas_call(attend_kernel, grid=(heads,), in_specs=[pl.BlockSpec(memor...  8.9 us
    pallas_call x2, Pallas kernels, project(): pl.pallas_call(project_kernel, grid_spec=pltpu.PrefetchScalarGridSpec(num...  3.03 us
    pallas_call x4, Pallas kernels, small(): pl.pallas_call(kernel, out_shape=jax.ShapeDtypeStruct((256, a.shape[1]),...  2.95 us
  transfers between devices with their start and end apart: 16, of which 9 were waited for; matrix products, arithmetic and copies ran while one was open for 1% of the time, Pallas kernels for 11%

profile of v1, /device:TPU:30, one launch (start us, length us, event | category | flops | bytes accessed | tf_op | source)
XLA Modules:
  0.0 128.6 jit_solution(16007835998942442063)
XLA Ops:
  0.0 1.9 %collective-permute-start.14 = (bf16[512,2048]{1,0:T(8,128)(2,1)}, bf16[512,2048]{1,0:T(8,128)(2,1)}, u32[]{:S(2)}, u32[]{:S(2)}) collective-permute-start(bf16[512,2048]{1,0:T(8,128)(2,1)} %wa_ref.3), channel_id=1, source_target_pairs={{0,1},{1,0},{2,3},{3,2},{4,5},{5,4},{6,7},{7,6},{8,9},{9,8},{10,11... | collective-permute-start | bytes 6291464 | tf_op jit(solution)/shard_map/ppermute | solution.py:23
  4.1 2.2 %collective-permute-start.2 = (bf16[256,512]{1,0:T(8,128)(2,1)S(1)}, bf16[256,512]{1,0:T(8,128)(2,1)S(1)}, u32[]{:S(2)}, u32[]{:S(2)}) collective-permute-start(bf16[256,512]{1,0:T(8,128)(2,1)S(1)} %get-tuple-element.9), channel_id=1, source_target_pairs={{0,8},{4,12},{8,0},{12,4},{16,24},{20,28},{24,16},{28,20},{32,40},... | collective-permute-start | bytes 786440 | tf_op jit(solution)/shard_map/ppermute | solution.py:18
  6.4 14.8 %collective-permute-done.2.one_ref.refs_4_ = bf16[256,512]{1,0:T(8,128)(2,1)S(1)} collective-permute-done((bf16[256,512]{1,0:T(8,128)(2,1)S(1)}, bf16[256,512]{1,0:T(8,128)(2,1)S(1)}, u32[]{:S(2)}, u32[]{:S(2)}) %collective-permute-start.2) | collective-permute-done | bytes 262176 | tf_op jit(solution)/shard_map/ppermute | solution.py:18
  21.3 1.9 %collective-permute-start.6 = (bf16[256,512]{1,0:T(8,128)(2,1)S(1)}, bf16[256,512]{1,0:T(8,128)(2,1)S(1)}, u32[]{:S(2)}, u32[]{:S(2)}) collective-permute-start(bf16[256,512]{1,0:T(8,128)(2,1)S(1)} %shard_map.46.a_ref), channel_id=1, source_target_pairs={{0,4},{4,0},{8,12},{12,8},{16,20},{20,16},{24,28},{28,24},{32,36},... | collective-permute-start | bytes 786440 | tf_op jit(solution)/shard_map/ppermute | solution.py:18
  23.3 11.2 %collective-permute-start.3 = (bf16[256,512]{1,0:T(8,128)(2,1)S(1)}, bf16[256,512]{1,0:T(8,128)(2,1)S(1)}, u32[]{:S(2)}, u32[]{:S(2)}) collective-permute-start(bf16[256,512]{1,0:T(8,128)(2,1)S(1)} %collective-permute-done.2.one_ref.refs_4_), channel_id=1, source_target_pairs={{0,16},{4,20},{16,32},{20,36},{24,8},{28,12},{32,48},{36,52},{40,2... | collective-permute-start | bytes 786440 | tf_op jit(solution)/shard_map/ppermute | solution.py:18
  34.5 1.9 %collective-permute-start.5 = (bf16[256,512]{1,0:T(8,128)(2,1)S(1)}, bf16[256,512]{1,0:T(8,128)(2,1)S(1)}, u32[]{:S(2)}, u32[]{:S(2)}) collective-permute-start(bf16[256,512]{1,0:T(8,128)(2,1)S(1)} %shard_map.46.a_ref), channel_id=1, source_target_pairs={{0,16},{4,20},{8,24},{12,28},{16,32},{20,36},{24,40},{28,44},{32,4... | collective-permute-start | bytes 786440 | tf_op jit(solution)/shard_map/ppermute | solution.py:18
  36.4 1.9 %collective-permute-start.7 = (bf16[256,512]{1,0:T(8,128)(2,1)S(1)}, bf16[256,512]{1,0:T(8,128)(2,1)S(1)}, u32[]{:S(2)}, u32[]{:S(2)}) collective-permute-start(bf16[256,512]{1,0:T(8,128)(2,1)S(1)} %collective-permute-done.6.b_ref), channel_id=1, source_target_pairs={{0,16},{4,20},{8,24},{12,28},{16,32},{20,36},{24,40},{28,44},{32,4... | collective-permute-start | bytes 786440 | tf_op jit(solution)/shard_map/ppermute | solution.py:18
  38.3 3.7 %collective-permute-start = (bf16[512,512]{1,0:T(8,128)(2,1)S(1)}, bf16[512,512]{1,0:T(8,128)(2,1)S(1)}, u32[]{:S(2)}, u32[]{:S(2)}) collective-permute-start(bf16[512,512]{1,0:T(8,128)(2,1)S(1)} %get-tuple-element.8), channel_id=1, source_target_pairs={{0,4},{4,8},{8,12},{12,16},{16,20},{20,24},{24,28},{28,32},{32,36}... | collective-permute-start | bytes 1572872 | tf_op jit(solution)/shard_map/ppermute | solution.py:18
  42.1 2.1 %collective-permute-start.1 = (bf16[512,512]{1,0:T(8,128)(2,1)S(1)}, bf16[512,512]{1,0:T(8,128)(2,1)}, u32[]{:S(2)}, u32[]{:S(2)}) collective-permute-start(bf16[512,512]{1,0:T(8,128)(2,1)S(1)} %get-tuple-element.8), channel_id=1, source_target_pairs={{4,0},{8,4},{12,8},{16,12},{20,16},{24,20},{28,24},{32,28},{36,32}... | collective-permute-start | bytes 1572872 | tf_op jit(solution)/shard_map/ppermute | solution.py:18
  44.3 3.4 %collective-permute-done.5.a_ref.refs_7_ = bf16[256,512]{1,0:T(8,128)(2,1)S(1)} collective-permute-done((bf16[256,512]{1,0:T(8,128)(2,1)S(1)}, bf16[256,512]{1,0:T(8,128)(2,1)S(1)}, u32[]{:S(2)}, u32[]{:S(2)}) %collective-permute-start.5) | collective-permute-done | bytes 262176 | tf_op jit(solution)/shard_map/ppermute | solution.py:18
  47.7 2.9 %collective-permute-start.8 = (bf16[256,512]{1,0:T(8,128)(2,1)S(1)}, bf16[256,512]{1,0:T(8,128)(2,1)S(1)}, u32[]{:S(2)}, u32[]{:S(2)}) collective-permute-start(bf16[256,512]{1,0:T(8,128)(2,1)S(1)} %shard_map.46.a_ref), channel_id=1, source_target_pairs={{16,0},{20,4},{24,8},{28,12},{32,16},{36,20},{40,24},{44,28},{48,3... | collective-permute-start | bytes 786440 | tf_op jit(solution)/shard_map/ppermute | solution.py:18
  52.1 2.4 %collective-permute-start.9 = (bf16[256,512]{1,0:T(8,128)(2,1)S(1)}, bf16[256,512]{1,0:T(8,128)(2,1)S(1)}, u32[]{:S(2)}, u32[]{:S(2)}) collective-permute-start(bf16[256,512]{1,0:T(8,128)(2,1)S(1)} %collective-permute-done.6.b_ref), channel_id=1, source_target_pairs={{16,0},{20,4},{24,8},{28,12},{32,16},{36,20},{40,24},{44,28},{48,3... | collective-permute-start | bytes 786440 | tf_op jit(solution)/shard_map/ppermute | solution.py:18
  57.1 11.8 %collective-permute-done.8.a_ref.refs_9_ = bf16[256,512]{1,0:T(8,128)(2,1)S(1)} collective-permute-done((bf16[256,512]{1,0:T(8,128)(2,1)S(1)}, bf16[256,512]{1,0:T(8,128)(2,1)S(1)}, u32[]{:S(2)}, u32[]{:S(2)}) %collective-permute-start.8) | collective-permute-done | bytes 262176 | tf_op jit(solution)/shard_map/ppermute | solution.py:18
  68.9 1.9 %collective-permute-start.4 = (bf16[256,512]{1,0:T(8,128)(2,1)}, bf16[256,512]{1,0:T(8,128)(2,1)}, u32[]{:S(2)}, u32[]{:S(2)}) collective-permute-start(bf16[256,512]{1,0:T(8,128)(2,1)} %broadcast_select_fusion), channel_id=1, source_target_pairs={{0,4},{4,0},{8,12},{12,8},{16,20},{20,16},{24,28},{28,24},{32,36},... | collective-permute-start | bytes 786440 | tf_op jit(solution)/shard_map/ppermute | solution.py:18
  70.8 1.6 %collective-permute-done.9.b_ref.refs_10_ = bf16[256,512]{1,0:T(8,128)(2,1)S(1)} collective-permute-done((bf16[256,512]{1,0:T(8,128)(2,1)S(1)}, bf16[256,512]{1,0:T(8,128)(2,1)S(1)}, u32[]{:S(2)}, u32[]{:S(2)}) %collective-permute-start.9) | collective-permute-done | bytes 262176 | tf_op jit(solution)/shard_map/ppermute | solution.py:18
  72.4 5.0 %collective-permute-start.12 = (bf16[256,512]{1,0:T(8,128)(2,1)}, bf16[256,512]{1,0:T(8,128)(2,1)}, u32[]{:S(2)}, u32[]{:S(2)}) collective-permute-start(bf16[256,512]{1,0:T(8,128)(2,1)} %shard_map.49), channel_id=1, source_target_pairs={{0,48},{4,52},{8,56},{12,60},{32,80},{36,84},{40,88},{44,92},{48,0... | collective-permute-start | bytes 786440 | tf_op jit(solution)/shard_map/ppermute | solution.py:18
  78.3 3.4 %collective-permute-start.10 = (bf16[256,512]{1,0:T(8,128)(2,1)}, bf16[256,512]{1,0:T(8,128)(2,1)}, u32[]{:S(2)}, u32[]{:S(2)}) collective-permute-start(bf16[256,512]{1,0:T(8,128)(2,1)} %shard_map.47.refs_14_), channel_id=1, source_target_pairs={{0,16},{4,20},{8,24},{12,28},{16,32},{20,36},{24,40},{28,44},{32,4... | collective-permute-start | bytes 786440 | tf_op jit(solution)/shard_map/ppermute | solution.py:18
  81.7 4.6 %collective-permute-start.11 = (bf16[256,512]{1,0:T(8,128)(2,1)}, bf16[256,512]{1,0:T(8,128)(2,1)}, u32[]{:S(2)}, u32[]{:S(2)}) collective-permute-start(bf16[256,512]{1,0:T(8,128)(2,1)} %shard_map.48.refs_15_), channel_id=1, source_target_pairs={{16,0},{20,4},{24,8},{28,12},{32,16},{36,20},{40,24},{44,28},{48,3... | collective-permute-start | bytes 786440 | tf_op jit(solution)/shard_map/ppermute | solution.py:18
  86.5 3.2 %collective-permute-done.12.refs_13_ = bf16[256,512]{1,0:T(8,128)(2,1)} collective-permute-done((bf16[256,512]{1,0:T(8,128)(2,1)}, bf16[256,512]{1,0:T(8,128)(2,1)}, u32[]{:S(2)}, u32[]{:S(2)}) %collective-permute-start.12) | collective-permute-done | bytes 262176 | tf_op jit(solution)/shard_map/ppermute | solution.py:18
  89.7 4.4 %collective-permute-done.11.refs_12_ = bf16[256,512]{1,0:T(8,128)(2,1)} collective-permute-done((bf16[256,512]{1,0:T(8,128)(2,1)}, bf16[256,512]{1,0:T(8,128)(2,1)}, u32[]{:S(2)}, u32[]{:S(2)}) %collective-permute-start.11) | collective-permute-done | bytes 262176 | tf_op jit(solution)/shard_map/ppermute | solution.py:18
  94.1 8.9 %attend.1.a_ref = bf16[256,512]{1,0:T(8,128)(2,1)S(1)} custom-call(s32[13]{0:T(128)S(1)} %convert_element_type.9.flags, bf16[256,512]{1,0:T(8,128)(2,1)} %q_ref.1, bf16[256,512]{1,0:T(8,128)(2,1)} %refs_0_.1, bf16[256,512]{1,0:T(8,128)(2,1)} %refs_1_.1, bf16[512,512]{1,0:T(8,128)(2,1)} %copy-done.9, bf16[512,512]{1,0:T(8,128)(2,1)} %collective-permute-done.1.refs_3_, ...), custom_call_target="tpu_custom_call" | custom-call | flops 3000000000 | bytes 6000000 | tf_op jit(solution)/shard_map/attend/pallas_call | solution.py:174
  103.0 1.9 %collective-permute-start.13 = (bf16[256,512]{1,0:T(8,128)(2,1)S(1)}, bf16[256,512]{1,0:T(8,128)(2,1)S(1)}, u32[]{:S(2)}, u32[]{:S(2)}) collective-permute-start(bf16[256,512]{1,0:T(8,128)(2,1)S(1)} %attend.1.a_ref), channel_id=1, source_target_pairs={{0,1},{1,0},{2,3},{3,2},{4,5},{5,4},{6,7},{7,6},{8,9},{9,8},{10,11... | collective-permute-start | bytes 786440 | tf_op jit(solution)/shard_map/ppermute | solution.py:23
  108.0 6.0 %collective-permute-start.15 = (bf16[256,512]{1,0:T(8,128)(2,1)S(1)}, bf16[256,512]{1,0:T(8,128)(2,1)S(1)}, u32[]{:S(2)}, u32[]{:S(2)}) collective-permute-start(bf16[256,512]{1,0:T(8,128)(2,1)S(1)} %shard_map.51), channel_id=1, source_target_pairs={{0,2},{1,3},{2,0},{3,1},{4,6},{5,7},{6,4},{7,5},{8,10},{9,11},{10,... | collective-permute-start | bytes 786440 | tf_op jit(solution)/shard_map/ppermute | solution.py:23
  115.5 12.3 %collective-permute-done.15 = bf16[256,512]{1,0:T(8,128)(2,1)S(1)} collective-permute-done((bf16[256,512]{1,0:T(8,128)(2,1)S(1)}, bf16[256,512]{1,0:T(8,128)(2,1)S(1)}, u32[]{:S(2)}, u32[]{:S(2)}) %collective-permute-start.15) | collective-permute-done | bytes 262176 | tf_op jit(solution)/shard_map/ppermute | solution.py:23
  (40 shorter events, 12.9 us)
Async XLA Ops:
  0.0 106.5 %collective-permute-start.14 = (bf16[512,2048]{1,0:T(8,128)(2,1)}, bf16[512,2048]{1,0:T(8,128)(2,1)}, u32[]{:S(2)}, u32[]{:S(2)}) collective-permute-start(bf16[512,2048]{1,0:T(8,128)(2,1)} %wa_ref.3), channel_id=1, source_target_pairs={{0,1},{1,0},{2,3},{3,2},{4,5},{5,4},{6,7},{7,6},{8,9},{9,8},{10,11... | collective-permute-start | bytes 6291464 | tf_op jit(solution)/shard_map/ppermute | solution.py:23
  4.1 17.0 %collective-permute-start.2 = (bf16[256,512]{1,0:T(8,128)(2,1)S(1)}, bf16[256,512]{1,0:T(8,128)(2,1)S(1)}, u32[]{:S(2)}, u32[]{:S(2)}) collective-permute-start(bf16[256,512]{1,0:T(8,128)(2,1)S(1)} %get-tuple-element.9), channel_id=1, source_target_pairs={{0,8},{4,12},{8,0},{12,4},{16,24},{20,28},{24,16},{28,20},{32,40},... | collective-permute-start | bytes 786440 | tf_op jit(solution)/shard_map/ppermute | solution.py:18
  21.2 73.0 %copy-start.1 = (bf16[256,512]{1,0:T(8,128)(2,1)}, bf16[256,512]{1,0:T(8,128)(2,1)S(1)}, u32[]{:S(2)}) copy-start(bf16[256,512]{1,0:T(8,128)(2,1)S(1)} %collective-permute-done.2.one_ref.refs_4_) | copy-start | bytes 786436
  21.3 15.1 %collective-permute-start.6 = (bf16[256,512]{1,0:T(8,128)(2,1)S(1)}, bf16[256,512]{1,0:T(8,128)(2,1)S(1)}, u32[]{:S(2)}, u32[]{:S(2)}) collective-permute-start(bf16[256,512]{1,0:T(8,128)(2,1)S(1)} %shard_map.46.a_ref), channel_id=1, source_target_pairs={{0,4},{4,0},{8,12},{12,8},{16,20},{20,16},{24,28},{28,24},{32,36},... | collective-permute-start | bytes 786440 | tf_op jit(solution)/shard_map/ppermute | solution.py:18
  23.3 18.8 %collective-permute-start.3 = (bf16[256,512]{1,0:T(8,128)(2,1)S(1)}, bf16[256,512]{1,0:T(8,128)(2,1)S(1)}, u32[]{:S(2)}, u32[]{:S(2)}) collective-permute-start(bf16[256,512]{1,0:T(8,128)(2,1)S(1)} %collective-permute-done.2.one_ref.refs_4_), channel_id=1, source_target_pairs={{0,16},{4,20},{16,32},{20,36},{24,8},{28,12},{32,48},{36,52},{40,2... | collective-permute-start | bytes 786440 | tf_op jit(solution)/shard_map/ppermute | solution.py:18
  34.5 13.2 %collective-permute-start.5 = (bf16[256,512]{1,0:T(8,128)(2,1)S(1)}, bf16[256,512]{1,0:T(8,128)(2,1)S(1)}, u32[]{:S(2)}, u32[]{:S(2)}) collective-permute-start(bf16[256,512]{1,0:T(8,128)(2,1)S(1)} %shard_map.46.a_ref), channel_id=1, source_target_pairs={{0,16},{4,20},{8,24},{12,28},{16,32},{20,36},{24,40},{28,44},{32,4... | collective-permute-start | bytes 786440 | tf_op jit(solution)/shard_map/ppermute | solution.py:18
  36.4 15.7 %collective-permute-start.7 = (bf16[256,512]{1,0:T(8,128)(2,1)S(1)}, bf16[256,512]{1,0:T(8,128)(2,1)S(1)}, u32[]{:S(2)}, u32[]{:S(2)}) collective-permute-start(bf16[256,512]{1,0:T(8,128)(2,1)S(1)} %collective-permute-done.6.b_ref), channel_id=1, source_target_pairs={{0,16},{4,20},{8,24},{12,28},{16,32},{20,36},{24,40},{28,44},{32,4... | collective-permute-start | bytes 786440 | tf_op jit(solution)/shard_map/ppermute | solution.py:18
  38.3 40.0 %collective-permute-start = (bf16[512,512]{1,0:T(8,128)(2,1)S(1)}, bf16[512,512]{1,0:T(8,128)(2,1)S(1)}, u32[]{:S(2)}, u32[]{:S(2)}) collective-permute-start(bf16[512,512]{1,0:T(8,128)(2,1)S(1)} %get-tuple-element.8), channel_id=1, source_target_pairs={{0,4},{4,8},{8,12},{12,16},{16,20},{20,24},{24,28},{28,32},{32,36}... | collective-permute-start | bytes 1572872 | tf_op jit(solution)/shard_map/ppermute | solution.py:18
  42.1 44.4 %copy-start.8 = (bf16[256,512]{1,0:T(8,128)(2,1)}, bf16[256,512]{1,0:T(8,128)(2,1)S(1)}, u32[]{:S(2)}) copy-start(bf16[256,512]{1,0:T(8,128)(2,1)S(1)} %collective-permute-done.3.refs_5_) | copy-start | bytes 786436
  42.1 39.6 %collective-permute-start.1 = (bf16[512,512]{1,0:T(8,128)(2,1)S(1)}, bf16[512,512]{1,0:T(8,128)(2,1)}, u32[]{:S(2)}, u32[]{:S(2)}) collective-permute-start(bf16[512,512]{1,0:T(8,128)(2,1)S(1)} %get-tuple-element.8), channel_id=1, source_target_pairs={{4,0},{8,4},{12,8},{16,12},{20,16},{24,20},{28,24},{32,28},{36,32}... | collective-permute-start | bytes 1572872 | tf_op jit(solution)/shard_map/ppermute | solution.py:18
  47.7 46.5 %copy-start.2 = (bf16[256,512]{1,0:T(8,128)(2,1)}, bf16[256,512]{1,0:T(8,128)(2,1)S(1)}, u32[]{:S(2)}) copy-start(bf16[256,512]{1,0:T(8,128)(2,1)S(1)} %collective-permute-done.5.a_ref.refs_7_) | copy-start | bytes 786436
  47.7 21.2 %collective-permute-start.8 = (bf16[256,512]{1,0:T(8,128)(2,1)S(1)}, bf16[256,512]{1,0:T(8,128)(2,1)S(1)}, u32[]{:S(2)}, u32[]{:S(2)}) collective-permute-start(bf16[256,512]{1,0:T(8,128)(2,1)S(1)} %shard_map.46.a_ref), channel_id=1, source_target_pairs={{16,0},{20,4},{24,8},{28,12},{32,16},{36,20},{40,24},{44,28},{48,3... | collective-permute-start | bytes 786440 | tf_op jit(solution)/shard_map/ppermute | solution.py:18
  52.1 42.0 %copy-start.3 = (bf16[256,512]{1,0:T(8,128)(2,1)}, bf16[256,512]{1,0:T(8,128)(2,1)S(1)}, u32[]{:S(2)}) copy-start(bf16[256,512]{1,0:T(8,128)(2,1)S(1)} %collective-permute-done.7.b_ref.refs_8_) | copy-start | bytes 786436
  52.1 20.3 %collective-permute-start.9 = (bf16[256,512]{1,0:T(8,128)(2,1)S(1)}, bf16[256,512]{1,0:T(8,128)(2,1)S(1)}, u32[]{:S(2)}, u32[]{:S(2)}) collective-permute-start(bf16[256,512]{1,0:T(8,128)(2,1)S(1)} %collective-permute-done.6.b_ref), channel_id=1, source_target_pairs={{16,0},{20,4},{24,8},{28,12},{32,16},{36,20},{40,24},{44,28},{48,3... | collective-permute-start | bytes 786440 | tf_op jit(solution)/shard_map/ppermute | solution.py:18
  68.9 25.3 %copy-start.4 = (bf16[256,512]{1,0:T(8,128)(2,1)}, bf16[256,512]{1,0:T(8,128)(2,1)S(1)}, u32[]{:S(2)}) copy-start(bf16[256,512]{1,0:T(8,128)(2,1)S(1)} %collective-permute-done.8.a_ref.refs_9_) | copy-start | bytes 786436
  68.9 17.6 %collective-permute-start.4 = (bf16[256,512]{1,0:T(8,128)(2,1)}, bf16[256,512]{1,0:T(8,128)(2,1)}, u32[]{:S(2)}, u32[]{:S(2)}) collective-permute-start(bf16[256,512]{1,0:T(8,128)(2,1)} %broadcast_select_fusion), channel_id=1, source_target_pairs={{0,4},{4,0},{8,12},{12,8},{16,20},{20,16},{24,28},{28,24},{32,36},... | collective-permute-start | bytes 786440 | tf_op jit(solution)/shard_map/ppermute | solution.py:18
  72.4 17.4 %copy-start.5 = (bf16[256,512]{1,0:T(8,128)(2,1)}, bf16[256,512]{1,0:T(8,128)(2,1)S(1)}, u32[]{:S(2)}) copy-start(bf16[256,512]{1,0:T(8,128)(2,1)S(1)} %collective-permute-done.9.b_ref.refs_10_) | copy-start | bytes 786436
  72.4 17.4 %collective-permute-start.12 = (bf16[256,512]{1,0:T(8,128)(2,1)}, bf16[256,512]{1,0:T(8,128)(2,1)}, u32[]{:S(2)}, u32[]{:S(2)}) collective-permute-start(bf16[256,512]{1,0:T(8,128)(2,1)} %shard_map.49), channel_id=1, source_target_pairs={{0,48},{4,52},{8,56},{12,60},{32,80},{36,84},{40,88},{44,92},{48,0... | collective-permute-start | bytes 786440 | tf_op jit(solution)/shard_map/ppermute | solution.py:18
  78.3 8.1 %copy-start.9 = (bf16[512,512]{1,0:T(8,128)(2,1)}, bf16[512,512]{1,0:T(8,128)(2,1)S(1)}, u32[]{:S(2)}) copy-start(bf16[512,512]{1,0:T(8,128)(2,1)S(1)} %collective-permute-done.refs_2_) | copy-start | bytes 1572868
  78.3 11.4 %collective-permute-start.10 = (bf16[256,512]{1,0:T(8,128)(2,1)}, bf16[256,512]{1,0:T(8,128)(2,1)}, u32[]{:S(2)}, u32[]{:S(2)}) collective-permute-start(bf16[256,512]{1,0:T(8,128)(2,1)} %shard_map.47.refs_14_), channel_id=1, source_target_pairs={{0,16},{4,20},{8,24},{12,28},{16,32},{20,36},{24,40},{28,44},{32,4... | collective-permute-start | bytes 786440 | tf_op jit(solution)/shard_map/ppermute | solution.py:18
  81.7 12.4 %collective-permute-start.11 = (bf16[256,512]{1,0:T(8,128)(2,1)}, bf16[256,512]{1,0:T(8,128)(2,1)}, u32[]{:S(2)}, u32[]{:S(2)}) collective-permute-start(bf16[256,512]{1,0:T(8,128)(2,1)} %shard_map.48.refs_15_), channel_id=1, source_target_pairs={{16,0},{20,4},{24,8},{28,12},{32,16},{36,20},{40,24},{44,28},{48,3... | collective-permute-start | bytes 786440 | tf_op jit(solution)/shard_map/ppermute | solution.py:18
  86.5 20.0 %copy-start = (bf16[512,2048]{1,0:T(8,128)(2,1)S(1)}, bf16[512,2048]{1,0:T(8,128)(2,1)}, u32[]{:S(2)}) copy-start(bf16[512,2048]{1,0:T(8,128)(2,1)} %wa_ref.3) | copy-start | bytes 6291460
  103.0 3.4 %collective-permute-start.13 = (bf16[256,512]{1,0:T(8,128)(2,1)S(1)}, bf16[256,512]{1,0:T(8,128)(2,1)S(1)}, u32[]{:S(2)}, u32[]{:S(2)}) collective-permute-start(bf16[256,512]{1,0:T(8,128)(2,1)S(1)} %attend.1.a_ref), channel_id=1, source_target_pairs={{0,1},{1,0},{2,3},{3,2},{4,5},{5,4},{6,7},{7,6},{8,9},{9,8},{10,11... | collective-permute-start | bytes 786440 | tf_op jit(solution)/shard_map/ppermute | solution.py:23
  108.0 19.8 %collective-permute-start.15 = (bf16[256,512]{1,0:T(8,128)(2,1)S(1)}, bf16[256,512]{1,0:T(8,128)(2,1)S(1)}, u32[]{:S(2)}, u32[]{:S(2)}) collective-permute-start(bf16[256,512]{1,0:T(8,128)(2,1)S(1)} %shard_map.51), channel_id=1, source_target_pairs={{0,2},{1,3},{2,0},{3,1},{4,6},{5,7},{6,4},{7,5},{8,10},{9,11},{10,... | collective-permute-start | bytes 786440 | tf_op jit(solution)/shard_map/ppermute | solution.py:23
  (2 other events, 1.9 us)

commit v2 on v1

--- a/solution.py
+++ b/solution.py
@@ -75,38 +75,52 @@
         out_ref[base + 64 : base + 128] = dot(half, one_ref[base : base + 128]).astype(jnp.bfloat16)
 
 
-def halve_kernel(a_ref, b_ref, out_ref):
+def halve_kernel(block_ref, out_ref):
+    half = mean_matrix(128, 2)
+    for part in range(2):
+        out_ref[part * 128 : (part + 1) * 128] = dot(
+            half, block_ref[part * 256 : (part + 1) * 256]
+        ).astype(jnp.bfloat16)
+
+
+def pack_kernel(a_ref, b_ref, two_ref, three_ref):
     half = mean_matrix(64, 2)
     for part in range(2):
-        base = part * 128
         for index, ref in enumerate((a_ref, b_ref)):
-            start = base + index * 64
-            out_ref[start : start + 64] = dot(half, ref[base : base + 128]).astype(jnp.bfloat16)
-
-
-def small(kernel, a, b):
+            value = ref[part * 128 : (part + 1) * 128]
+            start = part * 256 + index * 128
+            two_ref[start : start + 128] = value
+            three_ref[start // 2 : start // 2 + 64] = dot(half, value).astype(jnp.bfloat16)
+
+
+def small(kernel, *operands, rows=(256,)):
+    width, dtype = operands[0].shape[1], operands[0].dtype
+    shapes = tuple(jax.ShapeDtypeStruct((count, width), dtype) for count in rows)
     return pl.pallas_call(
         kernel,
-        out_shape=jax.ShapeDtypeStruct((256, a.shape[1]), a.dtype),
+        out_shape=shapes if len(rows) > 1 else shapes[0],
         compiler_params=pltpu.CompilerParams(vmem_limit_bytes=4 * MIB),
         cost_estimate=pl.CostEstimate(flops=10**8, bytes_accessed=10**6, transcendentals=0),
-    )(a, b)
-
-
-KEYS = 768 + 3 * 512
-
-
-def attend_kernel(flags, q_ref, *refs):
+    )(*operands)
+
+
+LATE = 2 * 128
+KEYS = 768 + 3 * 512 - LATE
+SCALE = LOG2E * HEAD_DIM**-0.5
+
+
+def bias(flags, index):
+    return jnp.where(flags[index] > 0, 0.0, -jnp.inf)
+
+
+def main_kernel(flags, q_ref, *refs):
     k_ref, v_ref, left, right = refs[0:4]
     ones = refs[4:7]
-    twos = refs[7:11]
-    threes = refs[11:14]
-    nears = refs[14:16]
-    out_ref = refs[16]
-    scores, weights, values = refs[17:20]
-
-    def bias(index):
-        return jnp.where(flags[index] > 0, 0.0, -jnp.inf)
+    twos = refs[7:9]
+    skew = refs[9]
+    nears = refs[10:12]
+    sum_ref, weight_ref, top_ref = refs[12:15]
+    scores, weights, values = refs[15:18]
 
     even = flags[6] > 0
     half = mean_matrix(128, 2)
@@ -129,9 +143,8 @@
         pieces.append((ref[:128], ref[128:], 1, (None, 10, 11)[index]))
     pieces.append((fourth[0], fourth[1], 1, 12))
     for index, ref in enumerate(twos):
-        pieces.append((ref[:128], ref[128:], 2, 3 + index // 2))
-    for index, ref in enumerate(threes):
-        pieces.append((ref[:128], ref[128:], 3, (5, 7, 8)[index]))
+        pieces.append((ref[:256], ref[256:], 2, 3 + index))
+    pieces.append((skew[:128], skew[128:], 3, 8))
     pieces.append((near[0], near[1], 3, 9))
 
     query = q_ref[...]
@@ -147,7 +160,7 @@
         count = keys.shape[0]
         part = dot_t(queries[level], keys)
         if flag is not None:
-            part = part + bias(flag)
+            part = part + bias(flags, flag)
         scores[:, start : start + count] = part
         values[start : start + count, :HEAD_DIM] = vals
         for column in range(0, count, 128):
@@ -155,37 +168,72 @@
             largest = piece if largest is None else jnp.maximum(largest, piece)
         spans.append((start, count, level))
         start += count
-    scale = LOG2E * HEAD_DIM**-0.5
-    top = jnp.max(largest, axis=1, keepdims=True) * scale
+    top = jnp.max(largest, axis=1, keepdims=True) * SCALE
     for start, count, level in spans:
-        shifted = scores[:, start : start + count] * scale - (top - level)
+        shifted = scores[:, start : start + count] * SCALE - (top - level)
         weights[:, start : start + count] = jnp.exp2(shifted).astype(jnp.bfloat16)
     total = dot(weights[...], values[...])
-    out_ref[...] = (total[:, :HEAD_DIM] / total[:, HEAD_DIM:]).astype(jnp.bfloat16)
-
-
-def attend(flags, q, tensors):
-    rows, width = q.shape
-    heads = width // HEAD_DIM
-
+    sum_ref[...] = total[:, :HEAD_DIM]
+    weight_ref[...] = total[:, HEAD_DIM:]
+    top_ref[...] = jnp.broadcast_to(top, top_ref.shape)
+
+
+def late_kernel(flags, q_ref, sum_ref, weight_ref, top_ref, low, high, out_ref, values):
+    query = q_ref[...]
+    query = dot(spread_mean_matrix(query.shape[0], 8), query).astype(jnp.bfloat16)
+    values[:, HEAD_DIM:] = jnp.ones((LATE, HEAD_DIM), jnp.bfloat16)
+    parts = []
+    for index, (ref, flag) in enumerate(((low, 5), (high, 7))):
+        parts.append(dot_t(query, ref[:128]) + bias(flags, flag))
+        values[index * 128 : (index + 1) * 128, :HEAD_DIM] = ref[128:]
+    early = top_ref[...]
+    top = jnp.max(jnp.maximum(parts[0], parts[1]), axis=1, keepdims=True) * SCALE
+    top = jnp.maximum(early, top)
+    kept = jnp.exp2(early - top)
+    part = jnp.concatenate([jnp.exp2(p * SCALE - (top - 3.0)) for p in parts], 1)
+    total = dot(part.astype(jnp.bfloat16), values[...])
+    numerator = sum_ref[...] * kept + total[:, :HEAD_DIM]
+    denominator = weight_ref[...] * kept + total[:, HEAD_DIM:]
+    out_ref[...] = (numerator / denominator).astype(jnp.bfloat16)
+
+
+def heads_call(kernel, flags, tensors, outs, scratch, limit, flops):
     def spec(value):
         return pl.BlockSpec((value.shape[0], HEAD_DIM), lambda h: (0, h))
 
+    out_specs = tuple(spec(out) for out in outs)
     return pl.pallas_call(
-        attend_kernel,
-        grid=(heads,),
-        in_specs=[pl.BlockSpec(memory_space=pltpu.SMEM), spec(q)] + [spec(t) for t in tensors],
-        out_specs=spec(q),
-        out_shape=jax.ShapeDtypeStruct((rows, width), jnp.bfloat16),
-        scratch_shapes=[
-            pltpu.VMEM((rows, KEYS), jnp.float32),
-            pltpu.VMEM((rows, KEYS), jnp.bfloat16),
-            pltpu.VMEM((KEYS, 2 * HEAD_DIM), jnp.bfloat16),
-        ],
-        compiler_params=pltpu.CompilerParams(vmem_limit_bytes=32 * MIB),
-        cost_estimate=pl.CostEstimate(flops=3 * 10**9, bytes_accessed=6 * 10**6, transcendentals=0),
-        name="attend",
-    )(flags, q, *tensors)
+        kernel,
+        grid=(tensors[0].shape[1] // HEAD_DIM,),
+        in_specs=[pl.BlockSpec(memory_space=pltpu.SMEM)] + [spec(t) for t in tensors],
+        out_specs=out_specs if len(outs) > 1 else out_specs[0],
+        out_shape=tuple(outs) if len(outs) > 1 else outs[0],
+        scratch_shapes=scratch,
+        compiler_params=pltpu.CompilerParams(vmem_limit_bytes=limit * MIB),
+        cost_estimate=pl.CostEstimate(flops=flops, bytes_accessed=6 * 10**6, transcendentals=0),
+    )(flags, *tensors)
+
+
+def in_hbm(values):
+    return [pltpu.with_memory_space_constraint(value, pltpu.HBM) for value in values]
+
+
+def attend_main(flags, tensors):
+    rows, width = tensors[0].shape
+    outs = [jax.ShapeDtypeStruct((rows, width), jnp.float32)] * 3
+    scratch = [
+        pltpu.VMEM((rows, KEYS), jnp.float32),
+        pltpu.VMEM((rows, KEYS), jnp.bfloat16),
+        pltpu.VMEM((KEYS, 2 * HEAD_DIM), jnp.bfloat16),
+    ]
+    return heads_call(main_kernel, flags, in_hbm(tensors), outs, scratch, 32, 3 * 10**9)
+
+
+def attend_late(flags, tensors):
+    rows, width = tensors[0].shape
+    outs = [jax.ShapeDtypeStruct((rows, width), jnp.bfloat16)]
+    scratch = [pltpu.VMEM((LATE, 2 * HEAD_DIM), jnp.bfloat16)]
+    return heads_call(late_kernel, flags, tensors, outs, scratch, 16, 3 * 10**8)
 
 
 def project_kernel(column, a_ref, b_ref, wa_ref, wb_ref, out_ref):
@@ -222,23 +270,21 @@
 
     raw, own_one, own_two = coarse(key_rows, value_rows)
     across = seq_permute(own_one, lambda i: i ^ 2)
+    peer_weight = head_permute(out_weight, 1)
     two_half = small(half_kernel, own_two, across)
     two_beside = seq_permute(two_half, lambda i: i ^ 1)
-    low_a = seq_permute(two_half, lambda i: i + 4)
-    high_a = seq_permute(two_half, lambda i: i - 4)
     far = seq_permute(across, lambda i: i + 4 if i % 4 < 2 else i - 4)
     left = seq_permute(raw, lambda i: i + 1)
     right = seq_permute(raw, lambda i: i - 1)
-    low_b = seq_permute(two_beside, lambda i: i + 4)
-    high_b = seq_permute(two_beside, lambda i: i - 4)
-    three_block = small(halve_kernel, two_half, two_beside)
-    three_skew = seq_permute(three_block, lambda i: i + 12 if i // 4 % 2 == 0 else i - 12)
-    peer_weight = head_permute(out_weight, 1)
+    two_block, three_block = small(pack_kernel, two_half, two_beside, rows=(512, 256))
+    two_low = seq_permute(two_block, lambda i: i + 4)
+    two_high = seq_permute(two_block, lambda i: i - 4)
     outer = (spot == 0) | (spot == 3)
     handed = jnp.where(outer, far, across)
     third = seq_permute(handed, lambda i: i ^ 1)
-    near_low = small(halve_kernel, low_a, low_b)
-    near_high = small(halve_kernel, high_a, high_b)
+    three_skew = seq_permute(three_block, lambda i: i + 12 if i // 4 % 2 == 0 else i - 12)
+    near_low = small(halve_kernel, two_low)
+    near_high = small(halve_kernel, two_high)
     three_low = seq_permute(near_low, lambda i: i + 4)
     three_high = seq_permute(near_high, lambda i: i - 4)
 
@@ -260,12 +306,10 @@
             jnp.logical_not(outer) | far_ok,
         ]
     ).astype(jnp.int32)
-    tensors = [key_rows, value_rows, left, right, across, far, third]
-    tensors += [low_a, low_b, high_a, high_b, three_low, three_high, three_skew]
-    tensors += [near_low, near_high]
-    tensors = [pltpu.with_memory_space_constraint(t, pltpu.HBM) for t in tensors]
-    own_queries = pltpu.with_memory_space_constraint(queries, pltpu.HBM)
-    attended = attend(flags, own_queries, tensors)
+    tensors = [queries, key_rows, value_rows, left, right, across, far, third]
+    tensors += [two_low, two_high, three_skew, near_low, near_high]
+    partial = attend_main(flags, tensors)
+    attended = attend_late(flags, [queries, *partial, three_low, three_high])
     peer = head_permute(attended, 1)
     here_column, away_column = head.reshape(1), (head ^ 2).reshape(1)
     weights = (out_weight, peer_weight)

time: 129 us -> 122 us (0.946)
  the two profiles are of different devices: /device:TPU:30 before, /device:TPU:15 now
where the time goes in v2:
time: 122 us; the launch traced here: 121 us
  starting transfers between devices  66.8 us (55%)
  waiting for transfers between devices  33.8 us (28%)
  Pallas kernels  16 us (13%)
  local copies, waits for them, and re-layouts  3.41 us (3%)
    ppermute x11, starting transfers between devices, seq_permute(): return lax.ppermute(value, 'seq', pairs)  48 us
    ppermute x11, waiting for transfers between devices, seq_permute(): return lax.ppermute(value, 'seq', pairs)  22.3 us
    ppermute x3, starting transfers between devices, head_permute(): return lax.ppermute(value, 'head', [(i, i ^ bit) for i in range(count)])  18.8 us
    pallas_call x2, Pallas kernels, heads_call(): pl.pallas_call(kernel, grid=(tensors[0].shape[1] // HEAD_DIM,), in_specs=...  11.8 us
    ppermute x3, waiting for transfers between devices, head_permute(): return lax.ppermute(value, 'head', [(i, i ^ bit) for i in range(count)])  11.5 us
    unnamed x24, local copies, waits for them, and re-layouts  3.3 us
    pallas_call x2, Pallas kernels, project(): pl.pallas_call(project_kernel, grid_spec=pltpu.PrefetchScalarGridSpec(num...  3.03 us
  transfers between devices with their start and end apart: 14, of which 7 were waited for; matrix products, arithmetic and copies ran while one was open for 0% of the time, Pallas kernels for 12%

profile of v2, /device:TPU:15, one launch (start us, length us, event | category | flops | bytes accessed | tf_op | source)
XLA Modules:
  0.0 121.3 jit_solution(10995854056574979592)
XLA Ops:
  0.0 2.6 %collective-permute-start.12 = (bf16[512,2048]{1,0:T(8,128)(2,1)}, bf16[512,2048]{1,0:T(8,128)(2,1)}, u32[]{:S(2)}, u32[]{:S(2)}) collective-permute-start(bf16[512,2048]{1,0:T(8,128)(2,1)} %wa_ref.3), channel_id=1, source_target_pairs={{0,1},{1,0},{2,3},{3,2},{4,5},{5,4},{6,7},{7,6},{8,9},{9,8},{10,11... | collective-permute-start | bytes 6291464 | tf_op jit(solution)/shard_map/ppermute | solution.py:23
  4.8 4.2 %collective-permute-start.2 = (bf16[256,512]{1,0:T(8,128)(2,1)S(1)}, bf16[256,512]{1,0:T(8,128)(2,1)S(1)}, u32[]{:S(2)}, u32[]{:S(2)}) collective-permute-start(bf16[256,512]{1,0:T(8,128)(2,1)S(1)} %get-tuple-element.14), channel_id=1, source_target_pairs={{0,8},{4,12},{8,0},{12,4},{16,24},{20,28},{24,16},{28,20},{32,40},... | collective-permute-start | bytes 786440 | tf_op jit(solution)/shard_map/ppermute | solution.py:18
  9.0 11.6 %collective-permute-done.2.one_ref.refs_4_ = bf16[256,512]{1,0:T(8,128)(2,1)S(1)} collective-permute-done((bf16[256,512]{1,0:T(8,128)(2,1)S(1)}, bf16[256,512]{1,0:T(8,128)(2,1)S(1)}, u32[]{:S(2)}, u32[]{:S(2)}) %collective-permute-start.2) | collective-permute-done | bytes 262176 | tf_op jit(solution)/shard_map/ppermute | solution.py:18
  20.8 2.5 %collective-permute-start.5 = (bf16[256,512]{1,0:T(8,128)(2,1)S(1)}, bf16[256,512]{1,0:T(8,128)(2,1)S(1)}, u32[]{:S(2)}, u32[]{:S(2)}) collective-permute-start(bf16[256,512]{1,0:T(8,128)(2,1)S(1)} %shard_map.46.a_ref), channel_id=1, source_target_pairs={{0,4},{4,0},{8,12},{12,8},{16,20},{20,16},{24,28},{28,24},{32,36},... | collective-permute-start | bytes 786440 | tf_op jit(solution)/shard_map/ppermute | solution.py:18
  23.3 4.0 %collective-permute-start.3 = (bf16[256,512]{1,0:T(8,128)(2,1)S(1)}, bf16[256,512]{1,0:T(8,128)(2,1)S(1)}, u32[]{:S(2)}, u32[]{:S(2)}) collective-permute-start(bf16[256,512]{1,0:T(8,128)(2,1)S(1)} %collective-permute-done.2.one_ref.refs_4_), channel_id=1, source_target_pairs={{0,16},{4,20},{16,32},{20,36},{24,8},{28,12},{32,48},{36,52},{40,2... | collective-permute-start | bytes 786440 | tf_op jit(solution)/shard_map/ppermute | solution.py:18
  27.3 2.7 %collective-permute-done.5.b_ref = bf16[256,512]{1,0:T(8,128)(2,1)S(1)} collective-permute-done((bf16[256,512]{1,0:T(8,128)(2,1)S(1)}, bf16[256,512]{1,0:T(8,128)(2,1)S(1)}, u32[]{:S(2)}, u32[]{:S(2)}) %collective-permute-start.5) | collective-permute-done | bytes 262176 | tf_op jit(solution)/shard_map/ppermute | solution.py:18
  30.3 4.0 %collective-permute-start.6 = (bf16[512,512]{1,0:T(8,128)(2,1)S(1)}, bf16[512,512]{1,0:T(8,128)(2,1)S(1)}, u32[]{:S(2)}, u32[]{:S(2)}) collective-permute-start(bf16[512,512]{1,0:T(8,128)(2,1)S(1)} %get-tuple-element.16), channel_id=1, source_target_pairs={{0,16},{4,20},{8,24},{12,28},{16,32},{20,36},{24,40},{28,44},{32,4... | collective-permute-start | bytes 1572872 | tf_op jit(solution)/shard_map/ppermute | solution.py:18
  34.3 8.9 %collective-permute-start.7 = (bf16[512,512]{1,0:T(8,128)(2,1)S(1)}, bf16[512,512]{1,0:T(8,128)(2,1)S(1)}, u32[]{:S(2)}, u32[]{:S(2)}) collective-permute-start(bf16[512,512]{1,0:T(8,128)(2,1)S(1)} %get-tuple-element.16), channel_id=1, source_target_pairs={{16,0},{20,4},{24,8},{28,12},{32,16},{36,20},{40,24},{44,28},{48,3... | collective-permute-start | bytes 1572872 | tf_op jit(solution)/shard_map/ppermute | solution.py:18
  43.2 4.1 %collective-permute-start = (bf16[512,512]{1,0:T(8,128)(2,1)S(1)}, bf16[512,512]{1,0:T(8,128)(2,1)}, u32[]{:S(2)}, u32[]{:S(2)}) collective-permute-start(bf16[512,512]{1,0:T(8,128)(2,1)S(1)} %get-tuple-element.13), channel_id=1, source_target_pairs={{0,4},{4,8},{8,12},{12,16},{16,20},{20,24},{24,28},{28,32},{32,36}... | collective-permute-start | bytes 1572872 | tf_op jit(solution)/shard_map/ppermute | solution.py:18
  47.3 1.9 %collective-permute-start.1 = (bf16[512,512]{1,0:T(8,128)(2,1)S(1)}, bf16[512,512]{1,0:T(8,128)(2,1)}, u32[]{:S(2)}, u32[]{:S(2)}) collective-permute-start(bf16[512,512]{1,0:T(8,128)(2,1)S(1)} %get-tuple-element.13), channel_id=1, source_target_pairs={{4,0},{8,4},{12,8},{16,12},{20,16},{24,20},{28,24},{32,28},{36,32}... | collective-permute-start | bytes 1572872 | tf_op jit(solution)/shard_map/ppermute | solution.py:18
  49.3 2.9 %collective-permute-done.6.block_ref.refs_7_ = bf16[512,512]{1,0:T(8,128)(2,1)S(1)} collective-permute-done((bf16[512,512]{1,0:T(8,128)(2,1)S(1)}, bf16[512,512]{1,0:T(8,128)(2,1)S(1)}, u32[]{:S(2)}, u32[]{:S(2)}) %collective-permute-start.6) | collective-permute-done | bytes 524320 | tf_op jit(solution)/shard_map/ppermute | solution.py:18
  52.2 3.3 %collective-permute-start.4 = (bf16[256,512]{1,0:T(8,128)(2,1)S(1)}, bf16[256,512]{1,0:T(8,128)(2,1)S(1)}, u32[]{:S(2)}, u32[]{:S(2)}) collective-permute-start(bf16[256,512]{1,0:T(8,128)(2,1)S(1)} %broadcast_select_fusion), channel_id=1, source_target_pairs={{0,4},{4,0},{8,12},{12,8},{16,20},{20,16},{24,28},{28,24},{32,36},... | collective-permute-start | bytes 786440 | tf_op jit(solution)/shard_map/ppermute | solution.py:18
  55.6 2.6 %collective-permute-start.8 = (bf16[256,512]{1,0:T(8,128)(2,1)S(1)}, bf16[256,512]{1,0:T(8,128)(2,1)S(1)}, u32[]{:S(2)}, u32[]{:S(2)}) collective-permute-start(bf16[256,512]{1,0:T(8,128)(2,1)S(1)} %get-tuple-element.17), channel_id=1, source_target_pairs={{0,48},{4,52},{8,56},{12,60},{32,80},{36,84},{40,88},{44,92},{48,0... | collective-permute-start | bytes 786440 | tf_op jit(solution)/shard_map/ppermute | solution.py:18
  58.8 10.6 %collective-permute-start.10 = (bf16[256,512]{1,0:T(8,128)(2,1)S(1)}, bf16[256,512]{1,0:T(8,128)(2,1)S(1)}, u32[]{:S(2)}, u32[]{:S(2)}) collective-permute-start(bf16[256,512]{1,0:T(8,128)(2,1)S(1)} %shard_map.49.refs_11_), channel_id=1, source_target_pairs={{16,0},{20,4},{24,8},{28,12},{32,16},{36,20},{40,24},{44,28},{48,3... | collective-permute-start | bytes 786440 | tf_op jit(solution)/shard_map/ppermute | solution.py:18
  69.4 2.5 %collective-permute-done.1.refs_3_ = bf16[512,512]{1,0:T(8,128)(2,1)} collective-permute-done((bf16[512,512]{1,0:T(8,128)(2,1)S(1)}, bf16[512,512]{1,0:T(8,128)(2,1)}, u32[]{:S(2)}, u32[]{:S(2)}) %collective-permute-start.1) | collective-permute-done | bytes 524320 | tf_op jit(solution)/shard_map/ppermute | solution.py:18
  71.9 1.9 %collective-permute-start.9 = (bf16[256,512]{1,0:T(8,128)(2,1)S(1)}, bf16[256,512]{1,0:T(8,128)(2,1)S(1)}, u32[]{:S(2)}, u32[]{:S(2)}) collective-permute-start(bf16[256,512]{1,0:T(8,128)(2,1)S(1)} %shard_map.48.refs_10_), channel_id=1, source_target_pairs={{0,16},{4,20},{8,24},{12,28},{16,32},{20,36},{24,40},{28,44},{32,4... | collective-permute-start | bytes 786440 | tf_op jit(solution)/shard_map/ppermute | solution.py:18
  73.8 2.6 %collective-permute-done.4.refs_6_ = bf16[256,512]{1,0:T(8,128)(2,1)S(1)} collective-permute-done((bf16[256,512]{1,0:T(8,128)(2,1)S(1)}, bf16[256,512]{1,0:T(8,128)(2,1)S(1)}, u32[]{:S(2)}, u32[]{:S(2)}) %collective-permute-start.4) | collective-permute-done | bytes 262176 | tf_op jit(solution)/shard_map/ppermute | solution.py:18
  77.8 8.5 %shard_map.50 = (f32[256,512]{1,0:T(8,128)S(1)}, f32[256,512]{1,0:T(8,128)S(1)}, f32[256,512]{1,0:T(8,128)S(1)}) custom-call(s32[13]{0:T(128)S(1)} %convert_element_type.9.flags, bf16[256,512]{1,0:T(8,128)(2,1)} %q_ref.3, bf16[256,512]{1,0:T(8,128)(2,1)} %refs_0_.1, bf16[256,512]{1,0:T(8,128)(2,1)} %refs_1_.1, ...), custom_call_target="tpu_custom_call" | custom-call | flops 3000000000 | bytes 6000000 | tf_op jit(solution)/shard_map/pallas_call | solution.py:205
  86.4 3.3 %shard_map.51.a_ref = bf16[256,512]{1,0:T(8,128)(2,1)S(1)} custom-call(s32[13]{0:T(128)S(1)} %convert_element_type.9.flags, bf16[256,512]{1,0:T(8,128)(2,1)S(1)} %copy-done.8, f32[256,512]{1,0:T(8,128)S(1)} %get-tuple-element.18.sum_ref, f32[256,512]{1,0:T(8,128)S(1)} %get-tuple-element.19.weight_ref, f32[256,512]{1,0:T(8,128)S(1)} %get-tuple-element.20.top_ref, ...), custom_call_target="tpu_custom_call" | custom-call | flops 300000000 | bytes 6000000 | tf_op jit(solution)/shard_map/pallas_call | solution.py:205
  89.7 4.9 %collective-permute-start.11 = (bf16[256,512]{1,0:T(8,128)(2,1)S(1)}, bf16[256,512]{1,0:T(8,128)(2,1)S(1)}, u32[]{:S(2)}, u32[]{:S(2)}) collective-permute-start(bf16[256,512]{1,0:T(8,128)(2,1)S(1)} %shard_map.51.a_ref), channel_id=1, source_target_pairs={{0,1},{1,0},{2,3},{3,2},{4,5},{5,4},{6,7},{7,6},{8,9},{9,8},{10,11... | collective-permute-start | bytes 786440 | tf_op jit(solution)/shard_map/ppermute | solution.py:23
  95.8 1.5 %shard_map.53 = bf16[256,512]{1,0:T(8,128)(2,1)S(1)} custom-call(s32[1]{0:T(128)} %bitcast.14.column, bf16[256,512]{1,0:T(8,128)(2,1)S(1)} %shard_map.51.a_ref, bf16[256,512]{1,0:T(8,128)(2,1)S(1)} %collective-permute-done.11.b_ref, bf16[512,2048]{1,0:T(8,128)(2,1)S(1)} %copy-done, bf16[512,2048]{1,0:T(8,128)(2,1)} %collective-permute-done.12.wb_ref), custom_call_target="tpu_custom_call" | custom-call | flops 1000000000 | bytes 1000000 | tf_op jit(solution)/shard_map/pallas_call | solution.py:248
  97.3 11.3 %collective-permute-start.13 = (bf16[256,512]{1,0:T(8,128)(2,1)S(1)}, bf16[256,512]{1,0:T(8,128)(2,1)S(1)}, u32[]{:S(2)}, u32[]{:S(2)}) collective-permute-start(bf16[256,512]{1,0:T(8,128)(2,1)S(1)} %shard_map.53), channel_id=1, source_target_pairs={{0,2},{1,3},{2,0},{3,1},{4,6},{5,7},{6,4},{7,5},{8,10},{9,11},{10,... | collective-permute-start | bytes 786440 | tf_op jit(solution)/shard_map/ppermute | solution.py:23
  108.6 1.5 %shard_map.52 = f32[256,512]{1,0:T(8,128)S(1)} custom-call(s32[1]{0:T(128)} %bitcast.column, bf16[256,512]{1,0:T(8,128)(2,1)S(1)} %shard_map.51.a_ref, bf16[256,512]{1,0:T(8,128)(2,1)S(1)} %collective-permute-done.11.b_ref, bf16[512,2048]{1,0:T(8,128)(2,1)S(1)} %copy-done, bf16[512,2048]{1,0:T(8,128)(2,1)} %collective-permute-done.12.wb_ref), custom_call_target="tpu_custom_call" | custom-call | flops 1000000000 | bytes 1000000 | tf_op jit(solution)/shard_map/pallas_call | solution.py:248
  110.1 10.4 %collective-permute-done.13 = bf16[256,512]{1,0:T(8,128)(2,1)S(1)} collective-permute-done((bf16[256,512]{1,0:T(8,128)(2,1)S(1)}, bf16[256,512]{1,0:T(8,128)(2,1)S(1)}, u32[]{:S(2)}, u32[]{:S(2)}) %collective-permute-start.13) | collective-permute-done | bytes 262176 | tf_op jit(solution)/shard_map/ppermute | solution.py:23
  (41 shorter events, 6.5 us)
Async XLA Ops:
  0.0 95.8 %collective-permute-start.12 = (bf16[512,2048]{1,0:T(8,128)(2,1)}, bf16[512,2048]{1,0:T(8,128)(2,1)}, u32[]{:S(2)}, u32[]{:S(2)}) collective-permute-start(bf16[512,2048]{1,0:T(8,128)(2,1)} %wa_ref.3), channel_id=1, source_target_pairs={{0,1},{1,0},{2,3},{3,2},{4,5},{5,4},{6,7},{7,6},{8,9},{9,8},{10,11... | collective-permute-start | bytes 6291464 | tf_op jit(solution)/shard_map/ppermute | solution.py:23
  2.6 1.0 copy-start.6
  3.5 0.9 copy-start.7
  4.8 15.8 %collective-permute-start.2 = (bf16[256,512]{1,0:T(8,128)(2,1)S(1)}, bf16[256,512]{1,0:T(8,128)(2,1)S(1)}, u32[]{:S(2)}, u32[]{:S(2)}) collective-permute-start(bf16[256,512]{1,0:T(8,128)(2,1)S(1)} %get-tuple-element.14), channel_id=1, source_target_pairs={{0,8},{4,12},{8,0},{12,4},{16,24},{20,28},{24,16},{28,20},{32,40},... | collective-permute-start | bytes 786440 | tf_op jit(solution)/shard_map/ppermute | solution.py:18
  20.6 55.8 %copy-start.1 = (bf16[256,512]{1,0:T(8,128)(2,1)}, bf16[256,512]{1,0:T(8,128)(2,1)S(1)}, u32[]{:S(2)}) copy-start(bf16[256,512]{1,0:T(8,128)(2,1)S(1)} %collective-permute-done.2.one_ref.refs_4_) | copy-start | bytes 786436
  20.8 9.3 %collective-permute-start.5 = (bf16[256,512]{1,0:T(8,128)(2,1)S(1)}, bf16[256,512]{1,0:T(8,128)(2,1)S(1)}, u32[]{:S(2)}, u32[]{:S(2)}) collective-permute-start(bf16[256,512]{1,0:T(8,128)(2,1)S(1)} %shard_map.46.a_ref), channel_id=1, source_target_pairs={{0,4},{4,0},{8,12},{12,8},{16,20},{20,16},{24,28},{28,24},{32,36},... | collective-permute-start | bytes 786440 | tf_op jit(solution)/shard_map/ppermute | solution.py:18
  23.3 24.0 %collective-permute-start.3 = (bf16[256,512]{1,0:T(8,128)(2,1)S(1)}, bf16[256,512]{1,0:T(8,128)(2,1)S(1)}, u32[]{:S(2)}, u32[]{:S(2)}) collective-permute-start(bf16[256,512]{1,0:T(8,128)(2,1)S(1)} %collective-permute-done.2.one_ref.refs_4_), channel_id=1, source_target_pairs={{0,16},{4,20},{16,32},{20,36},{24,8},{28,12},{32,48},{36,52},{40,2... | collective-permute-start | bytes 786440 | tf_op jit(solution)/shard_map/ppermute | solution.py:18
  30.3 21.9 %collective-permute-start.6 = (bf16[512,512]{1,0:T(8,128)(2,1)S(1)}, bf16[512,512]{1,0:T(8,128)(2,1)S(1)}, u32[]{:S(2)}, u32[]{:S(2)}) collective-permute-start(bf16[512,512]{1,0:T(8,128)(2,1)S(1)} %get-tuple-element.16), channel_id=1, source_target_pairs={{0,16},{4,20},{8,24},{12,28},{16,32},{20,36},{24,40},{28,44},{32,4... | collective-permute-start | bytes 1572872 | tf_op jit(solution)/shard_map/ppermute | solution.py:18
  34.3 21.2 %collective-permute-start.7 = (bf16[512,512]{1,0:T(8,128)(2,1)S(1)}, bf16[512,512]{1,0:T(8,128)(2,1)S(1)}, u32[]{:S(2)}, u32[]{:S(2)}) collective-permute-start(bf16[512,512]{1,0:T(8,128)(2,1)S(1)} %get-tuple-element.16), channel_id=1, source_target_pairs={{16,0},{20,4},{24,8},{28,12},{32,16},{36,20},{40,24},{44,28},{48,3... | collective-permute-start | bytes 1572872 | tf_op jit(solution)/shard_map/ppermute | solution.py:18
  43.2 15.7 %collective-permute-start = (bf16[512,512]{1,0:T(8,128)(2,1)S(1)}, bf16[512,512]{1,0:T(8,128)(2,1)}, u32[]{:S(2)}, u32[]{:S(2)}) collective-permute-start(bf16[512,512]{1,0:T(8,128)(2,1)S(1)} %get-tuple-element.13), channel_id=1, source_target_pairs={{0,4},{4,8},{8,12},{12,16},{16,20},{20,24},{24,28},{28,32},{32,36}... | collective-permute-start | bytes 1572872 | tf_op jit(solution)/shard_map/ppermute | solution.py:18
  47.3 29.1 %copy-start.9 = (bf16[256,512]{1,0:T(8,128)(2,1)}, bf16[256,512]{1,0:T(8,128)(2,1)S(1)}, u32[]{:S(2)}) copy-start(bf16[256,512]{1,0:T(8,128)(2,1)S(1)} %collective-permute-done.3.refs_5_) | copy-start | bytes 786436
  47.3 24.6 %collective-permute-start.1 = (bf16[512,512]{1,0:T(8,128)(2,1)S(1)}, bf16[512,512]{1,0:T(8,128)(2,1)}, u32[]{:S(2)}, u32[]{:S(2)}) collective-permute-start(bf16[512,512]{1,0:T(8,128)(2,1)S(1)} %get-tuple-element.13), channel_id=1, source_target_pairs={{4,0},{8,4},{12,8},{16,12},{20,16},{24,20},{28,24},{32,28},{36,32}... | collective-permute-start | bytes 1572872 | tf_op jit(solution)/shard_map/ppermute | solution.py:18
  52.2 24.2 %copy-start.2 = (bf16[512,512]{1,0:T(8,128)(2,1)}, bf16[512,512]{1,0:T(8,128)(2,1)S(1)}, u32[]{:S(2)}) copy-start(bf16[512,512]{1,0:T(8,128)(2,1)S(1)} %collective-permute-done.6.block_ref.refs_7_) | copy-start | bytes 1572868
  52.2 24.2 %collective-permute-start.4 = (bf16[256,512]{1,0:T(8,128)(2,1)S(1)}, bf16[256,512]{1,0:T(8,128)(2,1)S(1)}, u32[]{:S(2)}, u32[]{:S(2)}) collective-permute-start(bf16[256,512]{1,0:T(8,128)(2,1)S(1)} %broadcast_select_fusion), channel_id=1, source_target_pairs={{0,4},{4,0},{8,12},{12,8},{16,20},{20,16},{24,28},{28,24},{32,36},... | collective-permute-start | bytes 786440 | tf_op jit(solution)/shard_map/ppermute | solution.py:18
  55.5 20.9 %copy-start.3 = (bf16[512,512]{1,0:T(8,128)(2,1)}, bf16[512,512]{1,0:T(8,128)(2,1)S(1)}, u32[]{:S(2)}) copy-start(bf16[512,512]{1,0:T(8,128)(2,1)S(1)} %collective-permute-done.7.block_ref.refs_8_) | copy-start | bytes 1572868
  55.6 20.9 %collective-permute-start.8 = (bf16[256,512]{1,0:T(8,128)(2,1)S(1)}, bf16[256,512]{1,0:T(8,128)(2,1)S(1)}, u32[]{:S(2)}, u32[]{:S(2)}) collective-permute-start(bf16[256,512]{1,0:T(8,128)(2,1)S(1)} %get-tuple-element.17), channel_id=1, source_target_pairs={{0,48},{4,52},{8,56},{12,60},{32,80},{36,84},{40,88},{44,92},{48,0... | collective-permute-start | bytes 786440 | tf_op jit(solution)/shard_map/ppermute | solution.py:18
  58.6 17.9 %copy-start.4 = (bf16[256,512]{1,0:T(8,128)(2,1)}, bf16[256,512]{1,0:T(8,128)(2,1)S(1)}, u32[]{:S(2)}) copy-start(bf16[256,512]{1,0:T(8,128)(2,1)S(1)} %shard_map.48.refs_10_) | copy-start | bytes 786436
  58.8 17.7 %copy-start.5 = (bf16[256,512]{1,0:T(8,128)(2,1)}, bf16[256,512]{1,0:T(8,128)(2,1)S(1)}, u32[]{:S(2)}) copy-start(bf16[256,512]{1,0:T(8,128)(2,1)S(1)} %shard_map.49.refs_11_) | copy-start | bytes 786436
  58.8 27.6 %copy-start.8 = (bf16[256,512]{1,0:T(8,128)(2,1)S(1)}, bf16[256,512]{1,0:T(8,128)(2,1)}, u32[]{:S(2)}) copy-start(bf16[256,512]{1,0:T(8,128)(2,1)} %q_ref.3) | copy-start | bytes 786436
  58.8 27.5 %collective-permute-start.10 = (bf16[256,512]{1,0:T(8,128)(2,1)S(1)}, bf16[256,512]{1,0:T(8,128)(2,1)S(1)}, u32[]{:S(2)}, u32[]{:S(2)}) collective-permute-start(bf16[256,512]{1,0:T(8,128)(2,1)S(1)} %shard_map.49.refs_11_), channel_id=1, source_target_pairs={{16,0},{20,4},{24,8},{28,12},{32,16},{36,20},{40,24},{44,28},{48,3... | collective-permute-start | bytes 786440 | tf_op jit(solution)/shard_map/ppermute | solution.py:18
  71.9 14.5 %collective-permute-start.9 = (bf16[256,512]{1,0:T(8,128)(2,1)S(1)}, bf16[256,512]{1,0:T(8,128)(2,1)S(1)}, u32[]{:S(2)}, u32[]{:S(2)}) collective-permute-start(bf16[256,512]{1,0:T(8,128)(2,1)S(1)} %shard_map.48.refs_10_), channel_id=1, source_target_pairs={{0,16},{4,20},{8,24},{12,28},{16,32},{20,36},{24,40},{28,44},{32,4... | collective-permute-start | bytes 786440 | tf_op jit(solution)/shard_map/ppermute | solution.py:18
  86.4 9.4 %copy-start = (bf16[512,2048]{1,0:T(8,128)(2,1)S(1)}, bf16[512,2048]{1,0:T(8,128)(2,1)}, u32[]{:S(2)}) copy-start(bf16[512,2048]{1,0:T(8,128)(2,1)} %wa_ref.3) | copy-start | bytes 6291460
  89.7 6.0 %collective-permute-start.11 = (bf16[256,512]{1,0:T(8,128)(2,1)S(1)}, bf16[256,512]{1,0:T(8,128)(2,1)S(1)}, u32[]{:S(2)}, u32[]{:S(2)}) collective-permute-start(bf16[256,512]{1,0:T(8,128)(2,1)S(1)} %shard_map.51.a_ref), channel_id=1, source_target_pairs={{0,1},{1,0},{2,3},{3,2},{4,5},{5,4},{6,7},{7,6},{8,9},{9,8},{10,11... | collective-permute-start | bytes 786440 | tf_op jit(solution)/shard_map/ppermute | solution.py:23
  97.3 23.2 %collective-permute-start.13 = (bf16[256,512]{1,0:T(8,128)(2,1)S(1)}, bf16[256,512]{1,0:T(8,128)(2,1)S(1)}, u32[]{:S(2)}, u32[]{:S(2)}) collective-permute-start(bf16[256,512]{1,0:T(8,128)(2,1)S(1)} %shard_map.53), channel_id=1, source_target_pairs={{0,2},{1,3},{2,0},{3,1},{4,6},{5,7},{6,4},{7,5},{8,10},{9,11},{10,... | collective-permute-start | bytes 786440 | tf_op jit(solution)/shard_map/ppermute | solution.py:23
  (2 other events, 1.4 us)

commit v3 on v2

v3 whole, which is shorter than its diff:
```python
import jax
import jax.numpy as jnp
from jax import lax
from jax.experimental import pallas as pl
from jax.experimental.pallas import tpu as pltpu
from jax.sharding import PartitionSpec as P


HEAD_DIM = 128
LOG2E = 1.4426950408889634
MIB = 1024 * 1024


def seq_permute(value, target_of):
    count = lax.axis_size("seq")
    pairs = [(i, target_of(i)) for i in range(count)]
    pairs = [(i, j) for i, j in pairs if 0 <= j < count]
    return lax.ppermute(value, "seq", pairs)


def head_permute(value, bit):
    count = lax.axis_size("head")
    return lax.ppermute(value, "head", [(i, i ^ bit) for i in range(count)])


def mean_matrix(rows, factor):
    row = lax.broadcasted_iota(jnp.int32, (rows, rows * factor), 0)
    col = lax.broadcasted_iota(jnp.int32, (rows, rows * factor), 1)
    return jnp.where(col // factor == row, 1.0 / factor, 0.0).astype(jnp.bfloat16)


def spread_mean_matrix(rows, factor):
    row = lax.broadcasted_iota(jnp.int32, (rows, rows), 0)
    col = lax.broadcasted_iota(jnp.int32, (rows, rows), 1)
    return jnp.where(col // factor == row // factor, 1.0 / factor, 0.0).astype(jnp.bfloat16)


def dot(left, right):
    return jnp.dot(left, right, preferred_element_type=jnp.float32)


def dot_t(left, right):
    return lax.dot_general(left, right, (((1,), (1,)), ((), ())), preferred_element_type=jnp.float32)


def coarse_kernel(k_ref, v_ref, raw_ref, one_ref, two_ref, three_ref):
    half, quarter, eighth = mean_matrix(128, 2), mean_matrix(64, 4), mean_matrix(32, 8)
    for index, ref in enumerate((k_ref, v_ref)):
        value = ref[...]
        raw_ref[index * 256 : (index + 1) * 256] = value
        one_ref[index * 128 : (index + 1) * 128] = dot(half, value).astype(jnp.bfloat16)
        two_ref[index * 64 : (index + 1) * 64] = dot(quarter, value).astype(jnp.bfloat16)
        three_ref[index * 32 : (index + 1) * 32] = dot(eighth, value).astype(jnp.bfloat16)


def coarse(k, v):
    width = k.shape[1]
    return pl.pallas_call(
        coarse_kernel,
        out_shape=(
            jax.ShapeDtypeStruct((512, width), jnp.bfloat16),
            jax.ShapeDtypeStruct((256, width), jnp.bfloat16),
            jax.ShapeDtypeStruct((128, width), jnp.bfloat16),
            jax.ShapeDtypeStruct((64, width), jnp.bfloat16),
        ),
        compiler_params=pltpu.CompilerParams(vmem_limit_bytes=8 * MIB),
        cost_estimate=pl.CostEstimate(flops=10**8, bytes_accessed=10**6, transcendentals=0),
        name="coarse",
    )(k, v)


def half_kernel(two_ref, one_ref, out_ref):
    half = mean_matrix(64, 2)
    for part in range(2):
        base = part * 128
        out_ref[base : base + 64] = two_ref[part * 64 : (part + 1) * 64]
        out_ref[base + 64 : base + 128] = dot(half, one_ref[base : base + 128]).astype(jnp.bfloat16)


def halve_kernel(block_ref, out_ref):
    half = mean_matrix(128, 2)
    for part in range(2):
        out_ref[part * 128 : (part + 1) * 128] = dot(
            half, block_ref[part * 256 : (part + 1) * 256]
        ).astype(jnp.bfloat16)


def pack_kernel(a_ref, b_ref, out_ref):
    for part in range(2):
        for index, ref in enumerate((a_ref, b_ref)):
            start = part * 256 + index * 128
            out_ref[start : start + 128] = ref[part * 128 : (part + 1) * 128]


def hand_kernel(outer, far_ref, across_ref, skew_ref, skew_across_ref, out_ref):
    out_ref[:256] = jnp.where(outer[0] > 0, far_ref[...], across_ref[...])
    out_ref[256:320] = skew_ref[...]
    out_ref[320:384] = skew_across_ref[...]


def hand(outer, far, across, skew, skew_across):
    whole = pl.BlockSpec(memory_space=pltpu.VMEM)
    return pl.pallas_call(
        hand_kernel,
        in_specs=[pl.BlockSpec(memory_space=pltpu.SMEM)] + [whole] * 4,
        out_specs=whole,
        out_shape=jax.ShapeDtypeStruct((384, far.shape[1]), far.dtype),
        compiler_params=pltpu.CompilerParams(vmem_limit_bytes=4 * MIB),
        cost_estimate=pl.CostEstimate(flops=10**8, bytes_accessed=10**6, transcendentals=0),
        name="hand",
    )(outer, far, across, skew, skew_across)


def small(kernel, *operands, rows=(256,)):
    width, dtype = operands[0].shape[1], operands[0].dtype
    shapes = tuple(jax.ShapeDtypeStruct((count, width), dtype) for count in rows)
    return pl.pallas_call(
        kernel,
        out_shape=shapes if len(rows) > 1 else shapes[0],
        compiler_params=pltpu.CompilerParams(vmem_limit_bytes=4 * MIB),
        cost_estimate=pl.CostEstimate(flops=10**8, bytes_accessed=10**6, transcendentals=0),
    )(*operands)


LATE = 2 * 128
KEYS = 768 + 3 * 512 - LATE
SCALE = LOG2E * HEAD_DIM**-0.5


def bias(flags, index):
    return jnp.where(flags[index] > 0, 0.0, -jnp.inf)


def main_kernel(flags, q_ref, *refs):
    k_ref, v_ref, left, right = refs[0:4]
    across, far, third = refs[4:7]
    twos = refs[7:9]
    skews = refs[9:11]
    nears = refs[11:13]
    sum_ref, weight_ref, top_ref = refs[13:16]
    scores, weights, values = refs[16:19]

    rows = q_ref.shape[0]
    even = flags[6] > 0
    beside_left = flags[2] > 0
    half = mean_matrix(128, 2)
    spreads = [spread_mean_matrix(rows, 2**level) for level in range(1, 4)]
    for slot in range(2):
        values[slot, :, HEAD_DIM:] = jnp.ones((KEYS, HEAD_DIM), jnp.bfloat16)

    for head in range(q_ref.shape[1] // HEAD_DIM):
        slot = head % 2
        lanes = slice(head * HEAD_DIM, (head + 1) * HEAD_DIM)

        def rows_of(ref, start, count):
            return ref[start : start + count, lanes]

        def either(flag, first, second, start, count):
            return jnp.where(flag, rows_of(first, start, count), rows_of(second, start, count))

        fourth = [
            dot(half, either(beside_left, left, right, part * 256, 256)).astype(jnp.bfloat16)
            for part in range(2)
        ]
        near = [either(even, nears[0], nears[1], part * 128, 128) for part in range(2)]
        skew = [
            jnp.concatenate(
                [
                    rows_of(skews[0], part * 32, 32),
                    rows_of(skews[1], part * 32, 32),
                    rows_of(third, 256 + part * 32, 32),
                    rows_of(third, 320 + part * 32, 32),
                ],
                0,
            )
            for part in range(2)
        ]
        pieces = [(rows_of(k_ref, 0, 256), rows_of(v_ref, 0, 256), 0, None)]
        for index, ref in enumerate((left, right)):
            pieces.append((rows_of(ref, 0, 256), rows_of(ref, 256, 256), 0, index))
        for ref, flag in ((across, None), (far, 10), (third, 11)):
            pieces.append((rows_of(ref, 0, 128), rows_of(ref, 128, 128), 1, flag))
        pieces.append((fourth[0], fourth[1], 1, 12))
        for index, ref in enumerate(twos):
            pieces.append((rows_of(ref, 0, 256), rows_of(ref, 256, 256), 2, 3 + index))
        pieces.append((skew[0], skew[1], 3, 8))
        pieces.append((near[0], near[1], 3, 9))

        query = rows_of(q_ref, 0, rows)
        queries = [query] + [dot(spread, query).astype(jnp.bfloat16) for spread in spreads]
        largest = None
        start = 0
        spans = []
        for keys, vals, level, flag in pieces:
            count = keys.shape[0]
            part = dot_t(queries[level], keys)
            if flag is not None:
                part = part + bias(flags, flag)
            scores[slot, :, start : start + count] = part
            values[slot, start : start + count, :HEAD_DIM] = vals
            for column in range(0, count, 128):
                piece = part[:, column : column + 128]
                largest = piece if largest is None else jnp.maximum(largest, piece)
            spans.append((start, count, level))
            start += count
        top = jnp.max(largest, axis=1, keepdims=True) * SCALE
        for start, count, level in spans:
            shifted = scores[slot, :, start : start + count] * SCALE - (top - level)
            weights[slot, :, start : start + count] = jnp.exp2(shifted).astype(jnp.bfloat16)
        total = dot(weights[slot], values[slot])
        sum_ref[:, lanes] = total[:, :HEAD_DIM]
        weight_ref[:, lanes] = total[:, HEAD_DIM:]
        top_ref[:, lanes] = jnp.broadcast_to(top, (rows, HEAD_DIM))


def late_kernel(flags, q_ref, sum_ref, weight_ref, top_ref, low, high, out_ref, values):
    rows = q_ref.shape[0]
    spread = spread_mean_matrix(rows, 8)
    for slot in range(2):
        values[slot, :, HEAD_DIM:] = jnp.ones((LATE, HEAD_DIM), jnp.bfloat16)
    for head in range(q_ref.shape[1] // HEAD_DIM):
        slot = head % 2
        lanes = slice(head * HEAD_DIM, (head + 1) * HEAD_DIM)
        query = dot(spread, q_ref[:, lanes]).astype(jnp.bfloat16)
        parts = []
        for index, (ref, flag) in enumerate(((low, 5), (high, 7))):
            parts.append(dot_t(query, ref[:128, lanes]) + bias(flags, flag))
            values[slot, index * 128 : (index + 1) * 128, :HEAD_DIM] = ref[128:, lanes]
        early = top_ref[:, lanes]
        top = jnp.max(jnp.maximum(parts[0], parts[1]), axis=1, keepdims=True) * SCALE
        top = jnp.maximum(early, top)
        kept = jnp.exp2(early - top)
        part = jnp.concatenate([jnp.exp2(p * SCALE - (top - 3.0)) for p in parts], 1)
        total = dot(part.astype(jnp.bfloat16), values[slot])
        numerator = sum_ref[:, lanes] * kept + total[:, :HEAD_DIM]
        denominator = weight_ref[:, lanes] * kept + total[:, HEAD_DIM:]
        out_ref[:, lanes] = (numerator / denominator).astype(jnp.bfloat16)


def heads_call(kernel, flags, tensors, outs, scratch, limit, flops):
    whole = pl.BlockSpec(memory_space=pltpu.VMEM)
    several = len(outs) > 1
    return pl.pallas_call(
        kernel,
        in_specs=[pl.BlockSpec(memory_space=pltpu.SMEM)] + [whole] * len(tensors),
        out_specs=(whole,) * len(outs) if several else whole,
        out_shape=tuple(outs) if several else outs[0],
        scratch_shapes=scratch,
        compiler_params=pltpu.CompilerParams(vmem_limit_bytes=limit * MIB),
        cost_estimate=pl.CostEstimate(flops=flops, bytes_accessed=6 * 10**6, transcendentals=0),
    )(flags, *tensors)


def attend_main(flags, tensors):
    rows, width = tensors[0].shape
    outs = [jax.ShapeDtypeStruct((rows, width), jnp.float32)] * 3
    scratch = [
        pltpu.VMEM((2, rows, KEYS), jnp.float32),
        pltpu.VMEM((2, rows, KEYS), jnp.bfloat16),
        pltpu.VMEM((2, KEYS, 2 * HEAD_DIM), jnp.bfloat16),
    ]
    return heads_call(main_kernel, flags, tensors, outs, scratch, 32, 3 * 10**9)


def attend_late(flags, tensors):
    rows, width = tensors[0].shape
    outs = [jax.ShapeDtypeStruct((rows, width), jnp.bfloat16)]
    scratch = [pltpu.VMEM((2, LATE, 2 * HEAD_DIM), jnp.bfloat16)]
    return heads_call(late_kernel, flags, tensors, outs, scratch, 16, 3 * 10**8)


def project_kernel(column, a_ref, b_ref, wa_ref, wb_ref, out_ref):
    total = dot(a_ref[...], wa_ref[...]) + dot(b_ref[...], wb_ref[...])
    out_ref[...] = total.astype(out_ref.dtype)


def project(column, own, peer, own_weight, peer_weight, dtype):
    rows, width = own.shape
    block = pl.BlockSpec((rows, width), lambda i, c: (0, 0))
    weight = pl.BlockSpec((width, width), lambda i, c: (0, c[0]))
    return pl.pallas_call(
        project_kernel,
        grid_spec=pltpu.PrefetchScalarGridSpec(
            num_scalar_prefetch=1,
            grid=(1,),
            in_specs=[block, block, weight, weight],
            out_specs=block,
        ),
        out_shape=jax.ShapeDtypeStruct((rows, width), dtype),
        compiler_params=pltpu.CompilerParams(vmem_limit_bytes=12 * MIB),
        cost_estimate=pl.CostEstimate(flops=10**9, bytes_accessed=10**6, transcendentals=0),
    )(column, own, peer, own_weight, peer_weight)


def layer(queries, key_rows, value_rows, out_weight):
    device = lax.axis_index("seq")
    head = lax.axis_index("head")
    last = lax.axis_size("seq") - 1
    lines = lax.axis_size("seq") // 4
    line = device // 4
    spot = device % 4
    even = line % 2 == 0

    raw, own_one, own_two, own_three = coarse(key_rows, value_rows)
    across = seq_permute(own_one, lambda i: i ^ 2)
    skew = seq_permute(own_three, lambda i: i + 12 if i // 4 % 2 == 0 else i - 12)
    peer_weight = head_permute(out_weight, 1)
    two_half = small(half_kernel, own_two, across)
    two_beside = seq_permute(two_half, lambda i: i ^ 1)
    skew_across = seq_permute(skew, lambda i: i ^ 2)
    far = seq_permute(across, lambda i: i + 4 if i % 4 < 2 else i - 4)
    left = seq_permute(raw, lambda i: i + 1)
    right = seq_permute(raw, lambda i: i - 1)
    two_block = small(pack_kernel, two_half, two_beside, rows=(512,))
    two_low = seq_permute(two_block, lambda i: i + 4)
    two_high = seq_permute(two_block, lambda i: i - 4)
    outer = (spot == 0) | (spot == 3)
    handed = hand(outer.astype(jnp.int32).reshape(1), far, across, skew, skew_across)
    third = seq_permute(handed, lambda i: i ^ 1)
    near_low = small(halve_kernel, two_low)
    near_high = small(halve_kernel, two_high)
    three_low = seq_permute(near_low, lambda i: i + 4)
    three_high = seq_permute(near_high, lambda i: i - 4)

    far_ok = jnp.where(spot < 2, line > 0, line < lines - 1)
    flags = jnp.stack(
        [
            device > 0,
            device < last,
            spot % 2 == 0,
            line > 0,
            line < lines - 1,
            line >= 2,
            even,
            line < lines - 2,
            jnp.where(even, line < lines - 3, line >= 3),
            jnp.where(even, line > 0, line < lines - 1),
            far_ok,
            outer | far_ok,
            jnp.logical_not(outer) | far_ok,
        ]
    ).astype(jnp.int32)
    tensors = [queries, key_rows, value_rows, left, right, across, far, third]
    tensors += [two_low, two_high, skew, skew_across, near_low, near_high]
    partial = attend_main(flags, tensors)
    attended = attend_late(flags, [queries, *partial, three_low, three_high])
    peer = head_permute(attended, 1)
    here_column, away_column = head.reshape(1), (head ^ 2).reshape(1)
    weights = (out_weight, peer_weight)
    away = project(away_column, attended, peer, *weights, jnp.bfloat16)
    arrived = head_permute(away, 2)
    here = project(here_column, attended, peer, *weights, jnp.float32)
    return (here + arrived.astype(jnp.float32)).astype(jnp.bfloat16)


def solution(mesh):
    in_specs = (P("seq", "head"), P("seq", "head"), P("seq", "head"), P("head", None))
    out_specs = P("seq", "head")
    return jax.shard_map(layer, mesh=mesh, in_specs=in_specs, out_specs=out_specs, check_vma=False)
```

time: 122 us -> 140 us (1.15)
  the two profiles are of different devices: /device:TPU:15 before, /device:TPU:55 now
where the time goes in v3:
time: 140 us
  starting transfers between devices  66.8 us (48%)
  waiting for transfers between devices  56.7 us (40%)
  Pallas kernels  13 us (9%)
  local copies, waits for them, and re-layouts  2.02 us (1%)
    ppermute x12, starting transfers between devices, seq_permute(): return lax.ppermute(value, 'seq', pairs)  55.8 us
    ppermute x12, waiting for transfers between devices, seq_permute(): return lax.ppermute(value, 'seq', pairs)  39.9 us
    ppermute x3, waiting for transfers between devices, head_permute(): return lax.ppermute(value, 'head', [(i, i ^ bit) for i in range(count)])  16.8 us
    ppermute x3, starting transfers between devices, head_permute(): return lax.ppermute(value, 'head', [(i, i ^ bit) for i in range(count)])  11 us
    pallas_call x2, Pallas kernels, heads_call(): pl.pallas_call(kernel, in_specs=[pl.BlockSpec(memory_space=pltpu.SMEM)] +...  8.41 us
    pallas_call x2, Pallas kernels, project(): pl.pallas_call(project_kernel, grid_spec=pltpu.PrefetchScalarGridSpec(num...  3.02 us
  transfers between devices with their start and end apart: 15, of which 7 were waited for; matrix products, arithmetic and copies ran while one was open for 0% of the time, Pallas kernels for 8%

profile of v3, /device:TPU:55, one launch (start us, length us, event | category | flops | bytes accessed | tf_op | source)
XLA Modules:
  0.0 139.7 jit_solution(1244561527142048876)
XLA Ops:
  0.0 2.6 %collective-permute-start.13 = (bf16[512,2048]{1,0:T(8,128)(2,1)}, bf16[512,2048]{1,0:T(8,128)(2,1)}, u32[]{:S(2)}, u32[]{:S(2)}) collective-permute-start(bf16[512,2048]{1,0:T(8,128)(2,1)} %wa_ref.3), channel_id=1, source_target_pairs={{0,1},{1,0},{2,3},{3,2},{4,5},{5,4},{6,7},{7,6},{8,9},{9,8},{10,11... | collective-permute-start | bytes 6291464 | tf_op jit(solution)/shard_map/ppermute | solution.py:23
  5.4 3.8 %collective-permute-start.2 = (bf16[256,512]{1,0:T(8,128)(2,1)S(1)}, bf16[256,512]{1,0:T(8,128)(2,1)S(1)}, u32[]{:S(2)}, u32[]{:S(2)}) collective-permute-start(bf16[256,512]{1,0:T(8,128)(2,1)S(1)} %get-tuple-element.13), channel_id=1, source_target_pairs={{0,8},{4,12},{8,0},{12,4},{16,24},{20,28},{24,16},{28,20},{32,40},... | collective-permute-start | bytes 786440 | tf_op jit(solution)/shard_map/ppermute | solution.py:18
  9.1 11.5 %collective-permute-done.2.across_ref.one_ref.refs_4_ = bf16[256,512]{1,0:T(8,128)(2,1)S(1)} collective-permute-done((bf16[256,512]{1,0:T(8,128)(2,1)S(1)}, bf16[256,512]{1,0:T(8,128)(2,1)S(1)}, u32[]{:S(2)}, u32[]{:S(2)}) %collective-permute-start.2) | collective-permute-done | bytes 262176 | tf_op jit(solution)/shard_map/ppermute | solution.py:18
  20.8 3.4 %collective-permute-start.7 = (bf16[256,512]{1,0:T(8,128)(2,1)S(1)}, bf16[256,512]{1,0:T(8,128)(2,1)S(1)}, u32[]{:S(2)}, u32[]{:S(2)}) collective-permute-start(bf16[256,512]{1,0:T(8,128)(2,1)S(1)} %shard_map.46.a_ref), channel_id=1, source_target_pairs={{0,4},{4,0},{8,12},{12,8},{16,20},{20,16},{24,28},{28,24},{32,36},... | collective-permute-start | bytes 786440 | tf_op jit(solution)/shard_map/ppermute | solution.py:18
  24.2 5.9 %collective-permute-done.7.b_ref = bf16[256,512]{1,0:T(8,128)(2,1)S(1)} collective-permute-done((bf16[256,512]{1,0:T(8,128)(2,1)S(1)}, bf16[256,512]{1,0:T(8,128)(2,1)S(1)}, u32[]{:S(2)}, u32[]{:S(2)}) %collective-permute-start.7) | collective-permute-done | bytes 262176 | tf_op jit(solution)/shard_map/ppermute | solution.py:18
  30.1 4.0 %collective-permute-start.8 = (bf16[512,512]{1,0:T(8,128)(2,1)S(1)}, bf16[512,512]{1,0:T(8,128)(2,1)S(1)}, u32[]{:S(2)}, u32[]{:S(2)}) collective-permute-start(bf16[512,512]{1,0:T(8,128)(2,1)S(1)} %shard_map.47), channel_id=1, source_target_pairs={{0,16},{4,20},{8,24},{12,28},{16,32},{20,36},{24,40},{28,44},{32,4... | collective-permute-start | bytes 1572872 | tf_op jit(solution)/shard_map/ppermute | solution.py:18
  34.1 8.9 %collective-permute-start.3 = (bf16[256,512]{1,0:T(8,128)(2,1)S(1)}, bf16[256,512]{1,0:T(8,128)(2,1)S(1)}, u32[]{:S(2)}, u32[]{:S(2)}) collective-permute-start(bf16[256,512]{1,0:T(8,128)(2,1)S(1)} %collective-permute-done.2.across_ref.one_ref.refs_4_), channel_id=1, source_target_pairs={{0,16},{4,20},{16,32},{20,36},{24,8},{28,12},{32,48},{36,52},{40,2... | collective-permute-start | bytes 786440 | tf_op jit(solution)/shard_map/ppermute | solution.py:18
  43.0 1.9 %collective-permute-start.4 = (bf16[64,512]{1,0:T(8,128)(2,1)S(1)}, bf16[64,512]{1,0:T(8,128)(2,1)S(1)}, u32[]{:S(2)}, u32[]{:S(2)}) collective-permute-start(bf16[64,512]{1,0:T(8,128)(2,1)S(1)} %get-tuple-element.14), channel_id=1, source_target_pairs={{0,48},{4,52},{8,56},{12,60},{32,80},{36,84},{40,88},{44,92},{48,0... | collective-permute-start | bytes 196616 | tf_op jit(solution)/shard_map/ppermute | solution.py:18
  44.9 6.3 %collective-permute-done.4.skew_ref.refs_9_ = bf16[64,512]{1,0:T(8,128)(2,1)S(1)} collective-permute-done((bf16[64,512]{1,0:T(8,128)(2,1)S(1)}, bf16[64,512]{1,0:T(8,128)(2,1)S(1)}, u32[]{:S(2)}, u32[]{:S(2)}) %collective-permute-start.4) | collective-permute-done | bytes 65568 | tf_op jit(solution)/shard_map/ppermute | solution.py:18
  51.2 4.7 %collective-permute-start.5 = (bf16[64,512]{1,0:T(8,128)(2,1)S(1)}, bf16[64,512]{1,0:T(8,128)(2,1)S(1)}, u32[]{:S(2)}, u32[]{:S(2)}) collective-permute-start(bf16[64,512]{1,0:T(8,128)(2,1)S(1)} %collective-permute-done.4.skew_ref.refs_9_), channel_id=1, source_target_pairs={{0,8},{4,12},{8,0},{12,4},{16,24},{20,28},{24,16},{28,20},{32,40},... | collective-permute-start | bytes 196616 | tf_op jit(solution)/shard_map/ppermute | solution.py:18
  56.0 11.4 %collective-permute-start.9 = (bf16[512,512]{1,0:T(8,128)(2,1)S(1)}, bf16[512,512]{1,0:T(8,128)(2,1)S(1)}, u32[]{:S(2)}, u32[]{:S(2)}) collective-permute-start(bf16[512,512]{1,0:T(8,128)(2,1)S(1)} %shard_map.47), channel_id=1, source_target_pairs={{16,0},{20,4},{24,8},{28,12},{32,16},{36,20},{40,24},{44,28},{48,3... | collective-permute-start | bytes 1572872 | tf_op jit(solution)/shard_map/ppermute | solution.py:18
  67.4 2.5 %collective-permute-start = (bf16[512,512]{1,0:T(8,128)(2,1)}, bf16[512,512]{1,0:T(8,128)(2,1)}, u32[]{:S(2)}, u32[]{:S(2)}) collective-permute-start(bf16[512,512]{1,0:T(8,128)(2,1)} %get-tuple-element.12), channel_id=1, source_target_pairs={{0,4},{4,8},{8,12},{12,16},{16,20},{20,24},{24,28},{28,32},{32,36}... | collective-permute-start | bytes 1572872 | tf_op jit(solution)/shard_map/ppermute | solution.py:18
  69.9 2.8 %collective-permute-start.1 = (bf16[512,512]{1,0:T(8,128)(2,1)}, bf16[512,512]{1,0:T(8,128)(2,1)}, u32[]{:S(2)}, u32[]{:S(2)}) collective-permute-start(bf16[512,512]{1,0:T(8,128)(2,1)} %get-tuple-element.12), channel_id=1, source_target_pairs={{4,0},{8,4},{12,8},{16,12},{20,16},{24,20},{28,24},{32,28},{36,32}... | collective-permute-start | bytes 1572872 | tf_op jit(solution)/shard_map/ppermute | solution.py:18
  72.8 5.1 %collective-permute-start.6 = (bf16[384,512]{1,0:T(8,128)(2,1)S(1)}, bf16[384,512]{1,0:T(8,128)(2,1)}, u32[]{:S(2)}, u32[]{:S(2)}) collective-permute-start(bf16[384,512]{1,0:T(8,128)(2,1)S(1)} %hand.1), channel_id=1, source_target_pairs={{0,4},{4,0},{8,12},{12,8},{16,20},{20,16},{24,28},{28,24},{32,36},... | collective-permute-start | bytes 1179656 | tf_op jit(solution)/shard_map/ppermute | solution.py:18
  78.3 2.6 %collective-permute-start.10 = (bf16[256,512]{1,0:T(8,128)(2,1)S(1)}, bf16[256,512]{1,0:T(8,128)(2,1)S(1)}, u32[]{:S(2)}, u32[]{:S(2)}) collective-permute-start(bf16[256,512]{1,0:T(8,128)(2,1)S(1)} %shard_map.48.refs_11_), channel_id=1, source_target_pairs={{0,16},{4,20},{8,24},{12,28},{16,32},{20,36},{24,40},{28,44},{32,4... | collective-permute-start | bytes 786440 | tf_op jit(solution)/shard_map/ppermute | solution.py:18
  81.1 4.8 %collective-permute-start.11 = (bf16[256,512]{1,0:T(8,128)(2,1)S(1)}, bf16[256,512]{1,0:T(8,128)(2,1)S(1)}, u32[]{:S(2)}, u32[]{:S(2)}) collective-permute-start(bf16[256,512]{1,0:T(8,128)(2,1)S(1)} %shard_map.49.refs_12_), channel_id=1, source_target_pairs={{16,0},{20,4},{24,8},{28,12},{32,16},{36,20},{40,24},{44,28},{48,3... | collective-permute-start | bytes 786440 | tf_op jit(solution)/shard_map/ppermute | solution.py:18
  85.9 9.0 %collective-permute-done.1.refs_3_ = bf16[512,512]{1,0:T(8,128)(2,1)} collective-permute-done((bf16[512,512]{1,0:T(8,128)(2,1)}, bf16[512,512]{1,0:T(8,128)(2,1)}, u32[]{:S(2)}, u32[]{:S(2)}) %collective-permute-start.1) | collective-permute-done | bytes 524320 | tf_op jit(solution)/shard_map/ppermute | solution.py:18
  94.9 7.3 %collective-permute-done.6.refs_6_ = bf16[384,512]{1,0:T(8,128)(2,1)} collective-permute-done((bf16[384,512]{1,0:T(8,128)(2,1)S(1)}, bf16[384,512]{1,0:T(8,128)(2,1)}, u32[]{:S(2)}, u32[]{:S(2)}) %collective-permute-start.6) | collective-permute-done | bytes 393248 | tf_op jit(solution)/shard_map/ppermute | solution.py:18
  102.2 6.4 %shard_map.50 = (f32[256,512]{1,0:T(8,128)S(1)}, f32[256,512]{1,0:T(8,128)S(1)}, f32[256,512]{1,0:T(8,128)S(1)}) custom-call(s32[13]{0:T(128)S(1)} %convert_element_type.10.flags, bf16[256,512]{1,0:T(8,128)(2,1)S(1)} %copy-done.5, bf16[256,512]{1,0:T(8,128)(2,1)S(1)} %copy-done.2, bf16[256,512]{1,0:T(8,128)(2,1)S(1)} %copy-done.4, ...), custom_call_target="tpu_custom_call" | custom-call | flops 3000000000 | bytes 6000000 | tf_op jit(solution)/shard_map/pallas_call | solution.py:243
  108.7 2.0 %shard_map.51.a_ref = bf16[256,512]{1,0:T(8,128)(2,1)S(1)} custom-call(s32[13]{0:T(128)S(1)} %convert_element_type.10.flags, bf16[256,512]{1,0:T(8,128)(2,1)S(1)} %copy-done.5, f32[256,512]{1,0:T(8,128)S(1)} %get-tuple-element.16.sum_ref, f32[256,512]{1,0:T(8,128)S(1)} %get-tuple-element.17.weight_ref, f32[256,512]{1,0:T(8,128)S(1)} %get-tuple-element.18.top_ref, ...), custom_call_target="tpu_custom_call" | custom-call | flops 300000000 | bytes 6000000 | tf_op jit(solution)/shard_map/pallas_call | solution.py:243
  110.7 6.5 %collective-permute-start.12 = (bf16[256,512]{1,0:T(8,128)(2,1)S(1)}, bf16[256,512]{1,0:T(8,128)(2,1)S(1)}, u32[]{:S(2)}, u32[]{:S(2)}) collective-permute-start(bf16[256,512]{1,0:T(8,128)(2,1)S(1)} %shard_map.51.a_ref), channel_id=1, source_target_pairs={{0,1},{1,0},{2,3},{3,2},{4,5},{5,4},{6,7},{7,6},{8,9},{9,8},{10,11... | collective-permute-start | bytes 786440 | tf_op jit(solution)/shard_map/ppermute | solution.py:23
  119.8 1.9 %collective-permute-start.14 = (bf16[256,512]{1,0:T(8,128)(2,1)S(1)}, bf16[256,512]{1,0:T(8,128)(2,1)S(1)}, u32[]{:S(2)}, u32[]{:S(2)}) collective-permute-start(bf16[256,512]{1,0:T(8,128)(2,1)S(1)} %shard_map.53), channel_id=1, source_target_pairs={{0,2},{1,3},{2,0},{3,1},{4,6},{5,7},{6,4},{7,5},{8,10},{9,11},{10,... | collective-permute-start | bytes 786440 | tf_op jit(solution)/shard_map/ppermute | solution.py:23
  121.8 1.5 %shard_map.52 = f32[256,512]{1,0:T(8,128)S(1)} custom-call(s32[1]{0:T(128)} %bitcast.column, bf16[256,512]{1,0:T(8,128)(2,1)S(1)} %shard_map.51.a_ref, bf16[256,512]{1,0:T(8,128)(2,1)S(1)} %collective-permute-done.12.b_ref, bf16[512,2048]{1,0:T(8,128)(2,1)S(1)} %copy-done, bf16[512,2048]{1,0:T(8,128)(2,1)} %collective-permute-done.13.wb_ref), custom_call_target="tpu_custom_call" | custom-call | flops 1000000000 | bytes 1000000 | tf_op jit(solution)/shard_map/pallas_call | solution.py:281
  123.3 15.6 %collective-permute-done.14 = bf16[256,512]{1,0:T(8,128)(2,1)S(1)} collective-permute-done((bf16[256,512]{1,0:T(8,128)(2,1)S(1)}, bf16[256,512]{1,0:T(8,128)(2,1)S(1)}, u32[]{:S(2)}, u32[]{:S(2)}) %collective-permute-start.14) | collective-permute-done | bytes 262176 | tf_op jit(solution)/shard_map/ppermute | solution.py:23
  (31 shorter events, 7.0 us)
Async XLA Ops:
  0.0 118.3 %collective-permute-start.13 = (bf16[512,2048]{1,0:T(8,128)(2,1)}, bf16[512,2048]{1,0:T(8,128)(2,1)}, u32[]{:S(2)}, u32[]{:S(2)}) collective-permute-start(bf16[512,2048]{1,0:T(8,128)(2,1)} %wa_ref.3), channel_id=1, source_target_pairs={{0,1},{1,0},{2,3},{3,2},{4,5},{5,4},{6,7},{7,6},{8,9},{9,8},{10,11... | collective-permute-start | bytes 6291464 | tf_op jit(solution)/shard_map/ppermute | solution.py:23
  2.6 1.0 copy-start.1
  3.5 0.9 copy-start.3
  5.4 15.3 %collective-permute-start.2 = (bf16[256,512]{1,0:T(8,128)(2,1)S(1)}, bf16[256,512]{1,0:T(8,128)(2,1)S(1)}, u32[]{:S(2)}, u32[]{:S(2)}) collective-permute-start(bf16[256,512]{1,0:T(8,128)(2,1)S(1)} %get-tuple-element.13), channel_id=1, source_target_pairs={{0,8},{4,12},{8,0},{12,4},{16,24},{20,28},{24,16},{28,20},{32,40},... | collective-permute-start | bytes 786440 | tf_op jit(solution)/shard_map/ppermute | solution.py:18
  20.6 81.6 %copy-start.2 = (bf16[256,512]{1,0:T(8,128)(2,1)S(1)}, bf16[256,512]{1,0:T(8,128)(2,1)}, u32[]{:S(2)}) copy-start(bf16[256,512]{1,0:T(8,128)(2,1)} %refs_0_.1) | copy-start | bytes 786436
  20.6 81.6 %copy-start.4 = (bf16[256,512]{1,0:T(8,128)(2,1)S(1)}, bf16[256,512]{1,0:T(8,128)(2,1)}, u32[]{:S(2)}) copy-start(bf16[256,512]{1,0:T(8,128)(2,1)} %refs_1_.1) | copy-start | bytes 786436
  20.6 81.6 %copy-start.5 = (bf16[256,512]{1,0:T(8,128)(2,1)S(1)}, bf16[256,512]{1,0:T(8,128)(2,1)}, u32[]{:S(2)}) copy-start(bf16[256,512]{1,0:T(8,128)(2,1)} %q_ref.3) | copy-start | bytes 786436
  20.8 9.3 %collective-permute-start.7 = (bf16[256,512]{1,0:T(8,128)(2,1)S(1)}, bf16[256,512]{1,0:T(8,128)(2,1)S(1)}, u32[]{:S(2)}, u32[]{:S(2)}) collective-permute-start(bf16[256,512]{1,0:T(8,128)(2,1)S(1)} %shard_map.46.a_ref), channel_id=1, source_target_pairs={{0,4},{4,0},{8,12},{12,8},{16,20},{20,16},{24,28},{28,24},{32,36},... | collective-permute-start | bytes 786440 | tf_op jit(solution)/shard_map/ppermute | solution.py:18
  30.1 42.6 %collective-permute-start.8 = (bf16[512,512]{1,0:T(8,128)(2,1)S(1)}, bf16[512,512]{1,0:T(8,128)(2,1)S(1)}, u32[]{:S(2)}, u32[]{:S(2)}) collective-permute-start(bf16[512,512]{1,0:T(8,128)(2,1)S(1)} %shard_map.47), channel_id=1, source_target_pairs={{0,16},{4,20},{8,24},{12,28},{16,32},{20,36},{24,40},{28,44},{32,4... | collective-permute-start | bytes 1572872 | tf_op jit(solution)/shard_map/ppermute | solution.py:18
  34.1 35.7 %collective-permute-start.3 = (bf16[256,512]{1,0:T(8,128)(2,1)S(1)}, bf16[256,512]{1,0:T(8,128)(2,1)S(1)}, u32[]{:S(2)}, u32[]{:S(2)}) collective-permute-start(bf16[256,512]{1,0:T(8,128)(2,1)S(1)} %collective-permute-done.2.across_ref.one_ref.refs_4_), channel_id=1, source_target_pairs={{0,16},{4,20},{16,32},{20,36},{24,8},{28,12},{32,48},{36,52},{40,2... | collective-permute-start | bytes 786440 | tf_op jit(solution)/shard_map/ppermute | solution.py:18
  43.0 8.2 %collective-permute-start.4 = (bf16[64,512]{1,0:T(8,128)(2,1)S(1)}, bf16[64,512]{1,0:T(8,128)(2,1)S(1)}, u32[]{:S(2)}, u32[]{:S(2)}) collective-permute-start(bf16[64,512]{1,0:T(8,128)(2,1)S(1)} %get-tuple-element.14), channel_id=1, source_target_pairs={{0,48},{4,52},{8,56},{12,60},{32,80},{36,84},{40,88},{44,92},{48,0... | collective-permute-start | bytes 196616 | tf_op jit(solution)/shard_map/ppermute | solution.py:18
  51.2 16.1 %collective-permute-start.5 = (bf16[64,512]{1,0:T(8,128)(2,1)S(1)}, bf16[64,512]{1,0:T(8,128)(2,1)S(1)}, u32[]{:S(2)}, u32[]{:S(2)}) collective-permute-start(bf16[64,512]{1,0:T(8,128)(2,1)S(1)} %collective-permute-done.4.skew_ref.refs_9_), channel_id=1, source_target_pairs={{0,8},{4,12},{8,0},{12,4},{16,24},{20,28},{24,16},{28,20},{32,40},... | collective-permute-start | bytes 196616 | tf_op jit(solution)/shard_map/ppermute | solution.py:18
  56.0 22.3 %collective-permute-start.9 = (bf16[512,512]{1,0:T(8,128)(2,1)S(1)}, bf16[512,512]{1,0:T(8,128)(2,1)S(1)}, u32[]{:S(2)}, u32[]{:S(2)}) collective-permute-start(bf16[512,512]{1,0:T(8,128)(2,1)S(1)} %shard_map.47), channel_id=1, source_target_pairs={{16,0},{20,4},{24,8},{28,12},{32,16},{36,20},{40,24},{44,28},{48,3... | collective-permute-start | bytes 1572872 | tf_op jit(solution)/shard_map/ppermute | solution.py:18
  67.4 13.7 %collective-permute-start = (bf16[512,512]{1,0:T(8,128)(2,1)}, bf16[512,512]{1,0:T(8,128)(2,1)}, u32[]{:S(2)}, u32[]{:S(2)}) collective-permute-start(bf16[512,512]{1,0:T(8,128)(2,1)} %get-tuple-element.12), channel_id=1, source_target_pairs={{0,4},{4,8},{8,12},{12,16},{16,20},{20,24},{24,28},{28,32},{32,36}... | collective-permute-start | bytes 1572872 | tf_op jit(solution)/shard_map/ppermute | solution.py:18
  69.9 25.0 %collective-permute-start.1 = (bf16[512,512]{1,0:T(8,128)(2,1)}, bf16[512,512]{1,0:T(8,128)(2,1)}, u32[]{:S(2)}, u32[]{:S(2)}) collective-permute-start(bf16[512,512]{1,0:T(8,128)(2,1)} %get-tuple-element.12), channel_id=1, source_target_pairs={{4,0},{8,4},{12,8},{16,12},{20,16},{24,20},{28,24},{32,28},{36,32}... | collective-permute-start | bytes 1572872 | tf_op jit(solution)/shard_map/ppermute | solution.py:18
  72.8 29.4 %collective-permute-start.6 = (bf16[384,512]{1,0:T(8,128)(2,1)S(1)}, bf16[384,512]{1,0:T(8,128)(2,1)}, u32[]{:S(2)}, u32[]{:S(2)}) collective-permute-start(bf16[384,512]{1,0:T(8,128)(2,1)S(1)} %hand.1), channel_id=1, source_target_pairs={{0,4},{4,0},{8,12},{12,8},{16,20},{20,16},{24,28},{28,24},{32,36},... | collective-permute-start | bytes 1179656 | tf_op jit(solution)/shard_map/ppermute | solution.py:18
  78.3 30.3 %collective-permute-start.10 = (bf16[256,512]{1,0:T(8,128)(2,1)S(1)}, bf16[256,512]{1,0:T(8,128)(2,1)S(1)}, u32[]{:S(2)}, u32[]{:S(2)}) collective-permute-start(bf16[256,512]{1,0:T(8,128)(2,1)S(1)} %shard_map.48.refs_11_), channel_id=1, source_target_pairs={{0,16},{4,20},{8,24},{12,28},{16,32},{20,36},{24,40},{28,44},{32,4... | collective-permute-start | bytes 786440 | tf_op jit(solution)/shard_map/ppermute | solution.py:18
  81.1 27.5 %collective-permute-start.11 = (bf16[256,512]{1,0:T(8,128)(2,1)S(1)}, bf16[256,512]{1,0:T(8,128)(2,1)S(1)}, u32[]{:S(2)}, u32[]{:S(2)}) collective-permute-start(bf16[256,512]{1,0:T(8,128)(2,1)S(1)} %shard_map.49.refs_12_), channel_id=1, source_target_pairs={{16,0},{20,4},{24,8},{28,12},{32,16},{36,20},{40,24},{44,28},{48,3... | collective-permute-start | bytes 786440 | tf_op jit(solution)/shard_map/ppermute | solution.py:18
  108.6 9.7 %copy-start = (bf16[512,2048]{1,0:T(8,128)(2,1)S(1)}, bf16[512,2048]{1,0:T(8,128)(2,1)}, u32[]{:S(2)}) copy-start(bf16[512,2048]{1,0:T(8,128)(2,1)} %wa_ref.3) | copy-start | bytes 6291460
  110.7 7.6 %collective-permute-start.12 = (bf16[256,512]{1,0:T(8,128)(2,1)S(1)}, bf16[256,512]{1,0:T(8,128)(2,1)S(1)}, u32[]{:S(2)}, u32[]{:S(2)}) collective-permute-start(bf16[256,512]{1,0:T(8,128)(2,1)S(1)} %shard_map.51.a_ref), channel_id=1, source_target_pairs={{0,1},{1,0},{2,3},{3,2},{4,5},{5,4},{6,7},{7,6},{8,9},{9,8},{10,11... | collective-permute-start | bytes 786440 | tf_op jit(solution)/shard_map/ppermute | solution.py:23
  119.8 19.1 %collective-permute-start.14 = (bf16[256,512]{1,0:T(8,128)(2,1)S(1)}, bf16[256,512]{1,0:T(8,128)(2,1)S(1)}, u32[]{:S(2)}, u32[]{:S(2)}) collective-permute-start(bf16[256,512]{1,0:T(8,128)(2,1)S(1)} %shard_map.53), channel_id=1, source_target_pairs={{0,2},{1,3},{2,0},{3,1},{4,6},{5,7},{6,4},{7,5},{8,10},{9,11},{10,... | collective-permute-start | bytes 786440 | tf_op jit(solution)/shard_map/ppermute | solution.py:23

commit v4 on v3

--- a/solution.py
+++ b/solution.py
@@ -9,6 +9,10 @@
 HEAD_DIM = 128
 LOG2E = 1.4426950408889634
 MIB = 1024 * 1024
+
+
+def in_hbm(values):
+    return [pltpu.with_memory_space_constraint(value, pltpu.HBM) for value in values]
 
 
 def seq_permute(value, target_of):
@@ -66,7 +70,7 @@
         compiler_params=pltpu.CompilerParams(vmem_limit_bytes=8 * MIB),
         cost_estimate=pl.CostEstimate(flops=10**8, bytes_accessed=10**6, transcendentals=0),
         name="coarse",
-    )(k, v)
+    )(*in_hbm((k, v)))
 
 
 def half_kernel(two_ref, one_ref, out_ref):
@@ -132,13 +136,21 @@
 
 
 def main_kernel(flags, q_ref, *refs):
-    k_ref, v_ref, left, right = refs[0:4]
-    across, far, third = refs[4:7]
+    k_ref, v_ref = refs[0:2]
+    across, far = refs[4:6]
     twos = refs[7:9]
     skews = refs[9:11]
     nears = refs[11:13]
     sum_ref, weight_ref, top_ref = refs[13:16]
-    scores, weights, values = refs[16:19]
+    scores, weights, values, left, right, third, arrived = refs[16:23]
+    copies = [
+        pltpu.make_async_copy(source, target, arrived.at[index])
+        for index, (source, target) in enumerate(
+            ((refs[2], left), (refs[3], right), (refs[6], third))
+        )
+    ]
+    for copy in copies:
+        copy.start()
 
     rows = q_ref.shape[0]
     even = flags[6] > 0
@@ -158,11 +170,36 @@
         def either(flag, first, second, start, count):
             return jnp.where(flag, rows_of(first, start, count), rows_of(second, start, count))
 
-        fourth = [
-            dot(half, either(beside_left, left, right, part * 256, 256)).astype(jnp.bfloat16)
-            for part in range(2)
-        ]
+        query = rows_of(q_ref, 0, rows)
+        queries = [query] + [dot(spread, query).astype(jnp.bfloat16) for spread in spreads]
+        largest = None
+        spans = []
+
+        def take(keys, vals, level, flag):
+            nonlocal largest
+            start = spans[-1][0] + spans[-1][1] if spans else 0
+            count = keys.shape[0]
+            part = dot_t(queries[level], keys)
+            if flag is not None:
+                part = part + bias(flags, flag)
+            scores[slot, :, start : start + count] = part
+            values[slot, start : start + count, :HEAD_DIM] = vals
+            for column in range(0, count, 128):
+                piece = part[:, column : column + 128]
+                largest = piece if largest is None else jnp.maximum(largest, piece)
+            spans.append((start, count, level))
+
+        take(rows_of(k_ref, 0, 256), rows_of(v_ref, 0, 256), 0, None)
+        for index, ref in enumerate(twos):
+            take(rows_of(ref, 0, 256), rows_of(ref, 256, 256), 2, 3 + index)
         near = [either(even, nears[0], nears[1], part * 128, 128) for part in range(2)]
+        take(near[0], near[1], 3, 9)
+        for ref, flag in ((across, None), (far, 10)):
+            take(rows_of(ref, 0, 128), rows_of(ref, 128, 128), 1, flag)
+        if head == 0:
+            for copy in copies:
+                copy.wait()
+        take(rows_of(third, 0, 128), rows_of(third, 128, 128), 1, 11)
         skew = [
             jnp.concatenate(
                 [
@@ -175,34 +212,14 @@
             )
             for part in range(2)
         ]
-        pieces = [(rows_of(k_ref, 0, 256), rows_of(v_ref, 0, 256), 0, None)]
+        take(skew[0], skew[1], 3, 8)
         for index, ref in enumerate((left, right)):
-            pieces.append((rows_of(ref, 0, 256), rows_of(ref, 256, 256), 0, index))
-        for ref, flag in ((across, None), (far, 10), (third, 11)):
-            pieces.append((rows_of(ref, 0, 128), rows_of(ref, 128, 128), 1, flag))
-        pieces.append((fourth[0], fourth[1], 1, 12))
-        for index, ref in enumerate(twos):
-            pieces.append((rows_of(ref, 0, 256), rows_of(ref, 256, 256), 2, 3 + index))
-        pieces.append((skew[0], skew[1], 3, 8))
-        pieces.append((near[0], near[1], 3, 9))
-
-        query = rows_of(q_ref, 0, rows)
-        queries = [query] + [dot(spread, query).astype(jnp.bfloat16) for spread in spreads]
-        largest = None
-        start = 0
-        spans = []
-        for keys, vals, level, flag in pieces:
-            count = keys.shape[0]
-            part = dot_t(queries[level], keys)
-            if flag is not None:
-                part = part + bias(flags, flag)
-            scores[slot, :, start : start + count] = part
-            values[slot, start : start + count, :HEAD_DIM] = vals
-            for column in range(0, count, 128):
-                piece = part[:, column : column + 128]
-                largest = piece if largest is None else jnp.maximum(largest, piece)
-            spans.append((start, count, level))
-            start += count
+            take(rows_of(ref, 0, 256), rows_of(ref, 256, 256), 0, index)
+        fourth = [
+            dot(half, either(beside_left, left, right, part * 256, 256)).astype(jnp.bfloat16)
+            for part in range(2)
+        ]
+        take(fourth[0], fourth[1], 1, 12)
         top = jnp.max(largest, axis=1, keepdims=True) * SCALE
         for start, count, level in spans:
             shifted = scores[slot, :, start : start + count] * SCALE - (top - level)
@@ -237,12 +254,13 @@
         out_ref[:, lanes] = (numerator / denominator).astype(jnp.bfloat16)
 
 
-def heads_call(kernel, flags, tensors, outs, scratch, limit, flops):
+def heads_call(kernel, flags, tensors, outs, scratch, limit, flops, away=()):
     whole = pl.BlockSpec(memory_space=pltpu.VMEM)
     several = len(outs) > 1
     return pl.pallas_call(
         kernel,
-        in_specs=[pl.BlockSpec(memory_space=pltpu.SMEM)] + [whole] * len(tensors),
+        in_specs=[pl.BlockSpec(memory_space=pltpu.SMEM)]
+        + [pl.BlockSpec(memory_space=pl.ANY) if i in away else whole for i in range(len(tensors))],
         out_specs=(whole,) * len(outs) if several else whole,
         out_shape=tuple(outs) if several else outs[0],
         scratch_shapes=scratch,
@@ -259,7 +277,10 @@
         pltpu.VMEM((2, rows, KEYS), jnp.bfloat16),
         pltpu.VMEM((2, KEYS, 2 * HEAD_DIM), jnp.bfloat16),
     ]
-    return heads_call(main_kernel, flags, tensors, outs, scratch, 32, 3 * 10**9)
+    away = (3, 4, 7)
+    scratch += [pltpu.VMEM(tensors[i].shape, jnp.bfloat16) for i in away]
+    scratch.append(pltpu.SemaphoreType.DMA((len(away),)))
+    return heads_call(main_kernel, flags, tensors, outs, scratch, 32, 3 * 10**9, away)
 
 
 def attend_late(flags, tensors):

time: 140 us -> 140 us (level)
  local copies, waits for them, and re-layouts: 2.02 us -> 0.13 us
  Pallas kernels: 13 us -> 14.6 us
    unnamed x12 -> x8, local copies, waits for them, and re-layouts: 1.91 us -> 0.02 us
  transfers between devices with their start and end apart: 15 -> 15, of which waited for: 7 -> 7; matrix products, arithmetic and copies ran while one was open for 0% -> 0% of each run, Pallas kernels for 8% -> 9%
where the time goes in v4:
time: 140 us; the launch traced here: 139 us
  starting transfers between devices  66.8 us (48%)
  waiting for transfers between devices  56.7 us (40%)
  Pallas kernels  14.6 us (10%)
    ppermute x12, starting transfers between devices, seq_permute(): return lax.ppermute(value, 'seq', pairs)  55.8 us
    ppermute x12, waiting for transfers between devices, seq_permute(): return lax.ppermute(value, 'seq', pairs)  39.9 us
    ppermute x3, waiting for transfers between devices, head_permute(): return lax.ppermute(value, 'head', [(i, i ^ bit) for i in range(count)])  16.8 us
    ppermute x3, starting transfers between devices, head_permute(): return lax.ppermute(value, 'head', [(i, i ^ bit) for i in range(count)])  11 us
    pallas_call x2, Pallas kernels, heads_call(): pl.pallas_call(kernel, in_specs=[pl.BlockSpec(memory_space=pltpu.SMEM)] +...  8.93 us
    pallas_call x2, Pallas kernels, project(): pl.pallas_call(project_kernel, grid_spec=pltpu.PrefetchScalarGridSpec(num...  3.02 us
  transfers between devices with their start and end apart: 15, of which 7 were waited for; matrix products, arithmetic and copies ran while one was open for 0% of the time, Pallas kernels for 9%

profile of v4, /device:TPU:55, one launch (start us, length us, event | category | flops | bytes accessed | tf_op | source)
XLA Modules:
  0.0 139.3 jit_solution(292622962630503719)
XLA Ops:
  0.0 2.6 %collective-permute-start.13 = (bf16[512,2048]{1,0:T(8,128)(2,1)}, bf16[512,2048]{1,0:T(8,128)(2,1)}, u32[]{:S(2)}, u32[]{:S(2)}) collective-permute-start(bf16[512,2048]{1,0:T(8,128)(2,1)} %wa_ref.3), channel_id=1, source_target_pairs={{0,1},{1,0},{2,3},{3,2},{4,5},{5,4},{6,7},{7,6},{8,9},{9,8},{10,11... | collective-permute-start | bytes 6291464 | tf_op jit(solution)/shard_map/ppermute | solution.py:27
  2.6 1.9 %coarse.1 = (bf16[512,512]{1,0:T(8,128)(2,1)}, bf16[256,512]{1,0:T(8,128)(2,1)S(1)}, bf16[128,512]{1,0:T(8,128)(2,1)S(1)}, bf16[64,512]{1,0:T(8,128)(2,1)S(1)}) custom-call(bf16[256,512]{1,0:T(8,128)(2,1)} %refs_0_.1, bf16[256,512]{1,0:T(8,128)(2,1)} %refs_1_.1), custom_call_target="tpu_custom_call" | custom-call | flops 100000000 | bytes 1000000 | tf_op jit(solution)/shard_map/coarse/pallas_call | solution.py:62
  4.5 3.8 %collective-permute-start.2 = (bf16[256,512]{1,0:T(8,128)(2,1)S(1)}, bf16[256,512]{1,0:T(8,128)(2,1)S(1)}, u32[]{:S(2)}, u32[]{:S(2)}) collective-permute-start(bf16[256,512]{1,0:T(8,128)(2,1)S(1)} %get-tuple-element.13), channel_id=1, source_target_pairs={{0,8},{4,12},{8,0},{12,4},{16,24},{20,28},{24,16},{28,20},{32,40},... | collective-permute-start | bytes 786440 | tf_op jit(solution)/shard_map/ppermute | solution.py:22
  8.3 11.5 %collective-permute-done.2.across_ref.one_ref.refs_4_ = bf16[256,512]{1,0:T(8,128)(2,1)S(1)} collective-permute-done((bf16[256,512]{1,0:T(8,128)(2,1)S(1)}, bf16[256,512]{1,0:T(8,128)(2,1)S(1)}, u32[]{:S(2)}, u32[]{:S(2)}) %collective-permute-start.2) | collective-permute-done | bytes 262176 | tf_op jit(solution)/shard_map/ppermute | solution.py:22
  20.0 3.4 %collective-permute-start.7 = (bf16[256,512]{1,0:T(8,128)(2,1)S(1)}, bf16[256,512]{1,0:T(8,128)(2,1)S(1)}, u32[]{:S(2)}, u32[]{:S(2)}) collective-permute-start(bf16[256,512]{1,0:T(8,128)(2,1)S(1)} %shard_map.46.a_ref), channel_id=1, source_target_pairs={{0,4},{4,0},{8,12},{12,8},{16,20},{20,16},{24,28},{28,24},{32,36},... | collective-permute-start | bytes 786440 | tf_op jit(solution)/shard_map/ppermute | solution.py:22
  23.4 5.8 %collective-permute-done.7.b_ref = bf16[256,512]{1,0:T(8,128)(2,1)S(1)} collective-permute-done((bf16[256,512]{1,0:T(8,128)(2,1)S(1)}, bf16[256,512]{1,0:T(8,128)(2,1)S(1)}, u32[]{:S(2)}, u32[]{:S(2)}) %collective-permute-start.7) | collective-permute-done | bytes 262176 | tf_op jit(solution)/shard_map/ppermute | solution.py:22
  29.3 4.0 %collective-permute-start.8 = (bf16[512,512]{1,0:T(8,128)(2,1)S(1)}, bf16[512,512]{1,0:T(8,128)(2,1)S(1)}, u32[]{:S(2)}, u32[]{:S(2)}) collective-permute-start(bf16[512,512]{1,0:T(8,128)(2,1)S(1)} %shard_map.47), channel_id=1, source_target_pairs={{0,16},{4,20},{8,24},{12,28},{16,32},{20,36},{24,40},{28,44},{32,4... | collective-permute-start | bytes 1572872 | tf_op jit(solution)/shard_map/ppermute | solution.py:22
  33.3 8.9 %collective-permute-start.3 = (bf16[256,512]{1,0:T(8,128)(2,1)S(1)}, bf16[256,512]{1,0:T(8,128)(2,1)S(1)}, u32[]{:S(2)}, u32[]{:S(2)}) collective-permute-start(bf16[256,512]{1,0:T(8,128)(2,1)S(1)} %collective-permute-done.2.across_ref.one_ref.refs_4_), channel_id=1, source_target_pairs={{0,16},{4,20},{16,32},{20,36},{24,8},{28,12},{32,48},{36,52},{40,2... | collective-permute-start | bytes 786440 | tf_op jit(solution)/shard_map/ppermute | solution.py:22
  42.1 1.9 %collective-permute-start.4 = (bf16[64,512]{1,0:T(8,128)(2,1)S(1)}, bf16[64,512]{1,0:T(8,128)(2,1)S(1)}, u32[]{:S(2)}, u32[]{:S(2)}) collective-permute-start(bf16[64,512]{1,0:T(8,128)(2,1)S(1)} %get-tuple-element.14), channel_id=1, source_target_pairs={{0,48},{4,52},{8,56},{12,60},{32,80},{36,84},{40,88},{44,92},{48,0... | collective-permute-start | bytes 196616 | tf_op jit(solution)/shard_map/ppermute | solution.py:22
  44.1 6.3 %collective-permute-done.4.skew_ref.refs_9_ = bf16[64,512]{1,0:T(8,128)(2,1)S(1)} collective-permute-done((bf16[64,512]{1,0:T(8,128)(2,1)S(1)}, bf16[64,512]{1,0:T(8,128)(2,1)S(1)}, u32[]{:S(2)}, u32[]{:S(2)}) %collective-permute-start.4) | collective-permute-done | bytes 65568 | tf_op jit(solution)/shard_map/ppermute | solution.py:22
  50.4 4.7 %collective-permute-start.5 = (bf16[64,512]{1,0:T(8,128)(2,1)S(1)}, bf16[64,512]{1,0:T(8,128)(2,1)S(1)}, u32[]{:S(2)}, u32[]{:S(2)}) collective-permute-start(bf16[64,512]{1,0:T(8,128)(2,1)S(1)} %collective-permute-done.4.skew_ref.refs_9_), channel_id=1, source_target_pairs={{0,8},{4,12},{8,0},{12,4},{16,24},{20,28},{24,16},{28,20},{32,40},... | collective-permute-start | bytes 196616 | tf_op jit(solution)/shard_map/ppermute | solution.py:22
  55.1 11.4 %collective-permute-start.9 = (bf16[512,512]{1,0:T(8,128)(2,1)S(1)}, bf16[512,512]{1,0:T(8,128)(2,1)S(1)}, u32[]{:S(2)}, u32[]{:S(2)}) collective-permute-start(bf16[512,512]{1,0:T(8,128)(2,1)S(1)} %shard_map.47), channel_id=1, source_target_pairs={{16,0},{20,4},{24,8},{28,12},{32,16},{36,20},{40,24},{44,28},{48,3... | collective-permute-start | bytes 1572872 | tf_op jit(solution)/shard_map/ppermute | solution.py:22
  66.6 2.5 %collective-permute-start = (bf16[512,512]{1,0:T(8,128)(2,1)}, bf16[512,512]{1,0:T(8,128)(2,1)}, u32[]{:S(2)}, u32[]{:S(2)}) collective-permute-start(bf16[512,512]{1,0:T(8,128)(2,1)} %get-tuple-element.12), channel_id=1, source_target_pairs={{0,4},{4,8},{8,12},{12,16},{16,20},{20,24},{24,28},{28,32},{32,36}... | collective-permute-start | bytes 1572872 | tf_op jit(solution)/shard_map/ppermute | solution.py:22
  69.1 2.8 %collective-permute-start.1 = (bf16[512,512]{1,0:T(8,128)(2,1)}, bf16[512,512]{1,0:T(8,128)(2,1)}, u32[]{:S(2)}, u32[]{:S(2)}) collective-permute-start(bf16[512,512]{1,0:T(8,128)(2,1)} %get-tuple-element.12), channel_id=1, source_target_pairs={{4,0},{8,4},{12,8},{16,12},{20,16},{24,20},{28,24},{32,28},{36,32}... | collective-permute-start | bytes 1572872 | tf_op jit(solution)/shard_map/ppermute | solution.py:22
  71.9 5.0 %collective-permute-start.6 = (bf16[384,512]{1,0:T(8,128)(2,1)S(1)}, bf16[384,512]{1,0:T(8,128)(2,1)}, u32[]{:S(2)}, u32[]{:S(2)}) collective-permute-start(bf16[384,512]{1,0:T(8,128)(2,1)S(1)} %hand.1), channel_id=1, source_target_pairs={{0,4},{4,0},{8,12},{12,8},{16,20},{20,16},{24,28},{28,24},{32,36},... | collective-permute-start | bytes 1179656 | tf_op jit(solution)/shard_map/ppermute | solution.py:22
  77.4 2.6 %collective-permute-start.10 = (bf16[256,512]{1,0:T(8,128)(2,1)S(1)}, bf16[256,512]{1,0:T(8,128)(2,1)S(1)}, u32[]{:S(2)}, u32[]{:S(2)}) collective-permute-start(bf16[256,512]{1,0:T(8,128)(2,1)S(1)} %shard_map.48.refs_11_), channel_id=1, source_target_pairs={{0,16},{4,20},{8,24},{12,28},{16,32},{20,36},{24,40},{28,44},{32,4... | collective-permute-start | bytes 786440 | tf_op jit(solution)/shard_map/ppermute | solution.py:22
  80.3 4.8 %collective-permute-start.11 = (bf16[256,512]{1,0:T(8,128)(2,1)S(1)}, bf16[256,512]{1,0:T(8,128)(2,1)S(1)}, u32[]{:S(2)}, u32[]{:S(2)}) collective-permute-start(bf16[256,512]{1,0:T(8,128)(2,1)S(1)} %shard_map.49.refs_12_), channel_id=1, source_target_pairs={{16,0},{20,4},{24,8},{28,12},{32,16},{36,20},{40,24},{44,28},{48,3... | collective-permute-start | bytes 786440 | tf_op jit(solution)/shard_map/ppermute | solution.py:22
  85.1 9.1 %collective-permute-done.1.refs_3_ = bf16[512,512]{1,0:T(8,128)(2,1)} collective-permute-done((bf16[512,512]{1,0:T(8,128)(2,1)}, bf16[512,512]{1,0:T(8,128)(2,1)}, u32[]{:S(2)}, u32[]{:S(2)}) %collective-permute-start.1) | collective-permute-done | bytes 524320 | tf_op jit(solution)/shard_map/ppermute | solution.py:22
  94.1 7.2 %collective-permute-done.6.refs_6_ = bf16[384,512]{1,0:T(8,128)(2,1)} collective-permute-done((bf16[384,512]{1,0:T(8,128)(2,1)S(1)}, bf16[384,512]{1,0:T(8,128)(2,1)}, u32[]{:S(2)}, u32[]{:S(2)}) %collective-permute-start.6) | collective-permute-done | bytes 393248 | tf_op jit(solution)/shard_map/ppermute | solution.py:22
  101.3 6.9 %shard_map.50 = (f32[256,512]{1,0:T(8,128)S(1)}, f32[256,512]{1,0:T(8,128)S(1)}, f32[256,512]{1,0:T(8,128)S(1)}) custom-call(s32[13]{0:T(128)S(1)} %convert_element_type.10.flags, bf16[256,512]{1,0:T(8,128)(2,1)S(1)} %copy-done.3, bf16[256,512]{1,0:T(8,128)(2,1)S(1)} %copy-done.1, bf16[256,512]{1,0:T(8,128)(2,1)S(1)} %copy-done.2, ...), custom_call_target="tpu_custom_call" | custom-call | flops 3000000000 | bytes 6000000 | tf_op jit(solution)/shard_map/pallas_call | solution.py:260
  108.3 2.0 %shard_map.51.a_ref = bf16[256,512]{1,0:T(8,128)(2,1)S(1)} custom-call(s32[13]{0:T(128)S(1)} %convert_element_type.10.flags, bf16[256,512]{1,0:T(8,128)(2,1)S(1)} %copy-done.3, f32[256,512]{1,0:T(8,128)S(1)} %get-tuple-element.16.sum_ref, f32[256,512]{1,0:T(8,128)S(1)} %get-tuple-element.17.weight_ref, f32[256,512]{1,0:T(8,128)S(1)} %get-tuple-element.18.top_ref, ...), custom_call_target="tpu_custom_call" | custom-call | flops 300000000 | bytes 6000000 | tf_op jit(solution)/shard_map/pallas_call | solution.py:260
  110.3 6.5 %collective-permute-start.12 = (bf16[256,512]{1,0:T(8,128)(2,1)S(1)}, bf16[256,512]{1,0:T(8,128)(2,1)S(1)}, u32[]{:S(2)}, u32[]{:S(2)}) collective-permute-start(bf16[256,512]{1,0:T(8,128)(2,1)S(1)} %shard_map.51.a_ref), channel_id=1, source_target_pairs={{0,1},{1,0},{2,3},{3,2},{4,5},{5,4},{6,7},{7,6},{8,9},{9,8},{10,11... | collective-permute-start | bytes 786440 | tf_op jit(solution)/shard_map/ppermute | solution.py:27
  119.5 1.9 %collective-permute-start.14 = (bf16[256,512]{1,0:T(8,128)(2,1)S(1)}, bf16[256,512]{1,0:T(8,128)(2,1)S(1)}, u32[]{:S(2)}, u32[]{:S(2)}) collective-permute-start(bf16[256,512]{1,0:T(8,128)(2,1)S(1)} %shard_map.53), channel_id=1, source_target_pairs={{0,2},{1,3},{2,0},{3,1},{4,6},{5,7},{6,4},{7,5},{8,10},{9,11},{10,... | collective-permute-start | bytes 786440 | tf_op jit(solution)/shard_map/ppermute | solution.py:27
  122.9 15.6 %collective-permute-done.14 = bf16[256,512]{1,0:T(8,128)(2,1)S(1)} collective-permute-done((bf16[256,512]{1,0:T(8,128)(2,1)S(1)}, bf16[256,512]{1,0:T(8,128)(2,1)S(1)}, u32[]{:S(2)}, u32[]{:S(2)}) %collective-permute-start.14) | collective-permute-done | bytes 262176 | tf_op jit(solution)/shard_map/ppermute | solution.py:27
  (27 shorter events, 5.8 us)
Async XLA Ops:
  0.0 118.0 %collective-permute-start.13 = (bf16[512,2048]{1,0:T(8,128)(2,1)}, bf16[512,2048]{1,0:T(8,128)(2,1)}, u32[]{:S(2)}, u32[]{:S(2)}) collective-permute-start(bf16[512,2048]{1,0:T(8,128)(2,1)} %wa_ref.3), channel_id=1, source_target_pairs={{0,1},{1,0},{2,3},{3,2},{4,5},{5,4},{6,7},{7,6},{8,9},{9,8},{10,11... | collective-permute-start | bytes 6291464 | tf_op jit(solution)/shard_map/ppermute | solution.py:27
  4.5 15.3 %collective-permute-start.2 = (bf16[256,512]{1,0:T(8,128)(2,1)S(1)}, bf16[256,512]{1,0:T(8,128)(2,1)S(1)}, u32[]{:S(2)}, u32[]{:S(2)}) collective-permute-start(bf16[256,512]{1,0:T(8,128)(2,1)S(1)} %get-tuple-element.13), channel_id=1, source_target_pairs={{0,8},{4,12},{8,0},{12,4},{16,24},{20,28},{24,16},{28,20},{32,40},... | collective-permute-start | bytes 786440 | tf_op jit(solution)/shard_map/ppermute | solution.py:22
  19.8 81.6 %copy-start.1 = (bf16[256,512]{1,0:T(8,128)(2,1)S(1)}, bf16[256,512]{1,0:T(8,128)(2,1)}, u32[]{:S(2)}) copy-start(bf16[256,512]{1,0:T(8,128)(2,1)} %refs_0_.1) | copy-start | bytes 786436
  19.8 81.6 %copy-start.2 = (bf16[256,512]{1,0:T(8,128)(2,1)S(1)}, bf16[256,512]{1,0:T(8,128)(2,1)}, u32[]{:S(2)}) copy-start(bf16[256,512]{1,0:T(8,128)(2,1)} %refs_1_.1) | copy-start | bytes 786436
  19.8 81.6 %copy-start.3 = (bf16[256,512]{1,0:T(8,128)(2,1)S(1)}, bf16[256,512]{1,0:T(8,128)(2,1)}, u32[]{:S(2)}) copy-start(bf16[256,512]{1,0:T(8,128)(2,1)} %q_ref.3) | copy-start | bytes 786436
  20.0 9.3 %collective-permute-start.7 = (bf16[256,512]{1,0:T(8,128)(2,1)S(1)}, bf16[256,512]{1,0:T(8,128)(2,1)S(1)}, u32[]{:S(2)}, u32[]{:S(2)}) collective-permute-start(bf16[256,512]{1,0:T(8,128)(2,1)S(1)} %shard_map.46.a_ref), channel_id=1, source_target_pairs={{0,4},{4,0},{8,12},{12,8},{16,20},{20,16},{24,28},{28,24},{32,36},... | collective-permute-start | bytes 786440 | tf_op jit(solution)/shard_map/ppermute | solution.py:22
  29.3 42.7 %collective-permute-start.8 = (bf16[512,512]{1,0:T(8,128)(2,1)S(1)}, bf16[512,512]{1,0:T(8,128)(2,1)S(1)}, u32[]{:S(2)}, u32[]{:S(2)}) collective-permute-start(bf16[512,512]{1,0:T(8,128)(2,1)S(1)} %shard_map.47), channel_id=1, source_target_pairs={{0,16},{4,20},{8,24},{12,28},{16,32},{20,36},{24,40},{28,44},{32,4... | collective-permute-start | bytes 1572872 | tf_op jit(solution)/shard_map/ppermute | solution.py:22
  33.3 35.8 %collective-permute-start.3 = (bf16[256,512]{1,0:T(8,128)(2,1)S(1)}, bf16[256,512]{1,0:T(8,128)(2,1)S(1)}, u32[]{:S(2)}, u32[]{:S(2)}) collective-permute-start(bf16[256,512]{1,0:T(8,128)(2,1)S(1)} %collective-permute-done.2.across_ref.one_ref.refs_4_), channel_id=1, source_target_pairs={{0,16},{4,20},{16,32},{20,36},{24,8},{28,12},{32,48},{36,52},{40,2... | collective-permute-start | bytes 786440 | tf_op jit(solution)/shard_map/ppermute | solution.py:22
  42.1 8.2 %collective-permute-start.4 = (bf16[64,512]{1,0:T(8,128)(2,1)S(1)}, bf16[64,512]{1,0:T(8,128)(2,1)S(1)}, u32[]{:S(2)}, u32[]{:S(2)}) collective-permute-start(bf16[64,512]{1,0:T(8,128)(2,1)S(1)} %get-tuple-element.14), channel_id=1, source_target_pairs={{0,48},{4,52},{8,56},{12,60},{32,80},{36,84},{40,88},{44,92},{48,0... | collective-permute-start | bytes 196616 | tf_op jit(solution)/shard_map/ppermute | solution.py:22
  50.4 16.2 %collective-permute-start.5 = (bf16[64,512]{1,0:T(8,128)(2,1)S(1)}, bf16[64,512]{1,0:T(8,128)(2,1)S(1)}, u32[]{:S(2)}, u32[]{:S(2)}) collective-permute-start(bf16[64,512]{1,0:T(8,128)(2,1)S(1)} %collective-permute-done.4.skew_ref.refs_9_), channel_id=1, source_target_pairs={{0,8},{4,12},{8,0},{12,4},{16,24},{20,28},{24,16},{28,20},{32,40},... | collective-permute-start | bytes 196616 | tf_op jit(solution)/shard_map/ppermute | solution.py:22
  55.1 22.3 %collective-permute-start.9 = (bf16[512,512]{1,0:T(8,128)(2,1)S(1)}, bf16[512,512]{1,0:T(8,128)(2,1)S(1)}, u32[]{:S(2)}, u32[]{:S(2)}) collective-permute-start(bf16[512,512]{1,0:T(8,128)(2,1)S(1)} %shard_map.47), channel_id=1, source_target_pairs={{16,0},{20,4},{24,8},{28,12},{32,16},{36,20},{40,24},{44,28},{48,3... | collective-permute-start | bytes 1572872 | tf_op jit(solution)/shard_map/ppermute | solution.py:22
  66.6 13.7 %collective-permute-start = (bf16[512,512]{1,0:T(8,128)(2,1)}, bf16[512,512]{1,0:T(8,128)(2,1)}, u32[]{:S(2)}, u32[]{:S(2)}) collective-permute-start(bf16[512,512]{1,0:T(8,128)(2,1)} %get-tuple-element.12), channel_id=1, source_target_pairs={{0,4},{4,8},{8,12},{12,16},{16,20},{20,24},{24,28},{28,32},{32,36}... | collective-permute-start | bytes 1572872 | tf_op jit(solution)/shard_map/ppermute | solution.py:22
  69.1 25.1 %collective-permute-start.1 = (bf16[512,512]{1,0:T(8,128)(2,1)}, bf16[512,512]{1,0:T(8,128)(2,1)}, u32[]{:S(2)}, u32[]{:S(2)}) collective-permute-start(bf16[512,512]{1,0:T(8,128)(2,1)} %get-tuple-element.12), channel_id=1, source_target_pairs={{4,0},{8,4},{12,8},{16,12},{20,16},{24,20},{28,24},{32,28},{36,32}... | collective-permute-start | bytes 1572872 | tf_op jit(solution)/shard_map/ppermute | solution.py:22
  71.9 29.4 %collective-permute-start.6 = (bf16[384,512]{1,0:T(8,128)(2,1)S(1)}, bf16[384,512]{1,0:T(8,128)(2,1)}, u32[]{:S(2)}, u32[]{:S(2)}) collective-permute-start(bf16[384,512]{1,0:T(8,128)(2,1)S(1)} %hand.1), channel_id=1, source_target_pairs={{0,4},{4,0},{8,12},{12,8},{16,20},{20,16},{24,28},{28,24},{32,36},... | collective-permute-start | bytes 1179656 | tf_op jit(solution)/shard_map/ppermute | solution.py:22
  77.4 30.9 %collective-permute-start.10 = (bf16[256,512]{1,0:T(8,128)(2,1)S(1)}, bf16[256,512]{1,0:T(8,128)(2,1)S(1)}, u32[]{:S(2)}, u32[]{:S(2)}) collective-permute-start(bf16[256,512]{1,0:T(8,128)(2,1)S(1)} %shard_map.48.refs_11_), channel_id=1, source_target_pairs={{0,16},{4,20},{8,24},{12,28},{16,32},{20,36},{24,40},{28,44},{32,4... | collective-permute-start | bytes 786440 | tf_op jit(solution)/shard_map/ppermute | solution.py:22
  80.3 28.0 %collective-permute-start.11 = (bf16[256,512]{1,0:T(8,128)(2,1)S(1)}, bf16[256,512]{1,0:T(8,128)(2,1)S(1)}, u32[]{:S(2)}, u32[]{:S(2)}) collective-permute-start(bf16[256,512]{1,0:T(8,128)(2,1)S(1)} %shard_map.49.refs_12_), channel_id=1, source_target_pairs={{16,0},{20,4},{24,8},{28,12},{32,16},{36,20},{40,24},{44,28},{48,3... | collective-permute-start | bytes 786440 | tf_op jit(solution)/shard_map/ppermute | solution.py:22
  108.3 9.7 %copy-start = (bf16[512,2048]{1,0:T(8,128)(2,1)S(1)}, bf16[512,2048]{1,0:T(8,128)(2,1)}, u32[]{:S(2)}) copy-start(bf16[512,2048]{1,0:T(8,128)(2,1)} %wa_ref.3) | copy-start | bytes 6291460
  110.3 7.6 %collective-permute-start.12 = (bf16[256,512]{1,0:T(8,128)(2,1)S(1)}, bf16[256,512]{1,0:T(8,128)(2,1)S(1)}, u32[]{:S(2)}, u32[]{:S(2)}) collective-permute-start(bf16[256,512]{1,0:T(8,128)(2,1)S(1)} %shard_map.51.a_ref), channel_id=1, source_target_pairs={{0,1},{1,0},{2,3},{3,2},{4,5},{5,4},{6,7},{7,6},{8,9},{9,8},{10,11... | collective-permute-start | bytes 786440 | tf_op jit(solution)/shard_map/ppermute | solution.py:27
  119.5 19.1 %collective-permute-start.14 = (bf16[256,512]{1,0:T(8,128)(2,1)S(1)}, bf16[256,512]{1,0:T(8,128)(2,1)S(1)}, u32[]{:S(2)}, u32[]{:S(2)}) collective-permute-start(bf16[256,512]{1,0:T(8,128)(2,1)S(1)} %shard_map.53), channel_id=1, source_target_pairs={{0,2},{1,3},{2,0},{3,1},{4,6},{5,7},{6,4},{7,5},{8,10},{9,11},{10,... | collective-permute-start | bytes 786440 | tf_op jit(solution)/shard_map/ppermute | solution.py:27

commit v5 on v4

--- a/solution.py
+++ b/solution.py
@@ -126,8 +126,7 @@
     )(*operands)
 
 
-LATE = 2 * 128
-KEYS = 768 + 3 * 512 - LATE
+KEYS = 1152
 SCALE = LOG2E * HEAD_DIM**-0.5
 
 
@@ -135,122 +134,136 @@
     return jnp.where(flags[index] > 0, 0.0, -jnp.inf)
 
 
-def main_kernel(flags, q_ref, *refs):
-    k_ref, v_ref = refs[0:2]
-    across, far = refs[4:6]
-    twos = refs[7:9]
-    skews = refs[9:11]
-    nears = refs[11:13]
-    sum_ref, weight_ref, top_ref = refs[13:16]
-    scores, weights, values, left, right, third, arrived = refs[16:23]
-    copies = [
-        pltpu.make_async_copy(source, target, arrived.at[index])
-        for index, (source, target) in enumerate(
-            ((refs[2], left), (refs[3], right), (refs[6], third))
-        )
-    ]
-    for copy in copies:
-        copy.start()
-
+class Pass:
+    def __init__(self, slot, queries, flags, scores, weights, values):
+        self.slot, self.queries, self.flags = slot, queries, flags
+        self.scores, self.weights, self.values = scores, weights, values
+        self.largest, self.spans = None, []
+
+    def take(self, keys, vals, level, flag):
+        start = self.spans[-1][0] + self.spans[-1][1] if self.spans else 0
+        count = keys.shape[0]
+        part = dot_t(self.queries[level], keys)
+        if flag is not None:
+            part = part + bias(self.flags, flag)
+        self.scores[self.slot, :, start : start + count] = part
+        self.values[self.slot, start : start + count, :HEAD_DIM] = vals
+        for column in range(0, count, 128):
+            piece = part[:, column : column + 128]
+            self.largest = piece if self.largest is None else jnp.maximum(self.largest, piece)
+        self.spans.append((start, count, level))
+
+    def top(self):
+        return jnp.max(self.largest, axis=1, keepdims=True) * SCALE
+
+    def sums(self, top):
+        for start, count, level in self.spans:
+            shifted = self.scores[self.slot, :, start : start + count] * SCALE - (top - level)
+            self.weights[self.slot, :, start : start + count] = jnp.exp2(shifted).astype(
+                jnp.bfloat16
+            )
+        total = dot(self.weights[self.slot], self.values[self.slot])
+        return total[:, :HEAD_DIM], total[:, HEAD_DIM:]
+
+
+def start_head(head, q_ref, spreads, flags, scratch):
+    lanes = slice(head * HEAD_DIM, (head + 1) * HEAD_DIM)
+    query = q_ref[:, lanes]
+    queries = {level: dot(spread, query).astype(jnp.bfloat16) for level, spread in spreads.items()}
+    queries[0] = query
+    return lanes, Pass(head % 2, queries, flags, *scratch)
+
+
+def spreads_for(rows, levels, values):
+    for slot in range(2):
+        values[slot, :, HEAD_DIM:] = jnp.ones((KEYS, HEAD_DIM), jnp.bfloat16)
+    return {level: spread_mean_matrix(rows, 2**level) for level in levels}
+
+
+def main_kernel(flags, q_ref, k_ref, v_ref, across, far, low, high, near_low, near_high, *refs):
+    sum_ref, weight_ref, top_ref = refs[:3]
+    scratch = refs[3:6]
     rows = q_ref.shape[0]
     even = flags[6] > 0
+    spreads = spreads_for(rows, (1, 2, 3), scratch[2])
+    for head in range(q_ref.shape[1] // HEAD_DIM):
+        lanes, work = start_head(head, q_ref, spreads, flags, scratch)
+        work.take(k_ref[:, lanes], v_ref[:, lanes], 0, None)
+        for ref, flag in ((low, 3), (high, 4)):
+            work.take(ref[:256, lanes], ref[256:, lanes], 2, flag)
+        near = [
+            jnp.where(
+                even,
+                near_low[part * 128 : (part + 1) * 128, lanes],
+                near_high[part * 128 : (part + 1) * 128, lanes],
+            )
+            for part in range(2)
+        ]
+        work.take(near[0], near[1], 3, 9)
+        for ref, flag in ((across, None), (far, 10)):
+            work.take(ref[:128, lanes], ref[128:, lanes], 1, flag)
+        top = work.top()
+        numerator, denominator = work.sums(top)
+        sum_ref[:, lanes] = numerator
+        weight_ref[:, lanes] = denominator
+        top_ref[:, lanes] = jnp.broadcast_to(top, (rows, HEAD_DIM))
+
+
+def late_kernel(flags, q_ref, sum_ref, weight_ref, top_ref, low, high, skew, skew_across, *refs):
+    third_from, left_from, right_from, left_wrap, right_wrap, out_ref = refs[:6]
+    scratch = refs[6:9]
+    third, left, right, arrived = refs[9:13]
+    copies = [pltpu.make_async_copy(third_from, third, arrived.at[0])]
+    copies[0].start()
+    sides = ((left_from, left_wrap, left, 13), (right_from, right_wrap, right, 14))
+    for index, (inner_from, wrap_from, target, flag) in enumerate(sides, 1):
+        inner = pltpu.make_async_copy(inner_from, target, arrived.at[index])
+        wrapped = pltpu.make_async_copy(wrap_from, target, arrived.at[index])
+        lax.cond(flags[flag] > 0, wrapped.start, inner.start)
+        copies.append(inner)
+
     beside_left = flags[2] > 0
     half = mean_matrix(128, 2)
-    spreads = [spread_mean_matrix(rows, 2**level) for level in range(1, 4)]
-    for slot in range(2):
-        values[slot, :, HEAD_DIM:] = jnp.ones((KEYS, HEAD_DIM), jnp.bfloat16)
-
+    spreads = spreads_for(q_ref.shape[0], (1, 3), scratch[2])
     for head in range(q_ref.shape[1] // HEAD_DIM):
-        slot = head % 2
-        lanes = slice(head * HEAD_DIM, (head + 1) * HEAD_DIM)
-
-        def rows_of(ref, start, count):
-            return ref[start : start + count, lanes]
-
-        def either(flag, first, second, start, count):
-            return jnp.where(flag, rows_of(first, start, count), rows_of(second, start, count))
-
-        query = rows_of(q_ref, 0, rows)
-        queries = [query] + [dot(spread, query).astype(jnp.bfloat16) for spread in spreads]
-        largest = None
-        spans = []
-
-        def take(keys, vals, level, flag):
-            nonlocal largest
-            start = spans[-1][0] + spans[-1][1] if spans else 0
-            count = keys.shape[0]
-            part = dot_t(queries[level], keys)
-            if flag is not None:
-                part = part + bias(flags, flag)
-            scores[slot, :, start : start + count] = part
-            values[slot, start : start + count, :HEAD_DIM] = vals
-            for column in range(0, count, 128):
-                piece = part[:, column : column + 128]
-                largest = piece if largest is None else jnp.maximum(largest, piece)
-            spans.append((start, count, level))
-
-        take(rows_of(k_ref, 0, 256), rows_of(v_ref, 0, 256), 0, None)
-        for index, ref in enumerate(twos):
-            take(rows_of(ref, 0, 256), rows_of(ref, 256, 256), 2, 3 + index)
-        near = [either(even, nears[0], nears[1], part * 128, 128) for part in range(2)]
-        take(near[0], near[1], 3, 9)
-        for ref, flag in ((across, None), (far, 10)):
-            take(rows_of(ref, 0, 128), rows_of(ref, 128, 128), 1, flag)
+        lanes, work = start_head(head, q_ref, spreads, flags, scratch)
+        for ref, flag in ((low, 5), (high, 7)):
+            work.take(ref[:128, lanes], ref[128:, lanes], 3, flag)
         if head == 0:
             for copy in copies:
                 copy.wait()
-        take(rows_of(third, 0, 128), rows_of(third, 128, 128), 1, 11)
-        skew = [
+        gathered = [
             jnp.concatenate(
                 [
-                    rows_of(skews[0], part * 32, 32),
-                    rows_of(skews[1], part * 32, 32),
-                    rows_of(third, 256 + part * 32, 32),
-                    rows_of(third, 320 + part * 32, 32),
+                    ref[base + part * 32 : base + (part + 1) * 32, lanes]
+                    for ref, base in ((skew, 0), (skew_across, 0), (third, 256), (third, 320))
                 ],
                 0,
             )
             for part in range(2)
         ]
-        take(skew[0], skew[1], 3, 8)
-        for index, ref in enumerate((left, right)):
-            take(rows_of(ref, 0, 256), rows_of(ref, 256, 256), 0, index)
+        work.take(gathered[0], gathered[1], 3, 8)
+        work.take(third[:128, lanes], third[128:256, lanes], 1, 11)
+        for ref, flag in ((left, 0), (right, 1)):
+            work.take(ref[:256, lanes], ref[256:, lanes], 0, flag)
         fourth = [
-            dot(half, either(beside_left, left, right, part * 256, 256)).astype(jnp.bfloat16)
+            dot(
+                half,
+                jnp.where(
+                    beside_left,
+                    left[part * 256 : (part + 1) * 256, lanes],
+                    right[part * 256 : (part + 1) * 256, lanes],
+                ),
+            ).astype(jnp.bfloat16)
             for part in range(2)
         ]
-        take(fourth[0], fourth[1], 1, 12)
-        top = jnp.max(largest, axis=1, keepdims=True) * SCALE
-        for start, count, level in spans:
-            shifted = scores[slot, :, start : start + count] * SCALE - (top - level)
-            weights[slot, :, start : start + count] = jnp.exp2(shifted).astype(jnp.bfloat16)
-        total = dot(weights[slot], values[slot])
-        sum_ref[:, lanes] = total[:, :HEAD_DIM]
-        weight_ref[:, lanes] = total[:, HEAD_DIM:]
-        top_ref[:, lanes] = jnp.broadcast_to(top, (rows, HEAD_DIM))
-
-
-def late_kernel(flags, q_ref, sum_ref, weight_ref, top_ref, low, high, out_ref, values):
-    rows = q_ref.shape[0]
-    spread = spread_mean_matrix(rows, 8)
-    for slot in range(2):
-        values[slot, :, HEAD_DIM:] = jnp.ones((LATE, HEAD_DIM), jnp.bfloat16)
-    for head in range(q_ref.shape[1] // HEAD_DIM):
-        slot = head % 2
-        lanes = slice(head * HEAD_DIM, (head + 1) * HEAD_DIM)
-        query = dot(spread, q_ref[:, lanes]).astype(jnp.bfloat16)
-        parts = []
-        for index, (ref, flag) in enumerate(((low, 5), (high, 7))):
-            parts.append(dot_t(query, ref[:128, lanes]) + bias(flags, flag))
-            values[slot, index * 128 : (index + 1) * 128, :HEAD_DIM] = ref[128:, lanes]
+        work.take(fourth[0], fourth[1], 1, 12)
         early = top_ref[:, lanes]
-        top = jnp.max(jnp.maximum(parts[0], parts[1]), axis=1, keepdims=True) * SCALE
-        top = jnp.maximum(early, top)
+        top = jnp.maximum(early[:, :1], work.top())
         kept = jnp.exp2(early - top)
-        part = jnp.concatenate([jnp.exp2(p * SCALE - (top - 3.0)) for p in parts], 1)
-        total = dot(part.astype(jnp.bfloat16), values[slot])
-        numerator = sum_ref[:, lanes] * kept + total[:, :HEAD_DIM]
-        denominator = weight_ref[:, lanes] * kept + total[:, HEAD_DIM:]
+        numerator, denominator = work.sums(top)
+        numerator = sum_ref[:, lanes] * kept + numerator
+        denominator = weight_ref[:, lanes] * kept + denominator
         out_ref[:, lanes] = (numerator / denominator).astype(jnp.bfloat16)
 
 
@@ -269,25 +282,28 @@
     )(flags, *tensors)
 
 
-def attend_main(flags, tensors):
-    rows, width = tensors[0].shape
-    outs = [jax.ShapeDtypeStruct((rows, width), jnp.float32)] * 3
-    scratch = [
+def scratch_for(rows):
+    return [
         pltpu.VMEM((2, rows, KEYS), jnp.float32),
         pltpu.VMEM((2, rows, KEYS), jnp.bfloat16),
         pltpu.VMEM((2, KEYS, 2 * HEAD_DIM), jnp.bfloat16),
     ]
-    away = (3, 4, 7)
-    scratch += [pltpu.VMEM(tensors[i].shape, jnp.bfloat16) for i in away]
-    scratch.append(pltpu.SemaphoreType.DMA((len(away),)))
-    return heads_call(main_kernel, flags, tensors, outs, scratch, 32, 3 * 10**9, away)
+
+
+def attend_main(flags, tensors):
+    rows, width = tensors[0].shape
+    outs = [jax.ShapeDtypeStruct((rows, width), jnp.float32)] * 3
+    scratch = scratch_for(rows)
+    return heads_call(main_kernel, flags, tensors, outs, scratch, 24, 2 * 10**9)
 
 
 def attend_late(flags, tensors):
     rows, width = tensors[0].shape
     outs = [jax.ShapeDtypeStruct((rows, width), jnp.bfloat16)]
-    scratch = [pltpu.VMEM((2, LATE, 2 * HEAD_DIM), jnp.bfloat16)]
-    return heads_call(late_kernel, flags, tensors, outs, scratch, 16, 3 * 10**8)
+    away = (8, 9, 10, 11, 12)
+    scratch = scratch_for(rows) + [pltpu.VMEM(tensors[i].shape, jnp.bfloat16) for i in away[:3]]
+    scratch.append(pltpu.SemaphoreType.DMA((3,)))
+    return heads_call(late_kernel, flags, tensors, outs, scratch, 24, 2 * 10**9, away)
 
 
 def project_kernel(column, a_ref, b_ref, wa_ref, wb_ref, out_ref):
@@ -330,14 +346,16 @@
     two_beside = seq_permute(two_half, lambda i: i ^ 1)
     skew_across = seq_permute(skew, lambda i: i ^ 2)
     far = seq_permute(across, lambda i: i + 4 if i % 4 < 2 else i - 4)
-    left = seq_permute(raw, lambda i: i + 1)
-    right = seq_permute(raw, lambda i: i - 1)
+    left = seq_permute(raw, lambda i: i + 1 if i % 4 < 3 else -1)
+    right = seq_permute(raw, lambda i: i - 1 if i % 4 > 0 else -1)
     two_block = small(pack_kernel, two_half, two_beside, rows=(512,))
     two_low = seq_permute(two_block, lambda i: i + 4)
     two_high = seq_permute(two_block, lambda i: i - 4)
     outer = (spot == 0) | (spot == 3)
     handed = hand(outer.astype(jnp.int32).reshape(1), far, across, skew, skew_across)
     third = seq_permute(handed, lambda i: i ^ 1)
+    left_wrap = seq_permute(raw, lambda i: i + 1 if i % 4 == 3 else -1)
+    right_wrap = seq_permute(raw, lambda i: i - 1 if i % 4 == 0 else -1)
     near_low = small(halve_kernel, two_low)
     near_high = small(halve_kernel, two_high)
     three_low = seq_permute(near_low, lambda i: i + 4)
@@ -359,12 +377,15 @@
             far_ok,
             outer | far_ok,
             jnp.logical_not(outer) | far_ok,
+            spot == 0,
+            spot == 3,
         ]
     ).astype(jnp.int32)
-    tensors = [queries, key_rows, value_rows, left, right, across, far, third]
-    tensors += [two_low, two_high, skew, skew_across, near_low, near_high]
-    partial = attend_main(flags, tensors)
-    attended = attend_late(flags, [queries, *partial, three_low, three_high])
+    tensors = [queries, key_rows, value_rows, across, far, two_low, two_high]
+    partial = attend_main(flags, tensors + [near_low, near_high])
+    tensors = [queries, *partial, three_low, three_high, skew, skew_across]
+    tensors += [third, left, right, left_wrap, right_wrap]
+    attended = attend_late(flags, tensors)
     peer = head_permute(attended, 1)
     here_column, away_column = head.reshape(1), (head ^ 2).reshape(1)
     weights = (out_weight, peer_weight)

time: 140 us -> 126 us (0.900)
  the two profiles are of different devices: /device:TPU:55 before, /device:TPU:7 now
where the time goes in v5:
time: 126 us
  starting transfers between devices  69.5 us (55%)
  waiting for transfers between devices  36.6 us (29%)
  Pallas kernels  16.4 us (13%)
  local copies, waits for them, and re-layouts  1.87 us (1%)
    ppermute x14, starting transfers between devices, seq_permute(): return lax.ppermute(value, 'seq', pairs)  54.6 us
    ppermute x14, waiting for transfers between devices, seq_permute(): return lax.ppermute(value, 'seq', pairs)  23.7 us
    ppermute x3, starting transfers between devices, head_permute(): return lax.ppermute(value, 'head', [(i, i ^ bit) for i in range(count)])  14.9 us
    ppermute x3, waiting for transfers between devices, head_permute(): return lax.ppermute(value, 'head', [(i, i ^ bit) for i in range(count)])  13 us
    pallas_call x2, Pallas kernels, heads_call(): pl.pallas_call(kernel, in_specs=[pl.BlockSpec(memory_space=pltpu.SMEM)] +...  10.8 us
    pallas_call x2, Pallas kernels, project(): pl.pallas_call(project_kernel, grid_spec=pltpu.PrefetchScalarGridSpec(num...  3.02 us
  transfers between devices with their start and end apart: 17, of which 6 were waited for; matrix products, arithmetic and copies ran while one was open for 0% of the time, Pallas kernels for 12%

profile of v5, /device:TPU:7, one launch (start us, length us, event | category | flops | bytes accessed | tf_op | source)
XLA Modules:
  0.0 125.5 jit_solution(10751024319022704307)
XLA Ops:
  0.0 2.6 %collective-permute-start.15 = (bf16[512,2048]{1,0:T(8,128)(2,1)}, bf16[512,2048]{1,0:T(8,128)(2,1)}, u32[]{:S(2)}, u32[]{:S(2)}) collective-permute-start(bf16[512,2048]{1,0:T(8,128)(2,1)} %wa_ref.3), channel_id=1, source_target_pairs={{0,1},{1,0},{2,3},{3,2},{4,5},{5,4},{6,7},{7,6},{8,9},{9,8},{10,11... | collective-permute-start | bytes 6291464 | tf_op jit(solution)/shard_map/ppermute | solution.py:27
  2.6 1.9 %coarse.1 = (bf16[512,512]{1,0:T(8,128)(2,1)}, bf16[256,512]{1,0:T(8,128)(2,1)S(1)}, bf16[128,512]{1,0:T(8,128)(2,1)S(1)}, bf16[64,512]{1,0:T(8,128)(2,1)S(1)}) custom-call(bf16[256,512]{1,0:T(8,128)(2,1)} %k_ref.3, bf16[256,512]{1,0:T(8,128)(2,1)} %v_ref.3), custom_call_target="tpu_custom_call" | custom-call | flops 100000000 | bytes 1000000 | tf_op jit(solution)/shard_map/coarse/pallas_call | solution.py:62
  4.5 4.2 %collective-permute-start = (bf16[256,512]{1,0:T(8,128)(2,1)S(1)}, bf16[256,512]{1,0:T(8,128)(2,1)S(1)}, u32[]{:S(2)}, u32[]{:S(2)}) collective-permute-start(bf16[256,512]{1,0:T(8,128)(2,1)S(1)} %get-tuple-element.12), channel_id=1, source_target_pairs={{0,8},{4,12},{8,0},{12,4},{16,24},{20,28},{24,16},{28,20},{32,40},... | collective-permute-start | bytes 786440 | tf_op jit(solution)/shard_map/ppermute | solution.py:22
  8.7 12.0 %collective-permute-done.one_ref.across.across_ref = bf16[256,512]{1,0:T(8,128)(2,1)S(1)} collective-permute-done((bf16[256,512]{1,0:T(8,128)(2,1)S(1)}, bf16[256,512]{1,0:T(8,128)(2,1)S(1)}, u32[]{:S(2)}, u32[]{:S(2)}) %collective-permute-start) | collective-permute-done | bytes 262176 | tf_op jit(solution)/shard_map/ppermute | solution.py:22
  20.9 2.7 %collective-permute-start.2 = (bf16[256,512]{1,0:T(8,128)(2,1)S(1)}, bf16[256,512]{1,0:T(8,128)(2,1)S(1)}, u32[]{:S(2)}, u32[]{:S(2)}) collective-permute-start(bf16[256,512]{1,0:T(8,128)(2,1)S(1)} %shard_map.46.a_ref), channel_id=1, source_target_pairs={{0,4},{4,0},{8,12},{12,8},{16,20},{20,16},{24,28},{28,24},{32,36},... | collective-permute-start | bytes 786440 | tf_op jit(solution)/shard_map/ppermute | solution.py:22
  23.7 2.6 %collective-permute-start.10 = (bf16[512,512]{1,0:T(8,128)(2,1)}, bf16[512,512]{1,0:T(8,128)(2,1)S(1)}, u32[]{:S(2)}, u32[]{:S(2)}) collective-permute-start(bf16[512,512]{1,0:T(8,128)(2,1)} %get-tuple-element.18), channel_id=1, source_target_pairs={{0,4},{4,8},{8,12},{16,20},{20,24},{24,28},{32,36},{36,40},{40,44}... | collective-permute-start | bytes 1572872 | tf_op jit(solution)/shard_map/ppermute | solution.py:22
  26.3 7.6 %collective-permute-start.7 = (bf16[64,512]{1,0:T(8,128)(2,1)S(1)}, bf16[64,512]{1,0:T(8,128)(2,1)S(1)}, u32[]{:S(2)}, u32[]{:S(2)}) collective-permute-start(bf16[64,512]{1,0:T(8,128)(2,1)S(1)} %get-tuple-element.17), channel_id=1, source_target_pairs={{0,48},{4,52},{8,56},{12,60},{32,80},{36,84},{40,88},{44,92},{48,0... | collective-permute-start | bytes 196616 | tf_op jit(solution)/shard_map/ppermute | solution.py:22
  33.9 6.4 %collective-permute-start.1 = (bf16[256,512]{1,0:T(8,128)(2,1)S(1)}, bf16[256,512]{1,0:T(8,128)(2,1)S(1)}, u32[]{:S(2)}, u32[]{:S(2)}) collective-permute-start(bf16[256,512]{1,0:T(8,128)(2,1)S(1)} %collective-permute-done.one_ref.across.across_ref), channel_id=1, source_target_pairs={{0,16},{4,20},{16,32},{20,36},{24,8},{28,12},{32,48},{36,52},{40,2... | collective-permute-start | bytes 786440 | tf_op jit(solution)/shard_map/ppermute | solution.py:22
  40.3 1.9 %collective-permute-start.3 = (bf16[512,512]{1,0:T(8,128)(2,1)S(1)}, bf16[512,512]{1,0:T(8,128)(2,1)S(1)}, u32[]{:S(2)}, u32[]{:S(2)}) collective-permute-start(bf16[512,512]{1,0:T(8,128)(2,1)S(1)} %shard_map.47), channel_id=1, source_target_pairs={{0,16},{4,20},{8,24},{12,28},{16,32},{20,36},{24,40},{28,44},{32,4... | collective-permute-start | bytes 1572872 | tf_op jit(solution)/shard_map/ppermute | solution.py:22
  42.3 4.4 %collective-permute-start.8 = (bf16[64,512]{1,0:T(8,128)(2,1)S(1)}, bf16[64,512]{1,0:T(8,128)(2,1)S(1)}, u32[]{:S(2)}, u32[]{:S(2)}) collective-permute-start(bf16[64,512]{1,0:T(8,128)(2,1)S(1)} %collective-permute-done.7.skew_ref.skew), channel_id=1, source_target_pairs={{0,8},{4,12},{8,0},{12,4},{16,24},{20,28},{24,16},{28,20},{32,40},... | collective-permute-start | bytes 196616 | tf_op jit(solution)/shard_map/ppermute | solution.py:22
  46.6 1.6 %collective-permute-done.8.skew_across_ref.skew_across = bf16[64,512]{1,0:T(8,128)(2,1)S(1)} collective-permute-done((bf16[64,512]{1,0:T(8,128)(2,1)S(1)}, bf16[64,512]{1,0:T(8,128)(2,1)S(1)}, u32[]{:S(2)}, u32[]{:S(2)}) %collective-permute-start.8) | collective-permute-done | bytes 65568 | tf_op jit(solution)/shard_map/ppermute | solution.py:22
  48.3 5.4 %collective-permute-start.4 = (bf16[512,512]{1,0:T(8,128)(2,1)S(1)}, bf16[512,512]{1,0:T(8,128)(2,1)S(1)}, u32[]{:S(2)}, u32[]{:S(2)}) collective-permute-start(bf16[512,512]{1,0:T(8,128)(2,1)S(1)} %shard_map.47), channel_id=1, source_target_pairs={{16,0},{20,4},{24,8},{28,12},{32,16},{36,20},{40,24},{44,28},{48,3... | collective-permute-start | bytes 1572872 | tf_op jit(solution)/shard_map/ppermute | solution.py:22
  57.1 10.4 %collective-permute-start.13 = (bf16[512,512]{1,0:T(8,128)(2,1)}, bf16[512,512]{1,0:T(8,128)(2,1)}, u32[]{:S(2)}, u32[]{:S(2)}) collective-permute-start(bf16[512,512]{1,0:T(8,128)(2,1)} %get-tuple-element.18), channel_id=1, source_target_pairs={{16,12},{32,28},{48,44},{64,60},{80,76},{96,92},{112,108},{128,124... | collective-permute-start | bytes 1572872 | tf_op jit(solution)/shard_map/ppermute | solution.py:22
  67.5 1.9 %collective-permute-start.9 = (bf16[384,512]{1,0:T(8,128)(2,1)S(1)}, bf16[384,512]{1,0:T(8,128)(2,1)S(1)}, u32[]{:S(2)}, u32[]{:S(2)}) collective-permute-start(bf16[384,512]{1,0:T(8,128)(2,1)S(1)} %hand.1), channel_id=1, source_target_pairs={{0,4},{4,0},{8,12},{12,8},{16,20},{20,16},{24,28},{28,24},{32,36},... | collective-permute-start | bytes 1179656 | tf_op jit(solution)/shard_map/ppermute | solution.py:22
  69.9 1.9 %collective-permute-start.5 = (bf16[256,512]{1,0:T(8,128)(2,1)S(1)}, bf16[256,512]{1,0:T(8,128)(2,1)}, u32[]{:S(2)}, u32[]{:S(2)}) collective-permute-start(bf16[256,512]{1,0:T(8,128)(2,1)S(1)} %shard_map.48.near_low), channel_id=1, source_target_pairs={{0,16},{4,20},{8,24},{12,28},{16,32},{20,36},{24,40},{28,44},{32,4... | collective-permute-start | bytes 786440 | tf_op jit(solution)/shard_map/ppermute | solution.py:22
  71.8 7.6 %collective-permute-done.12.refs_3_ = bf16[512,512]{1,0:T(8,128)(2,1)} collective-permute-done((bf16[512,512]{1,0:T(8,128)(2,1)}, bf16[512,512]{1,0:T(8,128)(2,1)}, u32[]{:S(2)}, u32[]{:S(2)}) %collective-permute-start.12) | collective-permute-done | bytes 524320 | tf_op jit(solution)/shard_map/ppermute | solution.py:22
  79.5 2.6 %collective-permute-start.6 = (bf16[256,512]{1,0:T(8,128)(2,1)S(1)}, bf16[256,512]{1,0:T(8,128)(2,1)}, u32[]{:S(2)}, u32[]{:S(2)}) collective-permute-start(bf16[256,512]{1,0:T(8,128)(2,1)S(1)} %shard_map.49.near_high), channel_id=1, source_target_pairs={{16,0},{20,4},{24,8},{28,12},{32,16},{36,20},{40,24},{44,28},{48,3... | collective-permute-start | bytes 786440 | tf_op jit(solution)/shard_map/ppermute | solution.py:22
  83.3 4.3 %shard_map.50 = (f32[256,512]{1,0:T(8,128)S(1)}, f32[256,512]{1,0:T(8,128)S(1)}, f32[256,512]{1,0:T(8,128)S(1)}) custom-call(s32[15]{0:T(128)S(1)} %convert_element_type.10.flags, bf16[256,512]{1,0:T(8,128)(2,1)S(1)} %copy-done.5, bf16[256,512]{1,0:T(8,128)(2,1)S(1)} %copy-done.1, bf16[256,512]{1,0:T(8,128)(2,1)S(1)} %copy-done.2, ...), custom_call_target="tpu_custom_call" | custom-call | flops 2000000000 | bytes 6000000 | tf_op jit(solution)/shard_map/pallas_call | solution.py:273
  87.6 2.3 %collective-permute-done.9.refs_0_ = bf16[384,512]{1,0:T(8,128)(2,1)S(1)} collective-permute-done((bf16[384,512]{1,0:T(8,128)(2,1)S(1)}, bf16[384,512]{1,0:T(8,128)(2,1)S(1)}, u32[]{:S(2)}, u32[]{:S(2)}) %collective-permute-start.9) | collective-permute-done | bytes 393248 | tf_op jit(solution)/shard_map/ppermute | solution.py:22
  89.9 6.5 %shard_map.51.a_ref = bf16[256,512]{1,0:T(8,128)(2,1)S(1)} custom-call(s32[15]{0:T(128)S(1)} %convert_element_type.10.flags, bf16[256,512]{1,0:T(8,128)(2,1)S(1)} %copy-done.6, f32[256,512]{1,0:T(8,128)S(1)} %get-tuple-element.14.sum_ref, f32[256,512]{1,0:T(8,128)S(1)} %get-tuple-element.15.weight_ref, f32[256,512]{1,0:T(8,128)S(1)} %get-tuple-element.16.top_ref, ...), custom_call_target="tpu_custom_call" | custom-call | flops 2000000000 | bytes 6000000 | tf_op jit(solution)/shard_map/pallas_call | solution.py:273
  96.4 6.5 %collective-permute-start.14 = (bf16[256,512]{1,0:T(8,128)(2,1)S(1)}, bf16[256,512]{1,0:T(8,128)(2,1)S(1)}, u32[]{:S(2)}, u32[]{:S(2)}) collective-permute-start(bf16[256,512]{1,0:T(8,128)(2,1)S(1)} %shard_map.51.a_ref), channel_id=1, source_target_pairs={{0,1},{1,0},{2,3},{3,2},{4,5},{5,4},{6,7},{7,6},{8,9},{9,8},{10,11... | collective-permute-start | bytes 786440 | tf_op jit(solution)/shard_map/ppermute | solution.py:27
  105.6 5.9 %collective-permute-start.16 = (bf16[256,512]{1,0:T(8,128)(2,1)S(1)}, bf16[256,512]{1,0:T(8,128)(2,1)S(1)}, u32[]{:S(2)}, u32[]{:S(2)}) collective-permute-start(bf16[256,512]{1,0:T(8,128)(2,1)S(1)} %shard_map.53), channel_id=1, source_target_pairs={{0,2},{1,3},{2,0},{3,1},{4,6},{5,7},{6,4},{7,5},{8,10},{9,11},{10,... | collective-permute-start | bytes 786440 | tf_op jit(solution)/shard_map/ppermute | solution.py:27
  111.4 1.5 %shard_map.52 = f32[256,512]{1,0:T(8,128)S(1)} custom-call(s32[1]{0:T(128)} %bitcast.column, bf16[256,512]{1,0:T(8,128)(2,1)S(1)} %shard_map.51.a_ref, bf16[256,512]{1,0:T(8,128)(2,1)S(1)} %collective-permute-done.14.b_ref, bf16[512,2048]{1,0:T(8,128)(2,1)S(1)} %copy-done, bf16[512,2048]{1,0:T(8,128)(2,1)} %collective-permute-done.15.wb_ref), custom_call_target="tpu_custom_call" | custom-call | flops 1000000000 | bytes 1000000 | tf_op jit(solution)/shard_map/pallas_call | solution.py:318
  112.9 11.8 %collective-permute-done.16 = bf16[256,512]{1,0:T(8,128)(2,1)S(1)} collective-permute-done((bf16[256,512]{1,0:T(8,128)(2,1)S(1)}, bf16[256,512]{1,0:T(8,128)(2,1)S(1)}, u32[]{:S(2)}, u32[]{:S(2)}) %collective-permute-start.16) | collective-permute-done | bytes 262176 | tf_op jit(solution)/shard_map/ppermute | solution.py:27
  (37 shorter events, 8.6 us)
Async XLA Ops:
  0.0 104.0 %collective-permute-start.15 = (bf16[512,2048]{1,0:T(8,128)(2,1)}, bf16[512,2048]{1,0:T(8,128)(2,1)}, u32[]{:S(2)}, u32[]{:S(2)}) collective-permute-start(bf16[512,2048]{1,0:T(8,128)(2,1)} %wa_ref.3), channel_id=1, source_target_pairs={{0,1},{1,0},{2,3},{3,2},{4,5},{5,4},{6,7},{7,6},{8,9},{9,8},{10,11... | collective-permute-start | bytes 6291464 | tf_op jit(solution)/shard_map/ppermute | solution.py:27
  4.5 16.2 %collective-permute-start = (bf16[256,512]{1,0:T(8,128)(2,1)S(1)}, bf16[256,512]{1,0:T(8,128)(2,1)S(1)}, u32[]{:S(2)}, u32[]{:S(2)}) collective-permute-start(bf16[256,512]{1,0:T(8,128)(2,1)S(1)} %get-tuple-element.12), channel_id=1, source_target_pairs={{0,8},{4,12},{8,0},{12,4},{16,24},{20,28},{24,16},{28,20},{32,40},... | collective-permute-start | bytes 786440 | tf_op jit(solution)/shard_map/ppermute | solution.py:22
  20.7 61.5 %copy-start.1 = (bf16[256,512]{1,0:T(8,128)(2,1)S(1)}, bf16[256,512]{1,0:T(8,128)(2,1)}, u32[]{:S(2)}) copy-start(bf16[256,512]{1,0:T(8,128)(2,1)} %k_ref.3) | copy-start | bytes 786436
  20.8 61.6 %copy-start.2 = (bf16[256,512]{1,0:T(8,128)(2,1)S(1)}, bf16[256,512]{1,0:T(8,128)(2,1)}, u32[]{:S(2)}) copy-start(bf16[256,512]{1,0:T(8,128)(2,1)} %v_ref.3) | copy-start | bytes 786436
  20.9 19.4 %collective-permute-start.2 = (bf16[256,512]{1,0:T(8,128)(2,1)S(1)}, bf16[256,512]{1,0:T(8,128)(2,1)S(1)}, u32[]{:S(2)}, u32[]{:S(2)}) collective-permute-start(bf16[256,512]{1,0:T(8,128)(2,1)S(1)} %shard_map.46.a_ref), channel_id=1, source_target_pairs={{0,4},{4,0},{8,12},{12,8},{16,20},{20,16},{24,28},{28,24},{32,36},... | collective-permute-start | bytes 786440 | tf_op jit(solution)/shard_map/ppermute | solution.py:22
  23.7 31.3 %collective-permute-start.10 = (bf16[512,512]{1,0:T(8,128)(2,1)}, bf16[512,512]{1,0:T(8,128)(2,1)S(1)}, u32[]{:S(2)}, u32[]{:S(2)}) collective-permute-start(bf16[512,512]{1,0:T(8,128)(2,1)} %get-tuple-element.18), channel_id=1, source_target_pairs={{0,4},{4,8},{8,12},{16,20},{20,24},{24,28},{32,36},{36,40},{40,44}... | collective-permute-start | bytes 1572872 | tf_op jit(solution)/shard_map/ppermute | solution.py:22
  26.3 16.0 %collective-permute-start.7 = (bf16[64,512]{1,0:T(8,128)(2,1)S(1)}, bf16[64,512]{1,0:T(8,128)(2,1)S(1)}, u32[]{:S(2)}, u32[]{:S(2)}) collective-permute-start(bf16[64,512]{1,0:T(8,128)(2,1)S(1)} %get-tuple-element.17), channel_id=1, source_target_pairs={{0,48},{4,52},{8,56},{12,60},{32,80},{36,84},{40,88},{44,92},{48,0... | collective-permute-start | bytes 196616 | tf_op jit(solution)/shard_map/ppermute | solution.py:22
  33.9 19.8 %collective-permute-start.1 = (bf16[256,512]{1,0:T(8,128)(2,1)S(1)}, bf16[256,512]{1,0:T(8,128)(2,1)S(1)}, u32[]{:S(2)}, u32[]{:S(2)}) collective-permute-start(bf16[256,512]{1,0:T(8,128)(2,1)S(1)} %collective-permute-done.one_ref.across.across_ref), channel_id=1, source_target_pairs={{0,16},{4,20},{16,32},{20,36},{24,8},{28,12},{32,48},{36,52},{40,2... | collective-permute-start | bytes 786440 | tf_op jit(solution)/shard_map/ppermute | solution.py:22
  40.3 16.7 %collective-permute-start.3 = (bf16[512,512]{1,0:T(8,128)(2,1)S(1)}, bf16[512,512]{1,0:T(8,128)(2,1)S(1)}, u32[]{:S(2)}, u32[]{:S(2)}) collective-permute-start(bf16[512,512]{1,0:T(8,128)(2,1)S(1)} %shard_map.47), channel_id=1, source_target_pairs={{0,16},{4,20},{8,24},{12,28},{16,32},{20,36},{24,40},{28,44},{32,4... | collective-permute-start | bytes 1572872 | tf_op jit(solution)/shard_map/ppermute | solution.py:22
  42.3 6.0 %collective-permute-start.8 = (bf16[64,512]{1,0:T(8,128)(2,1)S(1)}, bf16[64,512]{1,0:T(8,128)(2,1)S(1)}, u32[]{:S(2)}, u32[]{:S(2)}) collective-permute-start(bf16[64,512]{1,0:T(8,128)(2,1)S(1)} %collective-permute-done.7.skew_ref.skew), channel_id=1, source_target_pairs={{0,8},{4,12},{8,0},{12,4},{16,24},{20,28},{24,16},{28,20},{32,40},... | collective-permute-start | bytes 196616 | tf_op jit(solution)/shard_map/ppermute | solution.py:22
  48.3 19.2 %collective-permute-start.4 = (bf16[512,512]{1,0:T(8,128)(2,1)S(1)}, bf16[512,512]{1,0:T(8,128)(2,1)S(1)}, u32[]{:S(2)}, u32[]{:S(2)}) collective-permute-start(bf16[512,512]{1,0:T(8,128)(2,1)S(1)} %shard_map.47), channel_id=1, source_target_pairs={{16,0},{20,4},{24,8},{28,12},{32,16},{36,20},{40,24},{44,28},{48,3... | collective-permute-start | bytes 1572872 | tf_op jit(solution)/shard_map/ppermute | solution.py:22
  53.7 16.2 %collective-permute-start.11 = (bf16[512,512]{1,0:T(8,128)(2,1)}, bf16[512,512]{1,0:T(8,128)(2,1)}, u32[]{:S(2)}, u32[]{:S(2)}) collective-permute-start(bf16[512,512]{1,0:T(8,128)(2,1)} %get-tuple-element.18), channel_id=1, source_target_pairs={{4,0},{8,4},{12,8},{20,16},{24,20},{28,24},{36,32},{40,36},{44,40}... | collective-permute-start | bytes 1572872 | tf_op jit(solution)/shard_map/ppermute | solution.py:22
  55.0 0.8 copy-start.3
  55.8 23.7 %collective-permute-start.12 = (bf16[512,512]{1,0:T(8,128)(2,1)}, bf16[512,512]{1,0:T(8,128)(2,1)}, u32[]{:S(2)}, u32[]{:S(2)}) collective-permute-start(bf16[512,512]{1,0:T(8,128)(2,1)} %get-tuple-element.18), channel_id=1, source_target_pairs={{12,16},{28,32},{44,48},{60,64},{76,80},{92,96},{108,112},{124,128... | collective-permute-start | bytes 1572872 | tf_op jit(solution)/shard_map/ppermute | solution.py:22
  57.1 30.5 %collective-permute-start.13 = (bf16[512,512]{1,0:T(8,128)(2,1)}, bf16[512,512]{1,0:T(8,128)(2,1)}, u32[]{:S(2)}, u32[]{:S(2)}) collective-permute-start(bf16[512,512]{1,0:T(8,128)(2,1)} %get-tuple-element.18), channel_id=1, source_target_pairs={{16,12},{32,28},{48,44},{64,60},{80,76},{96,92},{112,108},{128,124... | collective-permute-start | bytes 1572872 | tf_op jit(solution)/shard_map/ppermute | solution.py:22
  67.5 22.4 %collective-permute-start.9 = (bf16[384,512]{1,0:T(8,128)(2,1)S(1)}, bf16[384,512]{1,0:T(8,128)(2,1)S(1)}, u32[]{:S(2)}, u32[]{:S(2)}) collective-permute-start(bf16[384,512]{1,0:T(8,128)(2,1)S(1)} %hand.1), channel_id=1, source_target_pairs={{0,4},{4,0},{8,12},{12,8},{16,20},{20,16},{24,28},{28,24},{32,36},... | collective-permute-start | bytes 1179656 | tf_op jit(solution)/shard_map/ppermute | solution.py:22
  69.9 20.0 %collective-permute-start.5 = (bf16[256,512]{1,0:T(8,128)(2,1)S(1)}, bf16[256,512]{1,0:T(8,128)(2,1)}, u32[]{:S(2)}, u32[]{:S(2)}) collective-permute-start(bf16[256,512]{1,0:T(8,128)(2,1)S(1)} %shard_map.48.near_low), channel_id=1, source_target_pairs={{0,16},{4,20},{8,24},{12,28},{16,32},{20,36},{24,40},{28,44},{32,4... | collective-permute-start | bytes 786440 | tf_op jit(solution)/shard_map/ppermute | solution.py:22
  79.5 10.4 %collective-permute-start.6 = (bf16[256,512]{1,0:T(8,128)(2,1)S(1)}, bf16[256,512]{1,0:T(8,128)(2,1)}, u32[]{:S(2)}, u32[]{:S(2)}) collective-permute-start(bf16[256,512]{1,0:T(8,128)(2,1)S(1)} %shard_map.49.near_high), channel_id=1, source_target_pairs={{16,0},{20,4},{24,8},{28,12},{32,16},{36,20},{40,24},{44,28},{48,3... | collective-permute-start | bytes 786440 | tf_op jit(solution)/shard_map/ppermute | solution.py:22
  82.3 1.0 copy-start.5
  83.3 6.6 %copy-start.4 = (bf16[512,512]{1,0:T(8,128)(2,1)S(1)}, bf16[512,512]{1,0:T(8,128)(2,1)}, u32[]{:S(2)}) copy-start(bf16[512,512]{1,0:T(8,128)(2,1)} %copy-done.3) | copy-start | bytes 1572868
  83.3 6.6 %copy-start.6 = (bf16[256,512]{1,0:T(8,128)(2,1)S(1)}, bf16[256,512]{1,0:T(8,128)(2,1)}, u32[]{:S(2)}) copy-start(bf16[256,512]{1,0:T(8,128)(2,1)} %q_ref.3) | copy-start | bytes 786436
  89.9 14.1 %copy-start = (bf16[512,2048]{1,0:T(8,128)(2,1)S(1)}, bf16[512,2048]{1,0:T(8,128)(2,1)}, u32[]{:S(2)}) copy-start(bf16[512,2048]{1,0:T(8,128)(2,1)} %wa_ref.3) | copy-start | bytes 6291460
  96.4 7.6 %collective-permute-start.14 = (bf16[256,512]{1,0:T(8,128)(2,1)S(1)}, bf16[256,512]{1,0:T(8,128)(2,1)S(1)}, u32[]{:S(2)}, u32[]{:S(2)}) collective-permute-start(bf16[256,512]{1,0:T(8,128)(2,1)S(1)} %shard_map.51.a_ref), channel_id=1, source_target_pairs={{0,1},{1,0},{2,3},{3,2},{4,5},{5,4},{6,7},{7,6},{8,9},{9,8},{10,11... | collective-permute-start | bytes 786440 | tf_op jit(solution)/shard_map/ppermute | solution.py:27
  105.6 19.2 %collective-permute-start.16 = (bf16[256,512]{1,0:T(8,128)(2,1)S(1)}, bf16[256,512]{1,0:T(8,128)(2,1)S(1)}, u32[]{:S(2)}, u32[]{:S(2)}) collective-permute-start(bf16[256,512]{1,0:T(8,128)(2,1)S(1)} %shard_map.53), channel_id=1, source_target_pairs={{0,2},{1,3},{2,0},{3,1},{4,6},{5,7},{6,4},{7,5},{8,10},{9,11},{10,... | collective-permute-start | bytes 786440 | tf_op jit(solution)/shard_map/ppermute | solution.py:27

commit v6 on v4

--- a/solution.py
+++ b/solution.py
@@ -136,21 +136,33 @@
 
 
 def main_kernel(flags, q_ref, *refs):
-    k_ref, v_ref = refs[0:2]
     across, far = refs[4:6]
     twos = refs[7:9]
     skews = refs[9:11]
     nears = refs[11:13]
-    sum_ref, weight_ref, top_ref = refs[13:16]
-    scores, weights, values, left, right, third, arrived = refs[16:23]
+    wraps = refs[13:15]
+    sum_ref, weight_ref, top_ref = refs[15:18]
+    scores, weights, values, left, right, third, k_ref, v_ref, arrived = refs[18:27]
     copies = [
         pltpu.make_async_copy(source, target, arrived.at[index])
         for index, (source, target) in enumerate(
-            ((refs[2], left), (refs[3], right), (refs[6], third))
+            (
+                (refs[2], left),
+                (refs[3], right),
+                (refs[6], third),
+                (refs[0], k_ref),
+                (refs[1], v_ref),
+            )
         )
     ]
-    for copy in copies:
+    for copy in copies[2:]:
         copy.start()
+    for index, flag in ((0, 13), (1, 14)):
+        wrapped = pltpu.make_async_copy(
+            wraps[index], (left, right)[index], arrived.at[index]
+        )
+
+        lax.cond(flags[flag] > 0, wrapped.start, copies[index].start)
 
     rows = q_ref.shape[0]
     even = flags[6] > 0
@@ -189,7 +201,6 @@
                 largest = piece if largest is None else jnp.maximum(largest, piece)
             spans.append((start, count, level))
 
-        take(rows_of(k_ref, 0, 256), rows_of(v_ref, 0, 256), 0, None)
         for index, ref in enumerate(twos):
             take(rows_of(ref, 0, 256), rows_of(ref, 256, 256), 2, 3 + index)
         near = [either(even, nears[0], nears[1], part * 128, 128) for part in range(2)]
@@ -199,6 +210,7 @@
         if head == 0:
             for copy in copies:
                 copy.wait()
+        take(rows_of(k_ref, 0, 256), rows_of(v_ref, 0, 256), 0, None)
         take(rows_of(third, 0, 128), rows_of(third, 128, 128), 1, 11)
         skew = [
             jnp.concatenate(
@@ -277,9 +289,9 @@
         pltpu.VMEM((2, rows, KEYS), jnp.bfloat16),
         pltpu.VMEM((2, KEYS, 2 * HEAD_DIM), jnp.bfloat16),
     ]
-    away = (3, 4, 7)
-    scratch += [pltpu.VMEM(tensors[i].shape, jnp.bfloat16) for i in away]
-    scratch.append(pltpu.SemaphoreType.DMA((len(away),)))
+    landed, away = (3, 4, 7, 1, 2), (3, 4, 7, 1, 2, 14, 15)
+    scratch += [pltpu.VMEM(tensors[i].shape, jnp.bfloat16) for i in landed]
+    scratch.append(pltpu.SemaphoreType.DMA((len(landed),)))
     return heads_call(main_kernel, flags, tensors, outs, scratch, 32, 3 * 10**9, away)
 
 
@@ -290,27 +302,50 @@
     return heads_call(late_kernel, flags, tensors, outs, scratch, 16, 3 * 10**8)
 
 
-def project_kernel(column, a_ref, b_ref, wa_ref, wb_ref, out_ref):
-    total = dot(a_ref[...], wa_ref[...]) + dot(b_ref[...], wb_ref[...])
-    out_ref[...] = total.astype(out_ref.dtype)
-
-
-def project(column, own, peer, own_weight, peer_weight, dtype):
-    rows, width = own.shape
-    block = pl.BlockSpec((rows, width), lambda i, c: (0, 0))
-    weight = pl.BlockSpec((width, width), lambda i, c: (0, c[0]))
-    return pl.pallas_call(
-        project_kernel,
+def pick_kernel(columns, own_ref, peer_ref, out_ref):
+    out_ref[:512] = own_ref[...]
+    out_ref[512:] = peer_ref[...]
+
+
+def pick(columns, own_weight, peer_weight):
+    rows = own_weight.shape[0]
+    source = pl.BlockSpec((rows, rows), lambda i, c: (0, c[i]))
+    return pl.pallas_call(
+        pick_kernel,
         grid_spec=pltpu.PrefetchScalarGridSpec(
             num_scalar_prefetch=1,
-            grid=(1,),
-            in_specs=[block, block, weight, weight],
-            out_specs=block,
+            grid=(2,),
+            in_specs=[source, source],
+            out_specs=pl.BlockSpec((2 * rows, rows), lambda i, c: (i, 0)),
         ),
-        out_shape=jax.ShapeDtypeStruct((rows, width), dtype),
+        out_shape=jax.ShapeDtypeStruct((4 * rows, rows), own_weight.dtype),
         compiler_params=pltpu.CompilerParams(vmem_limit_bytes=12 * MIB),
-        cost_estimate=pl.CostEstimate(flops=10**9, bytes_accessed=10**6, transcendentals=0),
-    )(column, own, peer, own_weight, peer_weight)
+        cost_estimate=pl.CostEstimate(flops=10**8, bytes_accessed=10**6, transcendentals=0),
+        name="pick",
+    )(columns, *in_hbm((own_weight, peer_weight)))
+
+
+def own_kernel(own_ref, weight_ref, out_ref):
+    out_ref[...] = dot(own_ref[...], weight_ref[:512])
+
+
+def away_kernel(part_ref, peer_ref, weight_ref, out_ref):
+    out_ref[...] = (part_ref[...] + dot(peer_ref[...], weight_ref[512:1024])).astype(jnp.bfloat16)
+
+
+def here_kernel(own_ref, peer_ref, weight_ref, out_ref):
+    out_ref[...] = dot(own_ref[...], weight_ref[1024:1536]) + dot(
+        peer_ref[...], weight_ref[1536:]
+    )
+
+
+def project(kernel, operands, dtype):
+    return pl.pallas_call(
+        kernel,
+        out_shape=jax.ShapeDtypeStruct(operands[0].shape, dtype),
+        compiler_params=pltpu.CompilerParams(vmem_limit_bytes=8 * MIB),
+        cost_estimate=pl.CostEstimate(flops=5 * 10**8, bytes_accessed=10**6, transcendentals=0),
+    )(*operands)
 
 
 def layer(queries, key_rows, value_rows, out_weight):
@@ -326,18 +361,21 @@
     across = seq_permute(own_one, lambda i: i ^ 2)
     skew = seq_permute(own_three, lambda i: i + 12 if i // 4 % 2 == 0 else i - 12)
     peer_weight = head_permute(out_weight, 1)
+    weights = pick(jnp.stack([head ^ 2, head]), out_weight, peer_weight)
     two_half = small(half_kernel, own_two, across)
     two_beside = seq_permute(two_half, lambda i: i ^ 1)
     skew_across = seq_permute(skew, lambda i: i ^ 2)
     far = seq_permute(across, lambda i: i + 4 if i % 4 < 2 else i - 4)
-    left = seq_permute(raw, lambda i: i + 1)
-    right = seq_permute(raw, lambda i: i - 1)
+    left = seq_permute(raw, lambda i: i + 1 if i % 4 < 3 else -1)
+    right = seq_permute(raw, lambda i: i - 1 if i % 4 > 0 else -1)
     two_block = small(pack_kernel, two_half, two_beside, rows=(512,))
     two_low = seq_permute(two_block, lambda i: i + 4)
     two_high = seq_permute(two_block, lambda i: i - 4)
     outer = (spot == 0) | (spot == 3)
     handed = hand(outer.astype(jnp.int32).reshape(1), far, across, skew, skew_across)
     third = seq_permute(handed, lambda i: i ^ 1)
+    left_wrap = seq_permute(raw, lambda i: i + 1 if i % 4 == 3 else -1)
+    right_wrap = seq_permute(raw, lambda i: i - 1 if i % 4 == 0 else -1)
     near_low = small(halve_kernel, two_low)
     near_high = small(halve_kernel, two_high)
     three_low = seq_permute(near_low, lambda i: i + 4)
@@ -359,18 +397,20 @@
             far_ok,
             outer | far_ok,
             jnp.logical_not(outer) | far_ok,
+            spot == 0,
+            spot == 3,
         ]
     ).astype(jnp.int32)
-    tensors = [queries, key_rows, value_rows, left, right, across, far, third]
+    tensors = in_hbm([queries, key_rows, value_rows]) + [left, right, across, far, third]
     tensors += [two_low, two_high, skew, skew_across, near_low, near_high]
+    tensors += [left_wrap, right_wrap]
     partial = attend_main(flags, tensors)
     attended = attend_late(flags, [queries, *partial, three_low, three_high])
     peer = head_permute(attended, 1)
-    here_column, away_column = head.reshape(1), (head ^ 2).reshape(1)
-    weights = (out_weight, peer_weight)
-    away = project(away_column, attended, peer, *weights, jnp.bfloat16)
+    part = project(own_kernel, (attended, weights), jnp.float32)
+    away = project(away_kernel, (part, peer, weights), jnp.bfloat16)
     arrived = head_permute(away, 2)
-    here = project(here_column, attended, peer, *weights, jnp.float32)
+    here = project(here_kernel, (attended, peer, weights), jnp.float32)
     return (here + arrived.astype(jnp.float32)).astype(jnp.bfloat16)
 
 

time: 140 us -> 140 us (level)
  the two profiles are of different devices: /device:TPU:55 before, /device:TPU:7 now
where the time goes in v6:
time: 140 us
  starting transfers between devices  78 us (56%)
  waiting for transfers between devices  43.4 us (31%)
  Pallas kernels  15 us (11%)
  local copies, waits for them, and re-layouts  1.94 us (1%)
    ppermute x14, starting transfers between devices, seq_permute(): return lax.ppermute(value, 'seq', pairs)  63.3 us
    ppermute x14, waiting for transfers between devices, seq_permute(): return lax.ppermute(value, 'seq', pairs)  28.9 us
    ppermute x3, starting transfers between devices, head_permute(): return lax.ppermute(value, 'head', [(i, i ^ bit) for i in range(count)])  14.7 us
    ppermute x3, waiting for transfers between devices, head_permute(): return lax.ppermute(value, 'head', [(i, i ^ bit) for i in range(count)])  14.5 us
    pallas_call x2, Pallas kernels, heads_call(): pl.pallas_call(kernel, in_specs=[pl.BlockSpec(memory_space=pltpu.SMEM)] +...  9.69 us
  transfers between devices with their start and end apart: 17, of which 7 were waited for; matrix products, arithmetic and copies ran while one was open for 0% of the time, Pallas kernels for 10%

profile of v6, /device:TPU:7, one launch (start us, length us, event | category | flops | bytes accessed | tf_op | source)
XLA Modules:
  0.0 139.6 jit_solution(11729213114423832066)
XLA Ops:
  1.4 4.2 %collective-permute-start.2 = (bf16[256,512]{1,0:T(8,128)(2,1)S(1)}, bf16[256,512]{1,0:T(8,128)(2,1)S(1)}, u32[]{:S(2)}, u32[]{:S(2)}) collective-permute-start(bf16[256,512]{1,0:T(8,128)(2,1)S(1)} %get-tuple-element.13), channel_id=1, source_target_pairs={{0,8},{4,12},{8,0},{12,4},{16,24},{20,28},{24,16},{28,20},{32,40},... | collective-permute-start | bytes 786440 | tf_op jit(solution)/shard_map/ppermute | solution.py:22
  5.6 2.9 %collective-permute-start.15 = (bf16[512,2048]{1,0:T(8,128)(2,1)}, bf16[512,2048]{1,0:T(8,128)(2,1)}, u32[]{:S(2)}, u32[]{:S(2)}) collective-permute-start(bf16[512,2048]{1,0:T(8,128)(2,1)} %own_ref.1), channel_id=1, source_target_pairs={{0,1},{1,0},{2,3},{3,2},{4,5},{5,4},{6,7},{7,6},{8,9},{9,8},{10,11... | collective-permute-start | bytes 6291464 | tf_op jit(solution)/shard_map/ppermute | solution.py:27
  8.5 8.5 %collective-permute-done.2.across_ref.one_ref.refs_4_ = bf16[256,512]{1,0:T(8,128)(2,1)S(1)} collective-permute-done((bf16[256,512]{1,0:T(8,128)(2,1)S(1)}, bf16[256,512]{1,0:T(8,128)(2,1)S(1)}, u32[]{:S(2)}, u32[]{:S(2)}) %collective-permute-start.2) | collective-permute-done | bytes 262176 | tf_op jit(solution)/shard_map/ppermute | solution.py:22
  17.2 3.3 %collective-permute-start.7 = (bf16[256,512]{1,0:T(8,128)(2,1)S(1)}, bf16[256,512]{1,0:T(8,128)(2,1)S(1)}, u32[]{:S(2)}, u32[]{:S(2)}) collective-permute-start(bf16[256,512]{1,0:T(8,128)(2,1)S(1)} %shard_map.46.a_ref), channel_id=1, source_target_pairs={{0,4},{4,0},{8,12},{12,8},{16,20},{20,16},{24,28},{28,24},{32,36},... | collective-permute-start | bytes 786440 | tf_op jit(solution)/shard_map/ppermute | solution.py:22
  20.5 2.0 %collective-permute-start = (bf16[512,512]{1,0:T(8,128)(2,1)S(1)}, bf16[512,512]{1,0:T(8,128)(2,1)S(1)}, u32[]{:S(2)}, u32[]{:S(2)}) collective-permute-start(bf16[512,512]{1,0:T(8,128)(2,1)S(1)} %get-tuple-element.12), channel_id=1, source_target_pairs={{0,4},{4,8},{8,12},{16,20},{20,24},{24,28},{32,36},{36,40},{40,44}... | collective-permute-start | bytes 1572872 | tf_op jit(solution)/shard_map/ppermute | solution.py:22
  22.5 3.1 %collective-permute-done.7.b_ref = bf16[256,512]{1,0:T(8,128)(2,1)S(1)} collective-permute-done((bf16[256,512]{1,0:T(8,128)(2,1)S(1)}, bf16[256,512]{1,0:T(8,128)(2,1)S(1)}, u32[]{:S(2)}, u32[]{:S(2)}) %collective-permute-start.7) | collective-permute-done | bytes 262176 | tf_op jit(solution)/shard_map/ppermute | solution.py:22
  25.7 4.0 %collective-permute-start.8 = (bf16[512,512]{1,0:T(8,128)(2,1)S(1)}, bf16[512,512]{1,0:T(8,128)(2,1)S(1)}, u32[]{:S(2)}, u32[]{:S(2)}) collective-permute-start(bf16[512,512]{1,0:T(8,128)(2,1)S(1)} %shard_map.47), channel_id=1, source_target_pairs={{0,16},{4,20},{8,24},{12,28},{16,32},{20,36},{24,40},{28,44},{32,4... | collective-permute-start | bytes 1572872 | tf_op jit(solution)/shard_map/ppermute | solution.py:22
  29.7 8.8 %collective-permute-start.4 = (bf16[64,512]{1,0:T(8,128)(2,1)S(1)}, bf16[64,512]{1,0:T(8,128)(2,1)S(1)}, u32[]{:S(2)}, u32[]{:S(2)}) collective-permute-start(bf16[64,512]{1,0:T(8,128)(2,1)S(1)} %get-tuple-element.14), channel_id=1, source_target_pairs={{0,48},{4,52},{8,56},{12,60},{32,80},{36,84},{40,88},{44,92},{48,0... | collective-permute-start | bytes 196616 | tf_op jit(solution)/shard_map/ppermute | solution.py:22
  38.6 3.4 %collective-permute-start.9 = (bf16[512,512]{1,0:T(8,128)(2,1)S(1)}, bf16[512,512]{1,0:T(8,128)(2,1)S(1)}, u32[]{:S(2)}, u32[]{:S(2)}) collective-permute-start(bf16[512,512]{1,0:T(8,128)(2,1)S(1)} %shard_map.47), channel_id=1, source_target_pairs={{16,0},{20,4},{24,8},{28,12},{32,16},{36,20},{40,24},{44,28},{48,3... | collective-permute-start | bytes 1572872 | tf_op jit(solution)/shard_map/ppermute | solution.py:22
  41.9 6.0 %collective-permute-start.5 = (bf16[64,512]{1,0:T(8,128)(2,1)S(1)}, bf16[64,512]{1,0:T(8,128)(2,1)S(1)}, u32[]{:S(2)}, u32[]{:S(2)}) collective-permute-start(bf16[64,512]{1,0:T(8,128)(2,1)S(1)} %collective-permute-done.4.skew_ref.refs_9_), channel_id=1, source_target_pairs={{0,8},{4,12},{8,0},{12,4},{16,24},{20,28},{24,16},{28,20},{32,40},... | collective-permute-start | bytes 196616 | tf_op jit(solution)/shard_map/ppermute | solution.py:22
  49.8 11.9 %collective-permute-start.3 = (bf16[256,512]{1,0:T(8,128)(2,1)S(1)}, bf16[256,512]{1,0:T(8,128)(2,1)S(1)}, u32[]{:S(2)}, u32[]{:S(2)}) collective-permute-start(bf16[256,512]{1,0:T(8,128)(2,1)S(1)} %collective-permute-done.2.across_ref.one_ref.refs_4_), channel_id=1, source_target_pairs={{0,16},{4,20},{16,32},{20,36},{24,8},{28,12},{32,48},{36,52},{40,2... | collective-permute-start | bytes 786440 | tf_op jit(solution)/shard_map/ppermute | solution.py:22
  61.7 3.3 %collective-permute-done.3.far_ref.refs_5_ = bf16[256,512]{1,0:T(8,128)(2,1)S(1)} collective-permute-done((bf16[256,512]{1,0:T(8,128)(2,1)S(1)}, bf16[256,512]{1,0:T(8,128)(2,1)S(1)}, u32[]{:S(2)}, u32[]{:S(2)}) %collective-permute-start.3) | collective-permute-done | bytes 262176 | tf_op jit(solution)/shard_map/ppermute | solution.py:22
  68.4 11.2 %collective-permute-start.11 = (bf16[512,512]{1,0:T(8,128)(2,1)S(1)}, bf16[512,512]{1,0:T(8,128)(2,1)}, u32[]{:S(2)}, u32[]{:S(2)}) collective-permute-start(bf16[512,512]{1,0:T(8,128)(2,1)S(1)} %get-tuple-element.12), channel_id=1, source_target_pairs={{16,12},{32,28},{48,44},{64,60},{80,76},{96,92},{112,108},{128,124... | collective-permute-start | bytes 1572872 | tf_op jit(solution)/shard_map/ppermute | solution.py:22
  79.7 1.9 %collective-permute-start.6 = (bf16[384,512]{1,0:T(8,128)(2,1)S(1)}, bf16[384,512]{1,0:T(8,128)(2,1)S(1)}, u32[]{:S(2)}, u32[]{:S(2)}) collective-permute-start(bf16[384,512]{1,0:T(8,128)(2,1)S(1)} %hand.1), channel_id=1, source_target_pairs={{0,4},{4,0},{8,12},{12,8},{16,20},{20,16},{24,28},{28,24},{32,36},... | collective-permute-start | bytes 1179656 | tf_op jit(solution)/shard_map/ppermute | solution.py:22
  82.3 2.1 %collective-permute-start.12 = (bf16[256,512]{1,0:T(8,128)(2,1)S(1)}, bf16[256,512]{1,0:T(8,128)(2,1)S(1)}, u32[]{:S(2)}, u32[]{:S(2)}) collective-permute-start(bf16[256,512]{1,0:T(8,128)(2,1)S(1)} %shard_map.48.refs_11_), channel_id=1, source_target_pairs={{0,16},{4,20},{8,24},{12,28},{16,32},{20,36},{24,40},{28,44},{32,4... | collective-permute-start | bytes 786440 | tf_op jit(solution)/shard_map/ppermute | solution.py:22
  84.3 7.3 %collective-permute-done.10.refs_13_ = bf16[512,512]{1,0:T(8,128)(2,1)} collective-permute-done((bf16[512,512]{1,0:T(8,128)(2,1)S(1)}, bf16[512,512]{1,0:T(8,128)(2,1)}, u32[]{:S(2)}, u32[]{:S(2)}) %collective-permute-start.10) | collective-permute-done | bytes 524320 | tf_op jit(solution)/shard_map/ppermute | solution.py:22
  91.6 1.9 %collective-permute-start.13 = (bf16[256,512]{1,0:T(8,128)(2,1)S(1)}, bf16[256,512]{1,0:T(8,128)(2,1)S(1)}, u32[]{:S(2)}, u32[]{:S(2)}) collective-permute-start(bf16[256,512]{1,0:T(8,128)(2,1)S(1)} %shard_map.49.refs_12_), channel_id=1, source_target_pairs={{16,0},{20,4},{24,8},{28,12},{32,16},{36,20},{40,24},{44,28},{48,3... | collective-permute-start | bytes 786440 | tf_op jit(solution)/shard_map/ppermute | solution.py:22
  93.6 4.8 %collective-permute-done.6.refs_6_ = bf16[384,512]{1,0:T(8,128)(2,1)S(1)} collective-permute-done((bf16[384,512]{1,0:T(8,128)(2,1)S(1)}, bf16[384,512]{1,0:T(8,128)(2,1)S(1)}, u32[]{:S(2)}, u32[]{:S(2)}) %collective-permute-start.6) | collective-permute-done | bytes 393248 | tf_op jit(solution)/shard_map/ppermute | solution.py:22
  99.4 7.7 %shard_map.50 = (f32[256,512]{1,0:T(8,128)S(1)}, f32[256,512]{1,0:T(8,128)S(1)}, f32[256,512]{1,0:T(8,128)S(1)}) custom-call(s32[15]{0:T(128)S(1)} %convert_element_type.10.flags, bf16[256,512]{1,0:T(8,128)(2,1)} %q_ref.3, bf16[256,512]{1,0:T(8,128)(2,1)} %refs_0_.1, bf16[256,512]{1,0:T(8,128)(2,1)} %refs_1_.1, bf16[512,512]{1,0:T(8,128)(2,1)S(1)} %copy-done.2, ...), custom_call_target="tpu_custom_call" | custom-call | flops 3000000000 | bytes 6000000 | tf_op jit(solution)/shard_map/pallas_call | solution.py:272
  107.2 2.0 %shard_map.51.own_ref = bf16[256,512]{1,0:T(8,128)(2,1)S(1)} custom-call(s32[15]{0:T(128)S(1)} %convert_element_type.10.flags, bf16[256,512]{1,0:T(8,128)(2,1)S(1)} %copy-done, f32[256,512]{1,0:T(8,128)S(1)} %get-tuple-element.16.sum_ref, f32[256,512]{1,0:T(8,128)S(1)} %get-tuple-element.17.weight_ref, f32[256,512]{1,0:T(8,128)S(1)} %get-tuple-element.18.top_ref, ...), custom_call_target="tpu_custom_call" | custom-call | flops 300000000 | bytes 6000000 | tf_op jit(solution)/shard_map/pallas_call | solution.py:272
  109.2 7.1 %collective-permute-start.14 = (bf16[256,512]{1,0:T(8,128)(2,1)S(1)}, bf16[256,512]{1,0:T(8,128)(2,1)S(1)}, u32[]{:S(2)}, u32[]{:S(2)}) collective-permute-start(bf16[256,512]{1,0:T(8,128)(2,1)S(1)} %shard_map.51.own_ref), channel_id=1, source_target_pairs={{0,1},{1,0},{2,3},{3,2},{4,5},{5,4},{6,7},{7,6},{8,9},{9,8},{10,11... | collective-permute-start | bytes 786440 | tf_op jit(solution)/shard_map/ppermute | solution.py:27
  116.4 2.2 %pick.1.weight_ref = bf16[2048,512]{1,0:T(8,128)(2,1)S(1)} custom-call(s32[2]{0:T(128)S(1)} %pad_add_fusion.columns, bf16[512,2048]{1,0:T(8,128)(2,1)} %own_ref.1, bf16[512,2048]{1,0:T(8,128)(2,1)} %collective-permute-done.15.peer_ref), custom_call_target="tpu_custom_call" | custom-call | flops 100000000 | bytes 1000000 | tf_op jit(solution)/shard_map/pick/pallas_call | solution.py:313
  119.2 4.7 %collective-permute-start.16 = (bf16[256,512]{1,0:T(8,128)(2,1)S(1)}, bf16[256,512]{1,0:T(8,128)(2,1)S(1)}, u32[]{:S(2)}, u32[]{:S(2)}) collective-permute-start(bf16[256,512]{1,0:T(8,128)(2,1)S(1)} %shard_map.54), channel_id=1, source_target_pairs={{0,2},{1,3},{2,0},{3,1},{4,6},{5,7},{6,4},{7,5},{8,10},{9,11},{10,... | collective-permute-start | bytes 786440 | tf_op jit(solution)/shard_map/ppermute | solution.py:27
  124.4 14.5 %collective-permute-done.16 = bf16[256,512]{1,0:T(8,128)(2,1)S(1)} collective-permute-done((bf16[256,512]{1,0:T(8,128)(2,1)S(1)}, bf16[256,512]{1,0:T(8,128)(2,1)S(1)}, u32[]{:S(2)}, u32[]{:S(2)}) %collective-permute-start.16) | collective-permute-done | bytes 262176 | tf_op jit(solution)/shard_map/ppermute | solution.py:27
  (32 shorter events, 10.4 us)
Async XLA Ops:
  1.4 15.6 %collective-permute-start.2 = (bf16[256,512]{1,0:T(8,128)(2,1)S(1)}, bf16[256,512]{1,0:T(8,128)(2,1)S(1)}, u32[]{:S(2)}, u32[]{:S(2)}) collective-permute-start(bf16[256,512]{1,0:T(8,128)(2,1)S(1)} %get-tuple-element.13), channel_id=1, source_target_pairs={{0,8},{4,12},{8,0},{12,4},{16,24},{20,28},{24,16},{28,20},{32,40},... | collective-permute-start | bytes 786440 | tf_op jit(solution)/shard_map/ppermute | solution.py:22
  5.6 110.8 %collective-permute-start.15 = (bf16[512,2048]{1,0:T(8,128)(2,1)}, bf16[512,2048]{1,0:T(8,128)(2,1)}, u32[]{:S(2)}, u32[]{:S(2)}) collective-permute-start(bf16[512,2048]{1,0:T(8,128)(2,1)} %own_ref.1), channel_id=1, source_target_pairs={{0,1},{1,0},{2,3},{3,2},{4,5},{5,4},{6,7},{7,6},{8,9},{9,8},{10,11... | collective-permute-start | bytes 6291464 | tf_op jit(solution)/shard_map/ppermute | solution.py:27
  17.2 8.5 %collective-permute-start.7 = (bf16[256,512]{1,0:T(8,128)(2,1)S(1)}, bf16[256,512]{1,0:T(8,128)(2,1)S(1)}, u32[]{:S(2)}, u32[]{:S(2)}) collective-permute-start(bf16[256,512]{1,0:T(8,128)(2,1)S(1)} %shard_map.46.a_ref), channel_id=1, source_target_pairs={{0,4},{4,0},{8,12},{12,8},{16,20},{20,16},{24,28},{28,24},{32,36},... | collective-permute-start | bytes 786440 | tf_op jit(solution)/shard_map/ppermute | solution.py:22
  20.5 45.8 %collective-permute-start = (bf16[512,512]{1,0:T(8,128)(2,1)S(1)}, bf16[512,512]{1,0:T(8,128)(2,1)S(1)}, u32[]{:S(2)}, u32[]{:S(2)}) collective-permute-start(bf16[512,512]{1,0:T(8,128)(2,1)S(1)} %get-tuple-element.12), channel_id=1, source_target_pairs={{0,4},{4,8},{8,12},{16,20},{20,24},{24,28},{32,36},{36,40},{40,44}... | collective-permute-start | bytes 1572872 | tf_op jit(solution)/shard_map/ppermute | solution.py:22
  25.7 42.7 %collective-permute-start.8 = (bf16[512,512]{1,0:T(8,128)(2,1)S(1)}, bf16[512,512]{1,0:T(8,128)(2,1)S(1)}, u32[]{:S(2)}, u32[]{:S(2)}) collective-permute-start(bf16[512,512]{1,0:T(8,128)(2,1)S(1)} %shard_map.47), channel_id=1, source_target_pairs={{0,16},{4,20},{8,24},{12,28},{16,32},{20,36},{24,40},{28,44},{32,4... | collective-permute-start | bytes 1572872 | tf_op jit(solution)/shard_map/ppermute | solution.py:22
  29.7 12.2 %collective-permute-start.4 = (bf16[64,512]{1,0:T(8,128)(2,1)S(1)}, bf16[64,512]{1,0:T(8,128)(2,1)S(1)}, u32[]{:S(2)}, u32[]{:S(2)}) collective-permute-start(bf16[64,512]{1,0:T(8,128)(2,1)S(1)} %get-tuple-element.14), channel_id=1, source_target_pairs={{0,48},{4,52},{8,56},{12,60},{32,80},{36,84},{40,88},{44,92},{48,0... | collective-permute-start | bytes 196616 | tf_op jit(solution)/shard_map/ppermute | solution.py:22
  38.6 41.1 %collective-permute-start.9 = (bf16[512,512]{1,0:T(8,128)(2,1)S(1)}, bf16[512,512]{1,0:T(8,128)(2,1)S(1)}, u32[]{:S(2)}, u32[]{:S(2)}) collective-permute-start(bf16[512,512]{1,0:T(8,128)(2,1)S(1)} %shard_map.47), channel_id=1, source_target_pairs={{16,0},{20,4},{24,8},{28,12},{32,16},{36,20},{40,24},{44,28},{48,3... | collective-permute-start | bytes 1572872 | tf_op jit(solution)/shard_map/ppermute | solution.py:22
  41.9 7.9 %collective-permute-start.5 = (bf16[64,512]{1,0:T(8,128)(2,1)S(1)}, bf16[64,512]{1,0:T(8,128)(2,1)S(1)}, u32[]{:S(2)}, u32[]{:S(2)}) collective-permute-start(bf16[64,512]{1,0:T(8,128)(2,1)S(1)} %collective-permute-done.4.skew_ref.refs_9_), channel_id=1, source_target_pairs={{0,8},{4,12},{8,0},{12,4},{16,24},{20,28},{24,16},{28,20},{32,40},... | collective-permute-start | bytes 196616 | tf_op jit(solution)/shard_map/ppermute | solution.py:22
  49.8 15.2 %collective-permute-start.3 = (bf16[256,512]{1,0:T(8,128)(2,1)S(1)}, bf16[256,512]{1,0:T(8,128)(2,1)S(1)}, u32[]{:S(2)}, u32[]{:S(2)}) collective-permute-start(bf16[256,512]{1,0:T(8,128)(2,1)S(1)} %collective-permute-done.2.across_ref.one_ref.refs_4_), channel_id=1, source_target_pairs={{0,16},{4,20},{16,32},{20,36},{24,8},{28,12},{32,48},{36,52},{40,2... | collective-permute-start | bytes 786440 | tf_op jit(solution)/shard_map/ppermute | solution.py:22
  65.0 17.3 %collective-permute-start.1 = (bf16[512,512]{1,0:T(8,128)(2,1)S(1)}, bf16[512,512]{1,0:T(8,128)(2,1)}, u32[]{:S(2)}, u32[]{:S(2)}) collective-permute-start(bf16[512,512]{1,0:T(8,128)(2,1)S(1)} %get-tuple-element.12), channel_id=1, source_target_pairs={{4,0},{8,4},{12,8},{20,16},{24,20},{28,24},{36,32},{40,36},{44,40}... | collective-permute-start | bytes 1572872 | tf_op jit(solution)/shard_map/ppermute | solution.py:22
  66.3 0.8 copy-start.1
  67.1 24.6 %collective-permute-start.10 = (bf16[512,512]{1,0:T(8,128)(2,1)S(1)}, bf16[512,512]{1,0:T(8,128)(2,1)}, u32[]{:S(2)}, u32[]{:S(2)}) collective-permute-start(bf16[512,512]{1,0:T(8,128)(2,1)S(1)} %get-tuple-element.12), channel_id=1, source_target_pairs={{12,16},{28,32},{44,48},{60,64},{76,80},{92,96},{108,112},{124,128... | collective-permute-start | bytes 1572872 | tf_op jit(solution)/shard_map/ppermute | solution.py:22
  68.4 25.2 %collective-permute-start.11 = (bf16[512,512]{1,0:T(8,128)(2,1)S(1)}, bf16[512,512]{1,0:T(8,128)(2,1)}, u32[]{:S(2)}, u32[]{:S(2)}) collective-permute-start(bf16[512,512]{1,0:T(8,128)(2,1)S(1)} %get-tuple-element.12), channel_id=1, source_target_pairs={{16,12},{32,28},{48,44},{64,60},{80,76},{96,92},{112,108},{128,124... | collective-permute-start | bytes 1572872 | tf_op jit(solution)/shard_map/ppermute | solution.py:22
  79.7 18.7 %collective-permute-start.6 = (bf16[384,512]{1,0:T(8,128)(2,1)S(1)}, bf16[384,512]{1,0:T(8,128)(2,1)S(1)}, u32[]{:S(2)}, u32[]{:S(2)}) collective-permute-start(bf16[384,512]{1,0:T(8,128)(2,1)S(1)} %hand.1), channel_id=1, source_target_pairs={{0,4},{4,0},{8,12},{12,8},{16,20},{20,16},{24,28},{28,24},{32,36},... | collective-permute-start | bytes 1179656 | tf_op jit(solution)/shard_map/ppermute | solution.py:22
  82.3 24.9 %copy-start = (bf16[256,512]{1,0:T(8,128)(2,1)S(1)}, bf16[256,512]{1,0:T(8,128)(2,1)}, u32[]{:S(2)}) copy-start(bf16[256,512]{1,0:T(8,128)(2,1)} %q_ref.3) | copy-start | bytes 786436
  82.3 24.8 %collective-permute-start.12 = (bf16[256,512]{1,0:T(8,128)(2,1)S(1)}, bf16[256,512]{1,0:T(8,128)(2,1)S(1)}, u32[]{:S(2)}, u32[]{:S(2)}) collective-permute-start(bf16[256,512]{1,0:T(8,128)(2,1)S(1)} %shard_map.48.refs_11_), channel_id=1, source_target_pairs={{0,16},{4,20},{8,24},{12,28},{16,32},{20,36},{24,40},{28,44},{32,4... | collective-permute-start | bytes 786440 | tf_op jit(solution)/shard_map/ppermute | solution.py:22
  91.6 15.5 %collective-permute-start.13 = (bf16[256,512]{1,0:T(8,128)(2,1)S(1)}, bf16[256,512]{1,0:T(8,128)(2,1)S(1)}, u32[]{:S(2)}, u32[]{:S(2)}) collective-permute-start(bf16[256,512]{1,0:T(8,128)(2,1)S(1)} %shard_map.49.refs_12_), channel_id=1, source_target_pairs={{16,0},{20,4},{24,8},{28,12},{32,16},{36,20},{40,24},{44,28},{48,3... | collective-permute-start | bytes 786440 | tf_op jit(solution)/shard_map/ppermute | solution.py:22
  98.4 1.0 copy-start.2
  109.2 9.7 %collective-permute-start.14 = (bf16[256,512]{1,0:T(8,128)(2,1)S(1)}, bf16[256,512]{1,0:T(8,128)(2,1)S(1)}, u32[]{:S(2)}, u32[]{:S(2)}) collective-permute-start(bf16[256,512]{1,0:T(8,128)(2,1)S(1)} %shard_map.51.own_ref), channel_id=1, source_target_pairs={{0,1},{1,0},{2,3},{3,2},{4,5},{5,4},{6,7},{7,6},{8,9},{9,8},{10,11... | collective-permute-start | bytes 786440 | tf_op jit(solution)/shard_map/ppermute | solution.py:27
  119.2 19.6 %collective-permute-start.16 = (bf16[256,512]{1,0:T(8,128)(2,1)S(1)}, bf16[256,512]{1,0:T(8,128)(2,1)S(1)}, u32[]{:S(2)}, u32[]{:S(2)}) collective-permute-start(bf16[256,512]{1,0:T(8,128)(2,1)S(1)} %shard_map.54), channel_id=1, source_target_pairs={{0,2},{1,3},{2,0},{3,1},{4,6},{5,7},{6,4},{7,5},{8,10},{9,11},{10,... | collective-permute-start | bytes 786440 | tf_op jit(solution)/shard_map/ppermute | solution.py:27

commit v7 on v4

--- a/solution.py
+++ b/solution.py
@@ -141,16 +141,22 @@
     twos = refs[7:9]
     skews = refs[9:11]
     nears = refs[11:13]
-    sum_ref, weight_ref, top_ref = refs[13:16]
-    scores, weights, values, left, right, third, arrived = refs[16:23]
+    wraps = refs[13:15]
+    sum_ref, weight_ref, top_ref = refs[15:18]
+    scores, weights, values, left, right, third, arrived = refs[18:25]
     copies = [
         pltpu.make_async_copy(source, target, arrived.at[index])
         for index, (source, target) in enumerate(
             ((refs[2], left), (refs[3], right), (refs[6], third))
         )
     ]
-    for copy in copies:
-        copy.start()
+    copies[2].start()
+    for index, flag in ((0, 13), (1, 14)):
+        wrapped = pltpu.make_async_copy(
+            wraps[index], (left, right)[index], arrived.at[index]
+        )
+
+        lax.cond(flags[flag] > 0, wrapped.start, copies[index].start)
 
     rows = q_ref.shape[0]
     even = flags[6] > 0
@@ -277,9 +283,9 @@
         pltpu.VMEM((2, rows, KEYS), jnp.bfloat16),
         pltpu.VMEM((2, KEYS, 2 * HEAD_DIM), jnp.bfloat16),
     ]
-    away = (3, 4, 7)
-    scratch += [pltpu.VMEM(tensors[i].shape, jnp.bfloat16) for i in away]
-    scratch.append(pltpu.SemaphoreType.DMA((len(away),)))
+    landed, away = (3, 4, 7), (3, 4, 7, 14, 15)
+    scratch += [pltpu.VMEM(tensors[i].shape, jnp.bfloat16) for i in landed]
+    scratch.append(pltpu.SemaphoreType.DMA((len(landed),)))
     return heads_call(main_kernel, flags, tensors, outs, scratch, 32, 3 * 10**9, away)
 
 
@@ -330,14 +336,16 @@
     two_beside = seq_permute(two_half, lambda i: i ^ 1)
     skew_across = seq_permute(skew, lambda i: i ^ 2)
     far = seq_permute(across, lambda i: i + 4 if i % 4 < 2 else i - 4)
-    left = seq_permute(raw, lambda i: i + 1)
-    right = seq_permute(raw, lambda i: i - 1)
+    left = seq_permute(raw, lambda i: i + 1 if i % 4 < 3 else -1)
+    right = seq_permute(raw, lambda i: i - 1 if i % 4 > 0 else -1)
     two_block = small(pack_kernel, two_half, two_beside, rows=(512,))
     two_low = seq_permute(two_block, lambda i: i + 4)
     two_high = seq_permute(two_block, lambda i: i - 4)
     outer = (spot == 0) | (spot == 3)
     handed = hand(outer.astype(jnp.int32).reshape(1), far, across, skew, skew_across)
     third = seq_permute(handed, lambda i: i ^ 1)
+    left_wrap = seq_permute(raw, lambda i: i + 1 if i % 4 == 3 else -1)
+    right_wrap = seq_permute(raw, lambda i: i - 1 if i % 4 == 0 else -1)
     near_low = small(halve_kernel, two_low)
     near_high = small(halve_kernel, two_high)
     three_low = seq_permute(near_low, lambda i: i + 4)
@@ -359,10 +367,13 @@
             far_ok,
             outer | far_ok,
             jnp.logical_not(outer) | far_ok,
+            spot == 0,
+            spot == 3,
         ]
     ).astype(jnp.int32)
     tensors = [queries, key_rows, value_rows, left, right, across, far, third]
     tensors += [two_low, two_high, skew, skew_across, near_low, near_high]
+    tensors += [left_wrap, right_wrap]
     partial = attend_main(flags, tensors)
     attended = attend_late(flags, [queries, *partial, three_low, three_high])
     peer = head_permute(attended, 1)

time: 140 us -> 140 us (level)
  the two profiles are of different devices: /device:TPU:55 before, /device:TPU:7 now
where the time goes in v7:
time: 140 us; the launch traced here: 139 us
  starting transfers between devices  78.9 us (56%)
  waiting for transfers between devices  42.7 us (30%)
  Pallas kernels  14.4 us (10%)
  local copies, waits for them, and re-layouts  1.96 us (1%)
    ppermute x14, starting transfers between devices, seq_permute(): return lax.ppermute(value, 'seq', pairs)  63.3 us
    ppermute x14, waiting for transfers between devices, seq_permute(): return lax.ppermute(value, 'seq', pairs)  28.4 us
    ppermute x3, starting transfers between devices, head_permute(): return lax.ppermute(value, 'head', [(i, i ^ bit) for i in range(count)])  15.6 us
    ppermute x3, waiting for transfers between devices, head_permute(): return lax.ppermute(value, 'head', [(i, i ^ bit) for i in range(count)])  14.4 us
    pallas_call x2, Pallas kernels, heads_call(): pl.pallas_call(kernel, in_specs=[pl.BlockSpec(memory_space=pltpu.SMEM)] +...  8.75 us
    pallas_call x2, Pallas kernels, project(): pl.pallas_call(project_kernel, grid_spec=pltpu.PrefetchScalarGridSpec(num...  3.03 us
  transfers between devices with their start and end apart: 17, of which 8 were waited for; matrix products, arithmetic and copies ran while one was open for 0% of the time, Pallas kernels for 8%

profile of v7, /device:TPU:7, one launch (start us, length us, event | category | flops | bytes accessed | tf_op | source)
XLA Modules:
  0.0 139.2 jit_solution(9818323736346149284)
XLA Ops:
  0.0 1.9 %coarse.1 = (bf16[512,512]{1,0:T(8,128)(2,1)}, bf16[256,512]{1,0:T(8,128)(2,1)S(1)}, bf16[128,512]{1,0:T(8,128)(2,1)S(1)}, bf16[64,512]{1,0:T(8,128)(2,1)S(1)}) custom-call(bf16[256,512]{1,0:T(8,128)(2,1)} %refs_0_.1, bf16[256,512]{1,0:T(8,128)(2,1)} %refs_1_.1), custom_call_target="tpu_custom_call" | custom-call | flops 100000000 | bytes 1000000 | tf_op jit(solution)/shard_map/coarse/pallas_call | solution.py:62
  1.9 4.2 %collective-permute-start.2 = (bf16[256,512]{1,0:T(8,128)(2,1)S(1)}, bf16[256,512]{1,0:T(8,128)(2,1)S(1)}, u32[]{:S(2)}, u32[]{:S(2)}) collective-permute-start(bf16[256,512]{1,0:T(8,128)(2,1)S(1)} %get-tuple-element.13), channel_id=1, source_target_pairs={{0,8},{4,12},{8,0},{12,4},{16,24},{20,28},{24,16},{28,20},{32,40},... | collective-permute-start | bytes 786440 | tf_op jit(solution)/shard_map/ppermute | solution.py:22
  6.1 2.9 %collective-permute-start.15 = (bf16[512,2048]{1,0:T(8,128)(2,1)}, bf16[512,2048]{1,0:T(8,128)(2,1)}, u32[]{:S(2)}, u32[]{:S(2)}) collective-permute-start(bf16[512,2048]{1,0:T(8,128)(2,1)} %wa_ref.3), channel_id=1, source_target_pairs={{0,1},{1,0},{2,3},{3,2},{4,5},{5,4},{6,7},{7,6},{8,9},{9,8},{10,11... | collective-permute-start | bytes 6291464 | tf_op jit(solution)/shard_map/ppermute | solution.py:27
  9.0 8.5 %collective-permute-done.2.across_ref.one_ref.refs_4_ = bf16[256,512]{1,0:T(8,128)(2,1)S(1)} collective-permute-done((bf16[256,512]{1,0:T(8,128)(2,1)S(1)}, bf16[256,512]{1,0:T(8,128)(2,1)S(1)}, u32[]{:S(2)}, u32[]{:S(2)}) %collective-permute-start.2) | collective-permute-done | bytes 262176 | tf_op jit(solution)/shard_map/ppermute | solution.py:22
  17.7 3.4 %collective-permute-start.7 = (bf16[256,512]{1,0:T(8,128)(2,1)S(1)}, bf16[256,512]{1,0:T(8,128)(2,1)S(1)}, u32[]{:S(2)}, u32[]{:S(2)}) collective-permute-start(bf16[256,512]{1,0:T(8,128)(2,1)S(1)} %shard_map.46.a_ref), channel_id=1, source_target_pairs={{0,4},{4,0},{8,12},{12,8},{16,20},{20,16},{24,28},{28,24},{32,36},... | collective-permute-start | bytes 786440 | tf_op jit(solution)/shard_map/ppermute | solution.py:22
  21.2 2.0 %collective-permute-start = (bf16[512,512]{1,0:T(8,128)(2,1)}, bf16[512,512]{1,0:T(8,128)(2,1)S(1)}, u32[]{:S(2)}, u32[]{:S(2)}) collective-permute-start(bf16[512,512]{1,0:T(8,128)(2,1)} %get-tuple-element.12), channel_id=1, source_target_pairs={{0,4},{4,8},{8,12},{16,20},{20,24},{24,28},{32,36},{36,40},{40,44}... | collective-permute-start | bytes 1572872 | tf_op jit(solution)/shard_map/ppermute | solution.py:22
  23.2 3.1 %collective-permute-done.7.b_ref = bf16[256,512]{1,0:T(8,128)(2,1)S(1)} collective-permute-done((bf16[256,512]{1,0:T(8,128)(2,1)S(1)}, bf16[256,512]{1,0:T(8,128)(2,1)S(1)}, u32[]{:S(2)}, u32[]{:S(2)}) %collective-permute-start.7) | collective-permute-done | bytes 262176 | tf_op jit(solution)/shard_map/ppermute | solution.py:22
  26.4 4.0 %collective-permute-start.8 = (bf16[512,512]{1,0:T(8,128)(2,1)S(1)}, bf16[512,512]{1,0:T(8,128)(2,1)S(1)}, u32[]{:S(2)}, u32[]{:S(2)}) collective-permute-start(bf16[512,512]{1,0:T(8,128)(2,1)S(1)} %shard_map.47), channel_id=1, source_target_pairs={{0,16},{4,20},{8,24},{12,28},{16,32},{20,36},{24,40},{28,44},{32,4... | collective-permute-start | bytes 1572872 | tf_op jit(solution)/shard_map/ppermute | solution.py:22
  30.4 8.8 %collective-permute-start.4 = (bf16[64,512]{1,0:T(8,128)(2,1)S(1)}, bf16[64,512]{1,0:T(8,128)(2,1)S(1)}, u32[]{:S(2)}, u32[]{:S(2)}) collective-permute-start(bf16[64,512]{1,0:T(8,128)(2,1)S(1)} %get-tuple-element.14), channel_id=1, source_target_pairs={{0,48},{4,52},{8,56},{12,60},{32,80},{36,84},{40,88},{44,92},{48,0... | collective-permute-start | bytes 196616 | tf_op jit(solution)/shard_map/ppermute | solution.py:22
  39.2 3.4 %collective-permute-start.9 = (bf16[512,512]{1,0:T(8,128)(2,1)S(1)}, bf16[512,512]{1,0:T(8,128)(2,1)S(1)}, u32[]{:S(2)}, u32[]{:S(2)}) collective-permute-start(bf16[512,512]{1,0:T(8,128)(2,1)S(1)} %shard_map.47), channel_id=1, source_target_pairs={{16,0},{20,4},{24,8},{28,12},{32,16},{36,20},{40,24},{44,28},{48,3... | collective-permute-start | bytes 1572872 | tf_op jit(solution)/shard_map/ppermute | solution.py:22
  42.6 6.0 %collective-permute-start.5 = (bf16[64,512]{1,0:T(8,128)(2,1)S(1)}, bf16[64,512]{1,0:T(8,128)(2,1)S(1)}, u32[]{:S(2)}, u32[]{:S(2)}) collective-permute-start(bf16[64,512]{1,0:T(8,128)(2,1)S(1)} %collective-permute-done.4.skew_ref.refs_9_), channel_id=1, source_target_pairs={{0,8},{4,12},{8,0},{12,4},{16,24},{20,28},{24,16},{28,20},{32,40},... | collective-permute-start | bytes 196616 | tf_op jit(solution)/shard_map/ppermute | solution.py:22
  50.5 11.9 %collective-permute-start.3 = (bf16[256,512]{1,0:T(8,128)(2,1)S(1)}, bf16[256,512]{1,0:T(8,128)(2,1)S(1)}, u32[]{:S(2)}, u32[]{:S(2)}) collective-permute-start(bf16[256,512]{1,0:T(8,128)(2,1)S(1)} %collective-permute-done.2.across_ref.one_ref.refs_4_), channel_id=1, source_target_pairs={{0,16},{4,20},{16,32},{20,36},{24,8},{28,12},{32,48},{36,52},{40,2... | collective-permute-start | bytes 786440 | tf_op jit(solution)/shard_map/ppermute | solution.py:22
  62.3 3.3 %collective-permute-done.3.far_ref.refs_5_ = bf16[256,512]{1,0:T(8,128)(2,1)S(1)} collective-permute-done((bf16[256,512]{1,0:T(8,128)(2,1)S(1)}, bf16[256,512]{1,0:T(8,128)(2,1)S(1)}, u32[]{:S(2)}, u32[]{:S(2)}) %collective-permute-start.3) | collective-permute-done | bytes 262176 | tf_op jit(solution)/shard_map/ppermute | solution.py:22
  69.0 11.3 %collective-permute-start.11 = (bf16[512,512]{1,0:T(8,128)(2,1)}, bf16[512,512]{1,0:T(8,128)(2,1)}, u32[]{:S(2)}, u32[]{:S(2)}) collective-permute-start(bf16[512,512]{1,0:T(8,128)(2,1)} %get-tuple-element.12), channel_id=1, source_target_pairs={{16,12},{32,28},{48,44},{64,60},{80,76},{96,92},{112,108},{128,124... | collective-permute-start | bytes 1572872 | tf_op jit(solution)/shard_map/ppermute | solution.py:22
  80.3 1.9 %collective-permute-start.6 = (bf16[384,512]{1,0:T(8,128)(2,1)S(1)}, bf16[384,512]{1,0:T(8,128)(2,1)S(1)}, u32[]{:S(2)}, u32[]{:S(2)}) collective-permute-start(bf16[384,512]{1,0:T(8,128)(2,1)S(1)} %hand.1), channel_id=1, source_target_pairs={{0,4},{4,0},{8,12},{12,8},{16,20},{20,16},{24,28},{28,24},{32,36},... | collective-permute-start | bytes 1179656 | tf_op jit(solution)/shard_map/ppermute | solution.py:22
  83.0 1.9 %collective-permute-start.12 = (bf16[256,512]{1,0:T(8,128)(2,1)S(1)}, bf16[256,512]{1,0:T(8,128)(2,1)S(1)}, u32[]{:S(2)}, u32[]{:S(2)}) collective-permute-start(bf16[256,512]{1,0:T(8,128)(2,1)S(1)} %shard_map.48.refs_11_), channel_id=1, source_target_pairs={{0,16},{4,20},{8,24},{12,28},{16,32},{20,36},{24,40},{28,44},{32,4... | collective-permute-start | bytes 786440 | tf_op jit(solution)/shard_map/ppermute | solution.py:22
  84.9 7.6 %collective-permute-done.10.refs_13_ = bf16[512,512]{1,0:T(8,128)(2,1)} collective-permute-done((bf16[512,512]{1,0:T(8,128)(2,1)}, bf16[512,512]{1,0:T(8,128)(2,1)}, u32[]{:S(2)}, u32[]{:S(2)}) %collective-permute-start.10) | collective-permute-done | bytes 524320 | tf_op jit(solution)/shard_map/ppermute | solution.py:22
  92.5 1.9 %collective-permute-start.13 = (bf16[256,512]{1,0:T(8,128)(2,1)S(1)}, bf16[256,512]{1,0:T(8,128)(2,1)S(1)}, u32[]{:S(2)}, u32[]{:S(2)}) collective-permute-start(bf16[256,512]{1,0:T(8,128)(2,1)S(1)} %shard_map.49.refs_12_), channel_id=1, source_target_pairs={{16,0},{20,4},{24,8},{28,12},{32,16},{36,20},{40,24},{44,28},{48,3... | collective-permute-start | bytes 786440 | tf_op jit(solution)/shard_map/ppermute | solution.py:22
  94.4 3.9 %collective-permute-done.6.refs_6_ = bf16[384,512]{1,0:T(8,128)(2,1)S(1)} collective-permute-done((bf16[384,512]{1,0:T(8,128)(2,1)S(1)}, bf16[384,512]{1,0:T(8,128)(2,1)S(1)}, u32[]{:S(2)}, u32[]{:S(2)}) %collective-permute-start.6) | collective-permute-done | bytes 393248 | tf_op jit(solution)/shard_map/ppermute | solution.py:22
  99.4 6.7 %shard_map.50 = (f32[256,512]{1,0:T(8,128)S(1)}, f32[256,512]{1,0:T(8,128)S(1)}, f32[256,512]{1,0:T(8,128)S(1)}) custom-call(s32[15]{0:T(128)S(1)} %convert_element_type.10.flags, bf16[256,512]{1,0:T(8,128)(2,1)S(1)} %copy-done.3, bf16[256,512]{1,0:T(8,128)(2,1)S(1)} %copy-done.1, bf16[256,512]{1,0:T(8,128)(2,1)S(1)} %copy-done.2, ...), custom_call_target="tpu_custom_call" | custom-call | flops 3000000000 | bytes 6000000 | tf_op jit(solution)/shard_map/pallas_call | solution.py:266
  106.2 2.0 %shard_map.51.a_ref = bf16[256,512]{1,0:T(8,128)(2,1)S(1)} custom-call(s32[15]{0:T(128)S(1)} %convert_element_type.10.flags, bf16[256,512]{1,0:T(8,128)(2,1)S(1)} %copy-done.3, f32[256,512]{1,0:T(8,128)S(1)} %get-tuple-element.16.sum_ref, f32[256,512]{1,0:T(8,128)S(1)} %get-tuple-element.17.weight_ref, f32[256,512]{1,0:T(8,128)S(1)} %get-tuple-element.18.top_ref, ...), custom_call_target="tpu_custom_call" | custom-call | flops 300000000 | bytes 6000000 | tf_op jit(solution)/shard_map/pallas_call | solution.py:266
  108.2 8.0 %collective-permute-start.14 = (bf16[256,512]{1,0:T(8,128)(2,1)S(1)}, bf16[256,512]{1,0:T(8,128)(2,1)S(1)}, u32[]{:S(2)}, u32[]{:S(2)}) collective-permute-start(bf16[256,512]{1,0:T(8,128)(2,1)S(1)} %shard_map.51.a_ref), channel_id=1, source_target_pairs={{0,1},{1,0},{2,3},{3,2},{4,5},{5,4},{6,7},{7,6},{8,9},{9,8},{10,11... | collective-permute-start | bytes 786440 | tf_op jit(solution)/shard_map/ppermute | solution.py:27
  118.9 4.7 %collective-permute-start.16 = (bf16[256,512]{1,0:T(8,128)(2,1)S(1)}, bf16[256,512]{1,0:T(8,128)(2,1)S(1)}, u32[]{:S(2)}, u32[]{:S(2)}) collective-permute-start(bf16[256,512]{1,0:T(8,128)(2,1)S(1)} %shard_map.53), channel_id=1, source_target_pairs={{0,2},{1,3},{2,0},{3,1},{4,6},{5,7},{6,4},{7,5},{8,10},{9,11},{10,... | collective-permute-start | bytes 786440 | tf_op jit(solution)/shard_map/ppermute | solution.py:27
  125.2 13.2 %collective-permute-done.16 = bf16[256,512]{1,0:T(8,128)(2,1)S(1)} collective-permute-done((bf16[256,512]{1,0:T(8,128)(2,1)S(1)}, bf16[256,512]{1,0:T(8,128)(2,1)S(1)}, u32[]{:S(2)}, u32[]{:S(2)}) %collective-permute-start.16) | collective-permute-done | bytes 262176 | tf_op jit(solution)/shard_map/ppermute | solution.py:27
  (35 shorter events, 12.0 us)
Async XLA Ops:
  1.9 15.6 %collective-permute-start.2 = (bf16[256,512]{1,0:T(8,128)(2,1)S(1)}, bf16[256,512]{1,0:T(8,128)(2,1)S(1)}, u32[]{:S(2)}, u32[]{:S(2)}) collective-permute-start(bf16[256,512]{1,0:T(8,128)(2,1)S(1)} %get-tuple-element.13), channel_id=1, source_target_pairs={{0,8},{4,12},{8,0},{12,4},{16,24},{20,28},{24,16},{28,20},{32,40},... | collective-permute-start | bytes 786440 | tf_op jit(solution)/shard_map/ppermute | solution.py:22
  6.1 111.3 %collective-permute-start.15 = (bf16[512,2048]{1,0:T(8,128)(2,1)}, bf16[512,2048]{1,0:T(8,128)(2,1)}, u32[]{:S(2)}, u32[]{:S(2)}) collective-permute-start(bf16[512,2048]{1,0:T(8,128)(2,1)} %wa_ref.3), channel_id=1, source_target_pairs={{0,1},{1,0},{2,3},{3,2},{4,5},{5,4},{6,7},{7,6},{8,9},{9,8},{10,11... | collective-permute-start | bytes 6291464 | tf_op jit(solution)/shard_map/ppermute | solution.py:27
  17.5 80.8 %copy-start.1 = (bf16[256,512]{1,0:T(8,128)(2,1)S(1)}, bf16[256,512]{1,0:T(8,128)(2,1)}, u32[]{:S(2)}) copy-start(bf16[256,512]{1,0:T(8,128)(2,1)} %refs_0_.1) | copy-start | bytes 786436
  17.5 80.8 %copy-start.2 = (bf16[256,512]{1,0:T(8,128)(2,1)S(1)}, bf16[256,512]{1,0:T(8,128)(2,1)}, u32[]{:S(2)}) copy-start(bf16[256,512]{1,0:T(8,128)(2,1)} %refs_1_.1) | copy-start | bytes 786436
  17.5 80.8 %copy-start.3 = (bf16[256,512]{1,0:T(8,128)(2,1)S(1)}, bf16[256,512]{1,0:T(8,128)(2,1)}, u32[]{:S(2)}) copy-start(bf16[256,512]{1,0:T(8,128)(2,1)} %q_ref.3) | copy-start | bytes 786436
  17.7 8.6 %collective-permute-start.7 = (bf16[256,512]{1,0:T(8,128)(2,1)S(1)}, bf16[256,512]{1,0:T(8,128)(2,1)S(1)}, u32[]{:S(2)}, u32[]{:S(2)}) collective-permute-start(bf16[256,512]{1,0:T(8,128)(2,1)S(1)} %shard_map.46.a_ref), channel_id=1, source_target_pairs={{0,4},{4,0},{8,12},{12,8},{16,20},{20,16},{24,28},{28,24},{32,36},... | collective-permute-start | bytes 786440 | tf_op jit(solution)/shard_map/ppermute | solution.py:22
  21.2 45.8 %collective-permute-start = (bf16[512,512]{1,0:T(8,128)(2,1)}, bf16[512,512]{1,0:T(8,128)(2,1)S(1)}, u32[]{:S(2)}, u32[]{:S(2)}) collective-permute-start(bf16[512,512]{1,0:T(8,128)(2,1)} %get-tuple-element.12), channel_id=1, source_target_pairs={{0,4},{4,8},{8,12},{16,20},{20,24},{24,28},{32,36},{36,40},{40,44}... | collective-permute-start | bytes 1572872 | tf_op jit(solution)/shard_map/ppermute | solution.py:22
  26.4 42.7 %collective-permute-start.8 = (bf16[512,512]{1,0:T(8,128)(2,1)S(1)}, bf16[512,512]{1,0:T(8,128)(2,1)S(1)}, u32[]{:S(2)}, u32[]{:S(2)}) collective-permute-start(bf16[512,512]{1,0:T(8,128)(2,1)S(1)} %shard_map.47), channel_id=1, source_target_pairs={{0,16},{4,20},{8,24},{12,28},{16,32},{20,36},{24,40},{28,44},{32,4... | collective-permute-start | bytes 1572872 | tf_op jit(solution)/shard_map/ppermute | solution.py:22
  30.4 12.2 %collective-permute-start.4 = (bf16[64,512]{1,0:T(8,128)(2,1)S(1)}, bf16[64,512]{1,0:T(8,128)(2,1)S(1)}, u32[]{:S(2)}, u32[]{:S(2)}) collective-permute-start(bf16[64,512]{1,0:T(8,128)(2,1)S(1)} %get-tuple-element.14), channel_id=1, source_target_pairs={{0,48},{4,52},{8,56},{12,60},{32,80},{36,84},{40,88},{44,92},{48,0... | collective-permute-start | bytes 196616 | tf_op jit(solution)/shard_map/ppermute | solution.py:22
  39.2 41.1 %collective-permute-start.9 = (bf16[512,512]{1,0:T(8,128)(2,1)S(1)}, bf16[512,512]{1,0:T(8,128)(2,1)S(1)}, u32[]{:S(2)}, u32[]{:S(2)}) collective-permute-start(bf16[512,512]{1,0:T(8,128)(2,1)S(1)} %shard_map.47), channel_id=1, source_target_pairs={{16,0},{20,4},{24,8},{28,12},{32,16},{36,20},{40,24},{44,28},{48,3... | collective-permute-start | bytes 1572872 | tf_op jit(solution)/shard_map/ppermute | solution.py:22
  42.6 7.9 %collective-permute-start.5 = (bf16[64,512]{1,0:T(8,128)(2,1)S(1)}, bf16[64,512]{1,0:T(8,128)(2,1)S(1)}, u32[]{:S(2)}, u32[]{:S(2)}) collective-permute-start(bf16[64,512]{1,0:T(8,128)(2,1)S(1)} %collective-permute-done.4.skew_ref.refs_9_), channel_id=1, source_target_pairs={{0,8},{4,12},{8,0},{12,4},{16,24},{20,28},{24,16},{28,20},{32,40},... | collective-permute-start | bytes 196616 | tf_op jit(solution)/shard_map/ppermute | solution.py:22
  50.5 15.2 %collective-permute-start.3 = (bf16[256,512]{1,0:T(8,128)(2,1)S(1)}, bf16[256,512]{1,0:T(8,128)(2,1)S(1)}, u32[]{:S(2)}, u32[]{:S(2)}) collective-permute-start(bf16[256,512]{1,0:T(8,128)(2,1)S(1)} %collective-permute-done.2.across_ref.one_ref.refs_4_), channel_id=1, source_target_pairs={{0,16},{4,20},{16,32},{20,36},{24,8},{28,12},{32,48},{36,52},{40,2... | collective-permute-start | bytes 786440 | tf_op jit(solution)/shard_map/ppermute | solution.py:22
  65.6 17.3 %collective-permute-start.1 = (bf16[512,512]{1,0:T(8,128)(2,1)}, bf16[512,512]{1,0:T(8,128)(2,1)}, u32[]{:S(2)}, u32[]{:S(2)}) collective-permute-start(bf16[512,512]{1,0:T(8,128)(2,1)} %get-tuple-element.12), channel_id=1, source_target_pairs={{4,0},{8,4},{12,8},{20,16},{24,20},{28,24},{36,32},{40,36},{44,40}... | collective-permute-start | bytes 1572872 | tf_op jit(solution)/shard_map/ppermute | solution.py:22
  66.9 0.8 copy-start.4
  67.7 24.8 %collective-permute-start.10 = (bf16[512,512]{1,0:T(8,128)(2,1)}, bf16[512,512]{1,0:T(8,128)(2,1)}, u32[]{:S(2)}, u32[]{:S(2)}) collective-permute-start(bf16[512,512]{1,0:T(8,128)(2,1)} %get-tuple-element.12), channel_id=1, source_target_pairs={{12,16},{28,32},{44,48},{60,64},{76,80},{92,96},{108,112},{124,128... | collective-permute-start | bytes 1572872 | tf_op jit(solution)/shard_map/ppermute | solution.py:22
  69.0 25.4 %collective-permute-start.11 = (bf16[512,512]{1,0:T(8,128)(2,1)}, bf16[512,512]{1,0:T(8,128)(2,1)}, u32[]{:S(2)}, u32[]{:S(2)}) collective-permute-start(bf16[512,512]{1,0:T(8,128)(2,1)} %get-tuple-element.12), channel_id=1, source_target_pairs={{16,12},{32,28},{48,44},{64,60},{80,76},{96,92},{112,108},{128,124... | collective-permute-start | bytes 1572872 | tf_op jit(solution)/shard_map/ppermute | solution.py:22
  80.3 18.0 %collective-permute-start.6 = (bf16[384,512]{1,0:T(8,128)(2,1)S(1)}, bf16[384,512]{1,0:T(8,128)(2,1)S(1)}, u32[]{:S(2)}, u32[]{:S(2)}) collective-permute-start(bf16[384,512]{1,0:T(8,128)(2,1)S(1)} %hand.1), channel_id=1, source_target_pairs={{0,4},{4,0},{8,12},{12,8},{16,20},{20,16},{24,28},{28,24},{32,36},... | collective-permute-start | bytes 1179656 | tf_op jit(solution)/shard_map/ppermute | solution.py:22
  83.0 23.2 %collective-permute-start.12 = (bf16[256,512]{1,0:T(8,128)(2,1)S(1)}, bf16[256,512]{1,0:T(8,128)(2,1)S(1)}, u32[]{:S(2)}, u32[]{:S(2)}) collective-permute-start(bf16[256,512]{1,0:T(8,128)(2,1)S(1)} %shard_map.48.refs_11_), channel_id=1, source_target_pairs={{0,16},{4,20},{8,24},{12,28},{16,32},{20,36},{24,40},{28,44},{32,4... | collective-permute-start | bytes 786440 | tf_op jit(solution)/shard_map/ppermute | solution.py:22
  92.5 13.7 %collective-permute-start.13 = (bf16[256,512]{1,0:T(8,128)(2,1)S(1)}, bf16[256,512]{1,0:T(8,128)(2,1)S(1)}, u32[]{:S(2)}, u32[]{:S(2)}) collective-permute-start(bf16[256,512]{1,0:T(8,128)(2,1)S(1)} %shard_map.49.refs_12_), channel_id=1, source_target_pairs={{16,0},{20,4},{24,8},{28,12},{32,16},{36,20},{40,24},{44,28},{48,3... | collective-permute-start | bytes 786440 | tf_op jit(solution)/shard_map/ppermute | solution.py:22
  98.4 1.0 copy-start.5
  106.2 11.2 %copy-start = (bf16[512,2048]{1,0:T(8,128)(2,1)S(1)}, bf16[512,2048]{1,0:T(8,128)(2,1)}, u32[]{:S(2)}) copy-start(bf16[512,2048]{1,0:T(8,128)(2,1)} %wa_ref.3) | copy-start | bytes 6291460
  108.2 9.2 %collective-permute-start.14 = (bf16[256,512]{1,0:T(8,128)(2,1)S(1)}, bf16[256,512]{1,0:T(8,128)(2,1)S(1)}, u32[]{:S(2)}, u32[]{:S(2)}) collective-permute-start(bf16[256,512]{1,0:T(8,128)(2,1)S(1)} %shard_map.51.a_ref), channel_id=1, source_target_pairs={{0,1},{1,0},{2,3},{3,2},{4,5},{5,4},{6,7},{7,6},{8,9},{9,8},{10,11... | collective-permute-start | bytes 786440 | tf_op jit(solution)/shard_map/ppermute | solution.py:27
  118.9 19.5 %collective-permute-start.16 = (bf16[256,512]{1,0:T(8,128)(2,1)S(1)}, bf16[256,512]{1,0:T(8,128)(2,1)S(1)}, u32[]{:S(2)}, u32[]{:S(2)}) collective-permute-start(bf16[256,512]{1,0:T(8,128)(2,1)S(1)} %shard_map.53), channel_id=1, source_target_pairs={{0,2},{1,3},{2,0},{3,1},{4,6},{5,7},{6,4},{7,5},{8,10},{9,11},{10,... | collective-permute-start | bytes 786440 | tf_op jit(solution)/shard_map/ppermute | solution.py:27
